TPU v7x, 32 devices: a whole 2x2x4 slice. The times are simulated.
32 devices in a mesh: shell: 2 (over x), pix: 16 (over z, y, core).
Axes of the slice: x: 2, y: 2, z: 4, core: 2. Of those that a mesh axis runs over, the one named last changes fastest.
Arguments:
- block_tile: int32 [4, 1024], P('shell'), may hold values from 0 to 2047, as said below
- cell_index: int32 [4, 1024, 512], P('shell', 'pix'), may hold values from 0 to 2047
- masses: bfloat16 [4, 1024, 512], P('shell', 'pix'), may hold values from 0.125 to 8, as said below
- plane_coef: float32 [4], P('shell'), may hold values from 0.1 to 0.4
- plane_dist: float32 [4], P('shell'), may hold values from 0.2 to 1
- source_inv: float32 [4], P('shell'), may hold values from 0.5 to 1
Outputs:
- convergence: float32 [4, 2048, 2048], P('shell', 'pix')
- shear_one: float32 [4, 2048, 2048], P('shell', 'pix')
- shear_two: float32 [4, 2048, 2048], P('shell', 'pix')
Inputs may be any that keep to these rules, and one draw needn't show every extreme that they name: `block_tile`: each row is 16 aligned runs of 64 entries, one run per index of pix. The entries of a run are distinct, and at most 8 of them lie in one index's rows of tiles (tile b lies in the rows of index b // 128). In every plane some index receives exactly 8 tiles from every run. `masses`: positive particle weights.
All inputs are finite; a program needn't handle non-finite values.
Results may differ from a plain program's by a relative error of at most 0.0003.
Values sent between devices are 32-bit elements; how exact they have to be, the bound alone decides.
No kernel may reach another device: no remote copies, remote signals or barrier semaphores. Data moves between devices by JAX's collectives and lax.ppermute only.
A program may use at most 64 MiB of HBM per device.

v0:
```python
from functools import partial
import math

import jax
import jax.numpy as jnp
from jax import lax
from jax.sharding import PartitionSpec as P

L = 2048
TR = 16
TC = 128


HIGHEST = lax.Precision.HIGHEST


def entering(value, axis, join, neutral):
    count, mine = (lax.axis_size(axis), lax.axis_index(axis))
    pieces = jax.tree.map(lambda part: lax.all_gather(part, axis), value)
    running = jax.tree.map(
        lambda part, zero: jnp.full_like(part, 0) + jnp.asarray(zero, part.dtype), value, neutral
    )

    def lap(position, running):
        longer = join(running, jax.tree.map(lambda part: part[position], pieces))
        return jax.tree.map(lambda new, old: jnp.where(position < mine, new, old), longer, running)

    return lax.fori_loop(0, count - 1, lap, running)


def dft_table(left_size, right_size, period, sign_value):
    left_idx = jnp.arange(left_size)[:, None]
    right_idx = jnp.arange(right_size)[None, :]
    angle = 2.0 * math.pi / period * (left_idx * right_idx % period).astype(jnp.float32)
    return (jnp.cos(angle), sign_value * jnp.sin(angle))


def mix_outer(table, real_part, imag_part):
    cosine, sine_part = table
    contract = partial(jnp.einsum, "ab,...bc->...ac", precision=HIGHEST)
    return (
        contract(cosine, real_part) - contract(sine_part, imag_part),
        contract(sine_part, real_part) + contract(cosine, imag_part),
    )


def mix_inner(table, real_part, imag_part):
    cosine, sine_part = table
    product = partial(jnp.matmul, precision=HIGHEST)
    return (
        product(real_part, cosine) - product(imag_part, sine_part),
        product(real_part, sine_part) + product(imag_part, cosine),
    )


def twist(table, real_part, imag_part):
    cosine, sine_part = table
    return (real_part * cosine - imag_part * sine_part, real_part * sine_part + imag_part * cosine)


def transform_last(real_part, imag_part, sign_value):
    length = real_part.shape[-1]
    inner = math.gcd(length, 128)
    outer = length // inner
    leading = real_part.shape[:-1]
    real_part = real_part.reshape(leading + (outer, inner))
    imag_part = imag_part.reshape(leading + (outer, inner))
    outer_table = dft_table(outer, outer, outer, sign_value)
    inner_table = dft_table(inner, inner, inner, sign_value)
    twiddle = dft_table(outer, inner, length, sign_value)
    if sign_value < 0:
        real_part, imag_part = mix_outer(outer_table, real_part, imag_part)
        real_part, imag_part = twist(twiddle, real_part, imag_part)
        real_part, imag_part = mix_inner(inner_table, real_part, imag_part)
    else:
        real_part, imag_part = mix_inner(inner_table, real_part, imag_part)
        real_part, imag_part = twist(twiddle, real_part, imag_part)
        real_part, imag_part = mix_outer(outer_table, real_part, imag_part)
    return (real_part.reshape(leading + (length,)), imag_part.reshape(leading + (length,)))


def frequency_of(position, length):
    inner = math.gcd(length, 128)
    outer = length // inner
    frequency = position // inner + outer * (position % inner)
    signed = jnp.where(frequency >= length // 2, frequency - length, frequency).astype(jnp.float32)
    keep_mask = (frequency != length // 2).astype(jnp.float32)
    return (signed, keep_mask)


def add_pairs(earlier_pair, later_pair):
    return (earlier_pair[0] + later_pair[0], earlier_pair[1] + later_pair[1])


def deposit_group(item):
    cell_ids, weights = item
    tile_rows = cell_ids // TC
    tile_cols = cell_ids % TC
    row_hot = jnp.where(
        tile_rows[:, None, :] == jnp.arange(TR)[None, :, None],
        weights[:, None, :],
        jnp.zeros((), jnp.bfloat16),
    )
    col_hot = (tile_cols[:, :, None] == jnp.arange(TC)[None, None, :]).astype(jnp.bfloat16)
    return jnp.einsum("grk,gkc->grc", row_hot, col_hot, preferred_element_type=jnp.float32)


def rows_to_sending(packed, groups, slab, cols_own):
    count, fields = (packed.shape[0], packed.shape[1])
    return (
        packed.reshape(count, fields, slab, groups, cols_own)
        .transpose(3, 0, 1, 4, 2)
        .reshape(groups, count, fields, cols_own * slab)
    )


def arrived_to_columns(arrived, groups, slab, cols_own):
    count, fields = (arrived.shape[1], arrived.shape[2])
    return (
        arrived.reshape(groups, count, fields, cols_own, slab)
        .transpose(1, 2, 3, 0, 4)
        .reshape(count, fields, cols_own, groups * slab)
    )


def columns_to_sending(stacked, groups, slab, cols_own):
    count, fields = (stacked.shape[0], stacked.shape[1])
    return (
        stacked.reshape(count, fields, cols_own, groups, slab)
        .transpose(3, 0, 1, 2, 4)
        .reshape(groups, count, fields, cols_own * slab)
    )


def landed_to_rows(landed, groups, slab, cols_own):
    count, fields = (landed.shape[1], landed.shape[2])
    return (
        landed.reshape(groups, count, fields, cols_own, slab)
        .transpose(1, 2, 4, 0, 3)
        .reshape(count, fields, slab, groups * cols_own)
    )


def local(block_tile, cell_index, masses, plane_coef, plane_dist, source_inv):
    groups = lax.axis_size("pix")
    my_index = lax.axis_index("pix")
    planes, local_tiles, per_tile = cell_index.shape
    slab = L // groups
    per_owner = slab // TR * (L // TC)
    cap = max(1, 2 * local_tiles // groups)
    flat = TR * TC
    batch_tiles = 8
    deposited = lax.map(
        deposit_group,
        (cell_index.reshape(-1, batch_tiles, per_tile), masses.reshape(-1, batch_tiles, per_tile)),
    )
    tile_sums = deposited.reshape(planes, local_tiles, flat)
    table = block_tile.reshape(planes, groups, local_tiles)
    owner = table // per_owner
    earlier = jnp.arange(local_tiles)[:, None] < jnp.arange(local_tiles)[None, :]
    same_owner = owner[:, :, :, None] == owner[:, :, None, :]
    rank = jnp.sum(jnp.where(same_owner & earlier[None, None], 1, 0), axis=2)
    slot = owner * cap + rank
    my_slots = lax.dynamic_index_in_dim(slot, my_index, axis=1, keepdims=False)
    slot_grid = jnp.arange(groups)[:, None] * cap + jnp.arange(cap)[None, :]
    send_hot = (my_slots[:, None, None, :] == slot_grid[None, :, :, None]).astype(jnp.float32)
    outgoing = jnp.einsum("pnct,ptf->npcf", send_hot, tile_sums, precision=HIGHEST)
    incoming = lax.all_to_all(outgoing, "pix", split_axis=0, concat_axis=0, tiled=True)
    local_index = table - my_index * per_owner
    is_mine = owner == my_index
    tile_hot = (is_mine[..., None] & (local_index[..., None] == jnp.arange(per_owner))).astype(
        jnp.float32
    )
    slot_hot = (rank[..., None] == jnp.arange(cap)).astype(jnp.float32)
    placing = jnp.einsum("pstl,pstc->plsc", tile_hot, slot_hot, precision=HIGHEST)
    slab_tiles = jnp.einsum("plsc,spcf->plf", placing, incoming, precision=HIGHEST)
    density = (
        slab_tiles.reshape(planes, slab // TR, L // TC, TR, TC)
        .transpose(0, 1, 3, 2, 4)
        .reshape(planes, slab, L)
    )
    total = lax.psum(jnp.sum(density, axis=(1, 2)), "pix")
    contrast = density / (total / (L * L))[:, None, None] - 1.0
    near_local = jnp.cumsum(plane_coef[:, None, None] * contrast, axis=0)
    far_local = jnp.cumsum((plane_coef * plane_dist)[:, None, None] * contrast, axis=0)
    blank = jnp.zeros((slab, L), jnp.float32)
    near_before, far_before = entering(
        (near_local[-1], far_local[-1]), "shell", add_pairs, (blank, blank)
    )
    convergence = near_before + near_local - source_inv[:, None, None] * (far_before + far_local)
    cols_own = L // groups
    wave_x, keep_x = frequency_of(my_index * cols_own + jnp.arange(cols_own), L)
    wave_y, keep_y = frequency_of(jnp.arange(L), L)
    wave_x = wave_x[:, None]
    wave_y = wave_y[None, :]
    both_keep = keep_x[:, None] * keep_y[None, :]
    wave_power = jnp.maximum(wave_x * wave_x + wave_y * wave_y, 1.0)
    kernel_one = both_keep * (wave_x * wave_x - wave_y * wave_y) / wave_power
    kernel_two = both_keep * 2.0 * wave_x * wave_y / wave_power
    scale = 1.0 / (L * L)
    spec_real, spec_imag = transform_last(convergence[0::2], convergence[1::2], -1.0)
    sending = rows_to_sending(jnp.stack([spec_real, spec_imag], axis=1), groups, slab, cols_own)
    arrived = lax.all_to_all(sending, "pix", split_axis=0, concat_axis=0, tiled=True)
    columns = arrived_to_columns(arrived, groups, slab, cols_own)
    row_real, row_imag = transform_last(columns[:, 0], columns[:, 1], -1.0)
    first_real, first_imag = transform_last(row_real * kernel_one, row_imag * kernel_one, 1.0)
    second_real, second_imag = transform_last(row_real * kernel_two, row_imag * kernel_two, 1.0)
    stacked = jnp.stack([first_real, first_imag, second_real, second_imag], axis=1)
    landed = lax.all_to_all(
        columns_to_sending(stacked, groups, slab, cols_own),
        "pix",
        split_axis=0,
        concat_axis=0,
        tiled=True,
    )
    row_layout = landed_to_rows(landed, groups, slab, cols_own)
    even_one, odd_one = transform_last(row_layout[:, 0], row_layout[:, 1], 1.0)
    even_two, odd_two = transform_last(row_layout[:, 2], row_layout[:, 3], 1.0)
    shear_one = jnp.stack([even_one, odd_one], axis=1).reshape(planes, slab, L)
    shear_two = jnp.stack([even_two, odd_two], axis=1).reshape(planes, slab, L)
    return (convergence, shear_one * scale, shear_two * scale)


def solution(mesh):
    placed = (
        P("shell", None),
        P("shell", "pix", None),
        P("shell", "pix", None),
        P("shell"),
        P("shell"),
        P("shell"),
    )
    return jax.shard_map(
        local,
        mesh=mesh,
        in_specs=placed,
        out_specs=(P("shell", "pix", None), P("shell", "pix", None), P("shell", "pix", None)),
        check_vma=False,
    )
```

profile of v0, /device:TPU:1, one launch (start us, length us, event | category | flops | bytes accessed | tf_op | source)
XLA Modules:
  0.0 498.4 jit_solution(13083244063688740668)
XLA Ops:
  8.0 56.0 %while.8 = (s32[]{:T(128)}, f32[16,8,16,128]{3,2,1,0:T(8,128)S(1)}, s32[16,8,512]{2,1,0:T(8,128)}, bf16[16,8,512]{2,1,0:T(8,128)(2,1)}, s32[]{:T(128)}) while((s32[]{:T(128)}, f32[16,8,16,128]{3,2,1,0:T(8,128)S(1)}, s32[16,8,512]{2,1,0:T(8,128)}, bf16[16,8,512]{2,1,0:T(8,128)(2,1)}, s32[]{:T(128)}) %tuple.63), condition=%wide.region_2.3_spmd, body=%wide.region_1.2_spmd.sunk | while | flops 17534976 | bytes 196693 | solution.py:153
  65.7 2.5 copy.183
  68.2 7.3 %all-to-all-start = ((f32[16,2,8,2048]{3,2,1,0:T(8,128)}), f32[16,2,8,2048]{3,2,1,0:T(8,128)S(1)}, u32[]{:S(2)}, u32[]{:S(2)}) async-start(f32[16,2,8,2048]{3,2,1,0:T(8,128)} %copy.183), calls=%async_computation | async-start | bytes 4194304 | tf_op jit(solution)/shard_map/all_to_all | solution.py:168
  76.9 40.2 %all-to-all-done = f32[16,2,8,2048]{3,2,1,0:T(8,128)S(1)} async-done(((f32[16,2,8,2048]{3,2,1,0:T(8,128)}), f32[16,2,8,2048]{3,2,1,0:T(8,128)S(1)}, u32[]{:S(2)}, u32[]{:S(2)}) %all-to-all-start) | async-done | bytes 2097184 | tf_op jit(solution)/shard_map/all_to_all | solution.py:168
  117.1 3.2 bitcast_reduce_fusion
  120.3 33.9 %psum.7 = f32[2]{0:T(128)S(1)} all-reduce(f32[2]{0:T(128)S(1)} %get-tuple-element.117), channel_id=1, replica_groups=mesh['shell'=2,'pix'=16] {'pix'}, use_global_device_ids=true, to_apply=%region_4.5 | all-reduce | flops 2 | bytes 16 | tf_op jit(solution)/shard_map/psum | solution.py:182
  154.2 2.0 copy.236
  156.2 2.0 copy.185
  158.2 1.7 reshape.931
  165.7 31.5 %all-gather.3.cloned.1.call-done = f32[2,128,2048]{2,1,0:T(8,128)} async-done(((f32[1,128,2048]{2,1,0:T(8,128)}), f32[2,128,2048]{2,1,0:T(8,128)}) %all-gather.3.cloned.1.call-update) | async-done | bytes 2097168 | tf_op jit(solution)/shard_map/all_gather | solution.py:19
  198.6 33.9 %all-gather.5.cloned.1.call-done = f32[2,128,2048]{2,1,0:T(8,128)} async-done(((f32[1,128,2048]{2,1,0:T(8,128)}), f32[2,128,2048]{2,1,0:T(8,128)}) %all-gather.5.cloned.1.call-update) | async-done | bytes 2097168 | tf_op jit(solution)/shard_map/all_gather | solution.py:19
  245.7 2.0 fusion.31
  247.9 1.8 copy.190
  249.7 6.4 %all-to-all-start.1 = ((f32[16,1,2,16384]{3,1,2,0:T(1,128)}), f32[16,1,2,16384]{3,1,2,0:T(1,128)S(1)}, u32[]{:S(2)}, u32[]{:S(2)}) async-start(f32[16,1,2,16384]{3,1,2,0:T(1,128)} %bitcast.319), calls=%async_computation.1 | async-start | bytes 4194304 | tf_op jit(solution)/shard_map/all_to_all | solution.py:203
  256.2 41.4 %all-to-all-done.1 = f32[16,1,2,16384]{3,1,2,0:T(1,128)S(1)} async-done(((f32[16,1,2,16384]{3,1,2,0:T(1,128)}), f32[16,1,2,16384]{3,1,2,0:T(1,128)S(1)}, u32[]{:S(2)}, u32[]{:S(2)}) %all-to-all-start.1) | async-done | bytes 2097184 | tf_op jit(solution)/shard_map/all_to_all | solution.py:203
  297.6 1.8 copy.191
  299.4 2.6 fusion.465
  304.7 1.7 copy.235
  314.4 1.6 fusion.97
  324.5 1.9 multiply_add_fusion.3
  326.4 2.0 fusion.65
  328.4 1.6 fusion.67
  330.0 1.6 fusion.59
  331.6 1.6 fusion.61
  333.3 1.6 fusion.28
  334.9 1.6 fusion.27
  336.6 1.6 fusion.26
  338.2 1.8 fusion.25
  341.7 103.1 %all_to_all.15 = f32[16,1,4,16384]{3,1,2,0:T(1,128)S(1)} all-to-all(f32[16,1,4,16384]{3,1,2,0:T(1,128)S(1)} %bitcast.304), channel_id=1, replica_groups=mesh['shell'=2,'pix'=16] {'pix'}, dimensions={0} | all-to-all | bytes 8388608 | tf_op jit(solution)/shard_map/all_to_all | solution.py:209
  445.6 1.9 fusion.91
  447.6 1.9 fusion.108
  449.5 1.9 fusion.94
  451.4 1.9 fusion.111
  453.4 2.0 convolution_subtract_fusion.3
  455.4 2.2 convolution_add_fusion.3
  457.5 2.0 convolution_subtract_fusion.1
  459.5 2.3 multiply_add_fusion
  461.8 1.6 fusion.47
  463.4 1.6 fusion.49
  465.1 1.6 fusion.53
  466.7 1.6 fusion.55
  468.3 2.8 fusion.22
  471.2 2.6 fusion.21
  473.8 2.4 stack_reshape.21
  476.2 2.4 stack_reshape.20
  478.5 2.6 fusion.24
  481.1 2.6 fusion.23
  483.7 2.5 stack_reshape.9
  (154 shorter events, 106.5 us)
Async XLA Ops:
  68.2 48.9 %all-to-all-start = ((f32[16,2,8,2048]{3,2,1,0:T(8,128)}), f32[16,2,8,2048]{3,2,1,0:T(8,128)S(1)}, u32[]{:S(2)}, u32[]{:S(2)}) async-start(f32[16,2,8,2048]{3,2,1,0:T(8,128)} %copy.183), calls=%async_computation | async-start | bytes 4194304 | tf_op jit(solution)/shard_map/all_to_all | solution.py:168
  75.6 121.7 %all-gather.3.cloned.1.call-start = ((), (), s32[]{:S(2)}) async-start(), calls=%async_computation.3 | async-start | bytes 3145728 | tf_op jit(solution)/shard_map/all_gather | solution.py:19
  158.2 1.7 copy-start.10
  160.2 1.3 copy-start
  161.6 1.4 copy-start.12
  162.7 69.9 %all-gather.5.cloned.1.call-start = ((), (), s32[]{:S(2)}) async-start(), calls=%async_computation.4 | async-start | bytes 3145728 | tf_op jit(solution)/shard_map/all_gather | solution.py:19
  163.3 1.3 copy-start.2
  165.7 68.3 %copy-start.1 = (f32[2,128,2048]{2,1,0:T(8,128)S(1)}, f32[2,128,2048]{2,1,0:T(8,128)}, u32[]{:S(2)}) copy-start(f32[2,128,2048]{2,1,0:T(8,128)} %copy-done) | copy-start | bytes 6291460
  165.7 68.3 %copy-start.11 = (f32[2]{0:T(128)S(1)}, f32[2]{0:T(128)}, u32[]{:S(2)}) copy-start(f32[2]{0:T(128)} %param.13) | copy-start | bytes 28
  232.5 1.9 copy-start.3
  235.1 1.3 copy-start.4
  249.7 47.9 %all-to-all-start.1 = ((f32[16,1,2,16384]{3,1,2,0:T(1,128)}), f32[16,1,2,16384]{3,1,2,0:T(1,128)S(1)}, u32[]{:S(2)}, u32[]{:S(2)}) async-start(f32[16,1,2,16384]{3,1,2,0:T(1,128)} %bitcast.319), calls=%async_computation.1 | async-start | bytes 4194304 | tf_op jit(solution)/shard_map/all_to_all | solution.py:203
  481.1 5.1 %copy-start.5 = (f32[1,128,16,128]{3,2,1,0:T(8,128)S(1)}, f32[1,128,16,128]{3,2,1,0:T(8,128)}, u32[]{:S(2)}) copy-start(f32[1,128,16,128]{3,2,1,0:T(8,128)} %fusion.24) | copy-start | bytes 3145732
  483.7 3.7 copy-start.6
  483.7 3.7 copy-start.7
  487.4 1.5 copy-start.8
  487.4 2.3 copy-start.9
Sparse Core Ops, SparseCore 0:
  162.8 34.4 all-gather.2
  199.4 33.0 all-gather.4
where the time goes:
time: 508 us; the launch traced here: 498 us
  waiting for transfers between devices  147 us (29%)
  blocking collectives  137 us (27%)
  matrix products  106 us (21%)
  local copies, waits for them, and re-layouts  47.2 us (9%)
  other arithmetic  31.7 us (6%)
  between operations  15.1 us (3%)
  starting transfers between devices  14 us (3%)
    all_to_all x1, blocking collectives, local(): lax.all_to_all(columns_to_sending(stacked, groups, slab, cols_own), 'pix'...  103 us
    all_gather x2, waiting for transfers between devices, entering(): pieces = jax.tree.map(lambda part: lax.all_gather(part, axis), value)  65.5 us
    all_to_all x1, waiting for transfers between devices, local(): lax.all_to_all(sending, 'pix', split_axis=0, concat_axis=0, tiled=True)  41.4 us
    all_to_all x1, waiting for transfers between devices, local(): lax.all_to_all(outgoing, 'pix', split_axis=0, concat_axis=0, tiled=True)  40.2 us
    psum x1, blocking collectives, local(): total = lax.psum(jnp.sum(density, axis=(1, 2)), 'pix')  33.9 us
    dot_general x16, matrix products, deposit_group(): jnp.einsum('grk,gkc->grc', row_hot, col_hot, preferred_element_type=jnp.f...  21.1 us
    select_n x16, other arithmetic, deposit_group(): tile_cols = cell_ids % TC  11.7 us
    select_n x16, other arithmetic, deposit_group(): tile_rows = cell_ids // TC  11.7 us
  transfers between devices with their start and end apart: 4, of which 4 were waited for; matrix products, arithmetic and copies ran while one was open for 1% of the time, Pallas kernels for 0%

commit v1 on v0

--- a/solution.py
+++ b/solution.py
@@ -3,7 +3,10 @@
 
 import jax
 import jax.numpy as jnp
+import numpy as np
 from jax import lax
+from jax.experimental import pallas as pl
+from jax.experimental.pallas import tpu as pltpu
 from jax.sharding import PartitionSpec as P
 
 L = 2048
@@ -221,6 +224,408 @@
     return (convergence, shear_one * scale, shear_two * scale)
 
 
+def bf16_pair(value):
+    high = value.astype(jnp.bfloat16)
+    return (high, (value - high.astype(jnp.float32)).astype(jnp.bfloat16))
+
+
+def dft_block(size, sign_value):
+    turn = 2.0 * np.pi / size * (np.outer(np.arange(size), np.arange(size)) % size)
+    cosine, sine = (np.cos(turn), sign_value * np.sin(turn))
+    whole = np.block([[cosine, sine], [-sine, cosine]]).astype(np.float32)
+    high = whole.astype(jnp.bfloat16)
+    low = (whole - high.astype(np.float32)).astype(jnp.bfloat16)
+    return np.stack([high, low])
+
+
+def twiddle_pair(outer, inner):
+    turn = 2.0 * np.pi / (outer * inner) * np.outer(np.arange(outer), np.arange(inner))
+    return np.stack([np.cos(turn), np.sin(turn)]).astype(np.float32)
+
+
+def quarter(values, sign_value):
+    (ar, ai), (br, bi), (cr, ci), (dr, di) = values
+    pr, pi, mr, mi = (ar + cr, ai + ci, ar - cr, ai - ci)
+    qr, qi, nr, ni = (br + dr, bi + di, br - dr, bi - di)
+    if sign_value < 0:
+        return [(pr + qr, pi + qi), (mr + ni, mi - nr), (pr - qr, pi - qi), (mr - ni, mi + nr)]
+    return [(pr + qr, pi + qi), (mr - ni, mi + nr), (pr - qr, pi - qi), (mr + ni, mi - nr)]
+
+
+def rotate(value, step, sign_value):
+    real_part, imag_part = value
+    if step == 0:
+        return value
+    if step == 4:
+        return (-sign_value * imag_part, sign_value * real_part)
+    cosine = math.cos(2.0 * math.pi * step / 16)
+    sine = sign_value * math.sin(2.0 * math.pi * step / 16)
+    return (real_part * cosine - imag_part * sine, real_part * sine + imag_part * cosine)
+
+
+def sixteen(values, sign_value):
+    inner = [quarter([values[4 * a + b] for a in range(4)], sign_value) for b in range(4)]
+    result = [None] * 16
+    for k in range(4):
+        turned = [rotate(inner[b][k], b * k, sign_value) for b in range(4)]
+        for place, value in enumerate(quarter(turned, sign_value)):
+            result[k + 4 * place] = value
+    return result
+
+
+def dot3(left, right, left_is_table):
+    mul = partial(jnp.dot, preferred_element_type=jnp.float32)
+    (lh, ll), (rh, rl) = (left, right)
+    return mul(lh, rh) + (mul(ll, rh) + mul(lh, rl))
+
+
+def pack_kernel(groups, cap, chunks, per_owner, me_ref, table_ref, cell_ref, mass_ref, out_ref, count_ref, cell_f, mass_f):
+    planes, local_tiles, per_tile = cell_ref.shape
+    out_ref[...] = jnp.zeros(out_ref.shape, jnp.float32)
+    cell_f[...] = cell_ref[...].astype(jnp.float32)
+    mass_f[...] = mass_ref[...].astype(jnp.float32)
+    base = me_ref[0] * local_tiles
+    for plane in range(planes):
+
+        @pl.loop(0, groups)
+        def _(slot):
+            count_ref[slot] = 0
+
+        @pl.loop(0, local_tiles // 8)
+        def _(bunch):
+            lists = [source[plane, pl.ds(pl.multiple_of(bunch * 8, 8), 8), :] for source in (cell_f, mass_f)]
+            for at in range(8):
+                owner = lax.div(table_ref[plane, base + bunch * 8 + at], per_owner)
+                rank = count_ref[owner]
+                count_ref[owner] = rank + 1
+                for kind, values in enumerate(lists):
+                    for chunk in range(chunks):
+                        row = (2 * plane + kind) * chunks * cap + chunk * cap + rank
+                        out_ref[owner, pl.ds(row, 1), :] = values[at : at + 1, chunk * TC : (chunk + 1) * TC]
+
+        total = jnp.sum(mass_f[plane], axis=0, keepdims=True)
+        total = jnp.sum(total, axis=1, keepdims=True)
+        line = jnp.broadcast_to(total, (1, TC))
+        for owner in range(groups):
+            out_ref[owner, planes * 2 * chunks * cap + plane : planes * 2 * chunks * cap + plane + 1, :] = line
+
+
+def deposit_kernel(cap, chunks, slots_ref, recv_ref, out_ref):
+    planes = out_ref.shape[0]
+    groups = recv_ref.shape[0]
+    out_ref[...] = jnp.zeros(out_ref.shape, jnp.float32)
+    low = lax.broadcasted_iota(jnp.int32, (TR, TC), 0).astype(jnp.float32)
+    lines = [(low + float(TR * part)).astype(jnp.bfloat16) for part in range(TC // TR)]
+    one = jnp.ones((TR, TC), jnp.bfloat16)
+    none = jnp.zeros((TR, TC), jnp.bfloat16)
+
+    def spread(value, slot):
+        return jnp.broadcast_to(value[slot : slot + 1, :], (TR, TC)).astype(jnp.bfloat16)
+
+    for plane in range(planes):
+
+        @pl.loop(0, groups)
+        def _(source):
+            start = plane * 2 * chunks * cap
+            cells = [recv_ref[source, start + k * cap : start + (k + 1) * cap, :] for k in range(chunks)]
+            start = start + chunks * cap
+            weights = [recv_ref[source, start + k * cap : start + (k + 1) * cap, :] for k in range(chunks)]
+            rows = [jnp.floor(cell * (1.0 / TC)) for cell in cells]
+            cols = [cell - row * float(TC) for cell, row in zip(cells, rows)]
+            sums = []
+            for slot in range(cap):
+                row_hot = [
+                    jnp.where(lines[0] == spread(rows[k], slot), spread(weights[k], slot), none) for k in range(chunks)
+                ]
+                col_hot = []
+                for k in range(chunks):
+                    col = spread(cols[k], slot)
+                    col_hot.append(jnp.concatenate([jnp.where(line == col, one, none) for line in lines], axis=0))
+                sums.append(
+                    lax.dot_general(
+                        jnp.concatenate(row_hot, axis=1),
+                        jnp.concatenate(col_hot, axis=1),
+                        (((1,), (1,)), ((), ())),
+                        preferred_element_type=jnp.float32,
+                    )
+                )
+            for slot in range(cap):
+                tile = slots_ref[(plane * groups + source) * cap + slot]
+                out_ref[plane, tile] = out_ref[plane, tile] + sums[slot]
+
+
+def rows_kernel(parts, weight_ref, *refs):
+    dens = refs[:parts]
+    totals = refs[parts : 2 * parts]
+    twiddle_ref, table_ref, conv_ref, out_ref, high_ref, low_ref = refs[2 * parts :]
+    planes, slab, length = conv_ref.shape
+    outer = length // TC
+    scales = []
+    for part in range(parts):
+        total = jnp.sum(totals[part][...], axis=0)
+        total = jnp.where(total > 0.0, total, 1.0)
+        scales.append(float(length * length) / total)
+    factors = [
+        [
+            jnp.broadcast_to(weight_ref[i, part * planes + j] * scales[part][j : j + 1, :], (TR, TC))
+            for part in range(parts)
+            for j in range(planes)
+        ]
+        for i in range(planes)
+    ]
+    shift = [weight_ref[i, parts * planes] for i in range(planes)]
+
+    @pl.loop(0, slab // TR)
+    def _(line):
+        values = []
+        here = pl.ds(line * TR, TR)
+        for col in range(outer):
+            tiles = [dens[part][j, line * outer + col] for part in range(parts) for j in range(planes)]
+            pair = []
+            for i in range(planes):
+                field = tiles[0] * factors[i][0]
+                for tile, factor in zip(tiles[1:], factors[i][1:]):
+                    field = field + tile * factor
+                field = field - shift[i]
+                conv_ref[i, here, col * TC : (col + 1) * TC] = field
+                pair.append(field)
+            values.append(tuple(pair))
+        for place, (real_part, imag_part) in enumerate(sixteen(values, -1.0)):
+            if place:
+                cosine = twiddle_ref[0, place : place + 1, :]
+                sine = twiddle_ref[1, place : place + 1, :]
+                real_part, imag_part = (
+                    real_part * cosine + imag_part * sine,
+                    imag_part * cosine - real_part * sine,
+                )
+            for at, value in enumerate((real_part, imag_part)):
+                high, low = bf16_pair(value)
+                high_ref[place, here, at * TC : (at + 1) * TC] = high
+                low_ref[place, here, at * TC : (at + 1) * TC] = low
+
+    table = (table_ref[0], table_ref[1])
+    for place in range(outer):
+        done = dot3((high_ref[place], low_ref[place]), table, False)
+        out_ref[place, 0] = done[:, :TC]
+        out_ref[place, 1] = done[:, TC:]
+
+
+def columns_kernel(me_ref, in_ref, turn_ref, forward_ref, back_ref, out_ref, high_ref, low_ref, back_f):
+    outer, _, inner, lanes = in_ref.shape
+    length = outer * inner
+
+    def turned(place, here, value, sign_value):
+        if place == 0:
+            return value
+        real_part, imag_part = value
+        cosine = jnp.broadcast_to(turn_ref[0, here, place : place + 1], (TR, lanes))
+        sine = jnp.broadcast_to(turn_ref[1, here, place : place + 1], (TR, lanes)) * sign_value
+        return (real_part * cosine - imag_part * sine, real_part * sine + imag_part * cosine)
+
+    @pl.loop(0, inner // TR)
+    def _(line):
+        here = pl.ds(line * TR, TR)
+        there = pl.ds(inner + line * TR, TR)
+        values = [(in_ref[place, 0, here, :], in_ref[place, 1, here, :]) for place in range(outer)]
+        for place, value in enumerate(sixteen(values, -1.0)):
+            real_part, imag_part = turned(place, here, value, -1.0)
+            for spot, part in ((here, real_part), (there, imag_part)):
+                high, low = bf16_pair(part)
+                high_ref[spot, place * lanes : (place + 1) * lanes] = high
+                low_ref[spot, place * lanes : (place + 1) * lanes] = low
+
+    forward = (forward_ref[0], forward_ref[1])
+    back = (back_ref[0], back_ref[1])
+    half = length // 2
+    wave_v = lax.broadcasted_iota(jnp.int32, (inner, lanes), 1) * outer + me_ref[0]
+    keep_v = wave_v != half
+    sv = jnp.where(wave_v >= half, wave_v - length, wave_v).astype(jnp.float32)
+    line_u = lax.broadcasted_iota(jnp.int32, (inner, lanes), 0) * outer
+    for pair in range(outer // 2):
+        span = slice(pair * 2 * lanes, (pair + 1) * 2 * lanes)
+        spectrum = dot3(forward, (high_ref[:, span], low_ref[:, span]), True)
+        for at in range(2):
+            place = 2 * pair + at
+            real_part = spectrum[:inner, at * lanes : (at + 1) * lanes]
+            imag_part = spectrum[inner:, at * lanes : (at + 1) * lanes]
+            wave_u = line_u + place
+            su = jnp.where(wave_u >= half, wave_u - length, wave_u).astype(jnp.float32)
+            keep = jnp.where(keep_v & (wave_u != half), 1.0 / (float(length) * float(length)), 0.0)
+            factor = keep / jnp.maximum(sv * sv + su * su, 1.0)
+            first = factor * (sv * sv - su * su)
+            second = factor * (2.0 * sv * su)
+            stacked = jnp.concatenate(
+                [
+                    jnp.concatenate([real_part * first, real_part * second], axis=1),
+                    jnp.concatenate([imag_part * first, imag_part * second], axis=1),
+                ],
+                axis=0,
+            )
+            back_f[place] = dot3(back, bf16_pair(stacked), True)
+
+    @pl.loop(0, inner // TR)
+    def _(line):
+        here = pl.ds(line * TR, TR)
+        there = pl.ds(inner + line * TR, TR)
+        for field in range(2):
+            side = slice(field * lanes, (field + 1) * lanes)
+            values = [
+                turned(place, here, (back_f[place, here, side], back_f[place, there, side]), 1.0)
+                for place in range(outer)
+            ]
+            for place, (real_part, imag_part) in enumerate(sixteen(values, 1.0)):
+                out_ref[place, 2 * field, here, :] = real_part
+                out_ref[place, 2 * field + 1, here, :] = imag_part
+
+
+def inverse_rows_kernel(in_ref, twiddle_ref, table_ref, first_ref, second_ref, back_f):
+    outer, _, slab, lanes = in_ref.shape
+    table = (table_ref[0], table_ref[1])
+    for field, out_ref in enumerate((first_ref, second_ref)):
+        for place in range(outer):
+            joined = jnp.concatenate([in_ref[place, 2 * field], in_ref[place, 2 * field + 1]], axis=1)
+            back_f[place] = dot3(bf16_pair(joined), table, False)
+
+        @pl.loop(0, slab // TR)
+        def _(line):
+            here = pl.ds(line * TR, TR)
+            values = []
+            for place in range(outer):
+                real_part = back_f[place, here, :lanes]
+                imag_part = back_f[place, here, lanes:]
+                if place:
+                    cosine = twiddle_ref[0, place : place + 1, :]
+                    sine = twiddle_ref[1, place : place + 1, :]
+                    real_part, imag_part = (
+                        real_part * cosine - imag_part * sine,
+                        real_part * sine + imag_part * cosine,
+                    )
+                values.append((real_part, imag_part))
+            for place, (real_part, imag_part) in enumerate(sixteen(values, 1.0)):
+                out_ref[0, here, place * lanes : (place + 1) * lanes] = real_part
+                out_ref[1, here, place * lanes : (place + 1) * lanes] = imag_part
+
+
+VMEM = pl.BlockSpec(memory_space=pltpu.VMEM)
+SMEM = pl.BlockSpec(memory_space=pltpu.SMEM)
+ROOM = pltpu.CompilerParams(vmem_limit_bytes=48 * 1024 * 1024)
+
+
+def slot_tiles(table, me, per_owner, cap):
+    local_tiles = table.shape[-1]
+    mine = table // per_owner == me
+    earlier = jnp.arange(local_tiles)[:, None] < jnp.arange(local_tiles)[None, :]
+    rank = jnp.sum(jnp.where(mine[..., :, None] & earlier, 1, 0), axis=-2)
+    chosen = mine[..., None, :] & (rank[..., None, :] == jnp.arange(cap)[:, None])
+    spot = table - me * per_owner
+    return jnp.sum(jnp.where(chosen, spot[..., None, :], 0), axis=-1).reshape(-1)
+
+
+def local_tiled(block_tile, cell_index, masses, plane_coef, plane_dist, source_inv):
+    groups = lax.axis_size("pix")
+    shells = lax.axis_size("shell")
+    me = lax.axis_index("pix")
+    planes, local_tiles, per_tile = cell_index.shape
+    slab = L // groups
+    outer = L // TC
+    per_owner = slab // TR * outer
+    cap = max(1, 2 * local_tiles // groups)
+    chunks = per_tile // TC
+    lines = planes * 2 * chunks * cap
+    me_list = me.reshape(1).astype(jnp.int32)
+
+    sent = pl.pallas_call(
+        partial(pack_kernel, groups, cap, chunks, per_owner),
+        in_specs=[SMEM, SMEM, VMEM, VMEM],
+        out_specs=VMEM,
+        out_shape=jax.ShapeDtypeStruct((groups, lines + 8, TC), jnp.float32),
+        scratch_shapes=[
+            pltpu.SMEM((groups,), jnp.int32),
+            pltpu.VMEM(cell_index.shape, jnp.float32),
+            pltpu.VMEM(cell_index.shape, jnp.float32),
+        ],
+        compiler_params=ROOM,
+        name="pack",
+    )(me_list, block_tile, cell_index, masses)
+    recv = lax.all_to_all(sent, "pix", split_axis=0, concat_axis=0, tiled=True)
+    near_of = plane_coef
+    far_of = plane_coef * plane_dist
+    note = jnp.concatenate([block_tile.astype(jnp.float32), near_of[:, None], far_of[:, None]], axis=1)
+
+    own = jnp.arange(planes)
+    until = own[None, :] <= own[:, None]
+    weights = [jnp.where(until, near_of[None, :] - source_inv[:, None] * far_of[None, :], 0.0)]
+    arrivals = [recv]
+    slots = [slot_tiles(block_tile.reshape(planes, groups, local_tiles), me, per_owner, cap)]
+    for step in range(1, shells):
+        pairs = [(at, at + step) for at in range(shells - step)]
+        other = lax.ppermute(note, "shell", pairs)
+        arrivals.append(lax.ppermute(recv, "shell", pairs))
+        tiles = other[:, : groups * local_tiles].astype(jnp.int32).reshape(planes, groups, local_tiles)
+        slots.append(slot_tiles(tiles, me, per_owner, cap))
+        weights.append(other[:, -2][None, :] - source_inv[:, None] * other[:, -1][None, :])
+    weight = jnp.concatenate(weights, axis=1)
+    weight = jnp.concatenate([weight, jnp.sum(weight, axis=1, keepdims=True)], axis=1)
+
+    deposit = pl.pallas_call(
+        partial(deposit_kernel, cap, chunks),
+        in_specs=[SMEM, VMEM],
+        out_specs=VMEM,
+        out_shape=jax.ShapeDtypeStruct((planes, per_owner, TR, TC), jnp.float32),
+        compiler_params=ROOM,
+        name="deposit",
+    )
+    dens = [deposit(spot, arrival) for spot, arrival in zip(slots, arrivals)]
+    parts = len(dens)
+    totals = [arrival[:, lines:, :] for arrival in arrivals]
+    twiddle = jnp.asarray(twiddle_pair(outer, TC))
+    forward = jnp.asarray(dft_block(TC, -1.0))
+    back = jnp.asarray(dft_block(TC, 1.0))
+    convergence, row_sent = pl.pallas_call(
+        partial(rows_kernel, parts),
+        in_specs=[SMEM] + [VMEM] * (2 * parts + 2),
+        out_specs=(VMEM, VMEM),
+        out_shape=(
+            jax.ShapeDtypeStruct((planes, slab, L), jnp.float32),
+            jax.ShapeDtypeStruct((groups, 2, slab, TC), jnp.float32),
+        ),
+        scratch_shapes=[
+            pltpu.VMEM((outer, slab, 2 * TC), jnp.bfloat16),
+            pltpu.VMEM((outer, slab, 2 * TC), jnp.bfloat16),
+        ],
+        compiler_params=ROOM,
+        name="rows",
+    )(weight, *dens, *totals, twiddle, forward)
+    arrived = lax.all_to_all(row_sent, "pix", split_axis=0, concat_axis=0, tiled=True)
+    col_sent = pl.pallas_call(
+        columns_kernel,
+        in_specs=[SMEM] + [VMEM] * 4,
+        out_specs=VMEM,
+        out_shape=jax.ShapeDtypeStruct((groups, 4, slab, TC), jnp.float32),
+        scratch_shapes=[
+            pltpu.VMEM((2 * slab, L), jnp.bfloat16),
+            pltpu.VMEM((2 * slab, L), jnp.bfloat16),
+            pltpu.VMEM((outer, 2 * slab, 2 * TC), jnp.float32),
+        ],
+        compiler_params=ROOM,
+        name="columns",
+    )(me_list, arrived, jnp.asarray(twiddle_pair(outer, TC).transpose(0, 2, 1)), back, forward)
+    landed = lax.all_to_all(col_sent, "pix", split_axis=0, concat_axis=0, tiled=True)
+    shear_one, shear_two = pl.pallas_call(
+        inverse_rows_kernel,
+        in_specs=[VMEM] * 3,
+        out_specs=(VMEM, VMEM),
+        out_shape=(
+            jax.ShapeDtypeStruct((planes, slab, L), jnp.float32),
+            jax.ShapeDtypeStruct((planes, slab, L), jnp.float32),
+        ),
+        scratch_shapes=[pltpu.VMEM((outer, slab, 2 * TC), jnp.float32)],
+        compiler_params=ROOM,
+        name="inverse_rows",
+    )(landed, twiddle, back)
+    return (convergence, shear_one, shear_two)
+
+
 def solution(mesh):
     placed = (
         P("shell", None),
@@ -230,8 +635,9 @@
         P("shell"),
         P("shell"),
     )
+    tiled = mesh.shape["pix"] * TC == L
     return jax.shard_map(
-        local,
+        local_tiled if tiled else local,
         mesh=mesh,
         in_specs=placed,
         out_specs=(P("shell", "pix", None), P("shell", "pix", None), P("shell", "pix", None)),

time: 508 us -> 253 us (0.50); the launches traced: 498 us -> 252 us
  waiting for transfers between devices: 147 us -> 28.6 us
  matrix products: 106 us -> 0 us
  Pallas kernels: 0 us -> 49.8 us
  local copies, waits for them, and re-layouts: 47.2 us -> 4.83 us
  other arithmetic: 31.7 us -> 2.31 us
  blocking collectives: 137 us -> 152 us
  between operations: 15.1 us -> 0.81 us
    dot_general x67 -> x0, matrix products: 106 us -> none  [the longest x16 21.1 us: deposit_group(): jnp.einsum('grk,gkc->grc', row_hot, col_hot, preferred_element_type=jnp.f...]
    all_gather x2 -> x0, waiting for transfers between devices: 65.5 us -> none  [entering(): pieces = jax.tree.map(lambda part: lax.all_gather(part, axis), value)]
    all_to_all x2 -> x1, waiting for transfers between devices: 81.6 us -> 19.7 us  [local_tiled(): recv = lax.all_to_all(sent, 'pix', split_axis=0, concat_axis=0, tiled=True)]
    pallas_call x0 -> x6, Pallas kernels: none -> 49.8 us  [the longest x2 26.9 us: local_tiled(): dens = [deposit(spot, arrival) for spot, arrival in zip(slots, arrivals)]]
    all_to_all x1 -> x2, blocking collectives: 103 us -> 152 us  [the longest x1 97.2 us: local_tiled(): lax.all_to_all(col_sent, 'pix', split_axis=0, concat_axis=0, tiled=True)]
    psum x1 -> x0, blocking collectives: 33.9 us -> none  [local(): total = lax.psum(jnp.sum(density, axis=(1, 2)), 'pix')]
    select_n x32 -> x0, other arithmetic: 23.4 us -> none  [the longest x16 11.7 us: deposit_group(): tile_cols = cell_ids % TC]
    broadcast_in_dim x16 -> x2, local copies, waits for them, and re-layouts: 11.3 us -> 0.19 us  [the longest x1 0.09 us: local_tiled(): far_of[:, None]]
  transfers between devices with their start and end apart: 4 -> 3, of which waited for: 4 -> 3; matrix products, arithmetic and copies ran while one was open for 1% -> 1% of each run, Pallas kernels for 0% -> 5%
where the time goes in v1:
time: 253 us; the launch traced here: 252 us
  blocking collectives  152 us (60%)
  Pallas kernels  49.8 us (20%)
  waiting for transfers between devices  28.6 us (11%)
  starting transfers between devices  13.6 us (5%)
  local copies, waits for them, and re-layouts  4.83 us (2%)
    all_to_all x1, blocking collectives, local_tiled(): lax.all_to_all(col_sent, 'pix', split_axis=0, concat_axis=0, tiled=True)  97.2 us
    all_to_all x1, blocking collectives, local_tiled(): lax.all_to_all(row_sent, 'pix', split_axis=0, concat_axis=0, tiled=True)  54.8 us
    pallas_call x2, Pallas kernels, local_tiled(): dens = [deposit(spot, arrival) for spot, arrival in zip(slots, arrivals)]  26.9 us
    all_to_all x1, waiting for transfers between devices, local_tiled(): recv = lax.all_to_all(sent, 'pix', split_axis=0, concat_axis=0, tiled=True)  19.7 us
    pallas_call x1, Pallas kernels, local_tiled(): pl.pallas_call(columns_kernel, in_specs=[SMEM] + [VMEM] * 4, out_specs=VM...  10.2 us
    ppermute x1, waiting for transfers between devices, local_tiled(): arrivals.append(lax.ppermute(recv, 'shell', pairs))  8.26 us
    all_to_all x1, starting transfers between devices, local_tiled(): recv = lax.all_to_all(sent, 'pix', split_axis=0, concat_axis=0, tiled=True)  7.34 us
    pallas_call x1, Pallas kernels, local_tiled(): pl.pallas_call(inverse_rows_kernel, in_specs=[VMEM] * 3, out_specs=(VMEM,...  5.33 us
  transfers between devices with their start and end apart: 3, of which 3 were waited for; matrix products, arithmetic and copies ran while one was open for 1% of the time, Pallas kernels for 5%

profile of v1, /device:TPU:1, one launch (start us, length us, event | category | flops | bytes accessed | tf_op | source)
XLA Modules:
  0.0 252.0 jit_solution(1738612213949421218)
XLA Ops:
  0.6 0.0 copy-start.9
  0.6 0.0 copy-start.11
  0.7 0.0 copy-start.10
  0.7 0.0 copy-start.3
  0.7 1.0 copy-done.3
  1.6 0.0 copy-start.5
  1.6 0.9 copy-done.5
  2.5 0.0 copy-start.6
  2.5 0.7 copy-done.6
  3.2 0.0 copy-start.7
  3.2 2.9 %pack.1 = f32[16,136,128]{2,1,0:T(8,128)} custom-call(s32[1]{0:T(128)} %bitcast.3.me_ref, s32[2,1024]{1,0:T(2,128)S(1)} %copy-done.6, s32[2,64,512]{2,1,0:T(8,128)S(1)} %copy-done.3, bf16[2,64,512]{2,1,0:T(8,128)(2,1)S(1)} %copy-done.5), custom_call_target="tpu_custom_call" | custom-call | tf_op jit(solution)/shard_map/pack/pallas_call | solution.py:537
  6.1 7.3 %all-to-all-start = ((f32[16,136,128]{2,1,0:T(8,128)}), f32[16,136,128]{2,1,0:T(8,128)S(1)}, u32[]{:S(2)}, u32[]{:S(2)}) async-start(f32[16,136,128]{2,1,0:T(8,128)} %pack.1), calls=%async_computation | async-start | bytes 2228224 | tf_op jit(solution)/shard_map/all_to_all | solution.py:550
  13.5 0.0 copy-done.7
  13.5 0.0 copy-done.9
  13.5 0.0 copy-done.11
  13.5 0.1 copy.20
  13.6 0.1 copy.19
  13.7 0.1 concatenate.8
  13.8 3.1 %collective-permute-start = (f32[2,1026]{1,0:T(2,128)S(1)}, f32[2,1026]{1,0:T(2,128)S(1)}, u32[]{:S(2)}, u32[]{:S(2)}) collective-permute-start(f32[2,1026]{1,0:T(2,128)S(1)} %concatenate.8), channel_id=1, source_target_pairs={{0,16},{1,17},{2,18},{3,19},{4,20},{5,21},{6,22},{7,23},{8,24},{9,... | collective-permute-start | bytes 24632 | tf_op jit(solution)/shard_map/ppermute | solution.py:562
  16.9 0.1 reshape.178
  17.0 0.6 collective-permute-done
  17.7 0.2 slice_reduce_fusion.1
  17.9 0.0 copy-done.10
  17.9 0.2 fusion.8
  18.1 19.7 %all-to-all-done.recv_ref = f32[16,136,128]{2,1,0:T(8,128)S(1)} async-done(((f32[16,136,128]{2,1,0:T(8,128)}), f32[16,136,128]{2,1,0:T(8,128)S(1)}, u32[]{:S(2)}, u32[]{:S(2)}) %all-to-all-start) | async-done | bytes 1114144 | tf_op jit(solution)/shard_map/all_to_all | solution.py:550
  37.8 3.2 %collective-permute-start.1 = (f32[16,136,128]{2,1,0:T(8,128)S(1)}, f32[16,136,128]{2,1,0:T(8,128)S(1)}, u32[]{:S(2)}, u32[]{:S(2)}) collective-permute-start(f32[16,136,128]{2,1,0:T(8,128)S(1)} %all-to-all-done.recv_ref), channel_id=1, source_target_pairs={{0,16},{1,17},{2,18},{3,19},{4,20},{5,21},{6,22},{7,23},{8,24},{9,... | collective-permute-start | bytes 3342344 | tf_op jit(solution)/shard_map/ppermute | solution.py:563
  41.0 0.1 copy.21
  41.1 0.1 reshape.181
  41.2 0.8 select_reduce_fusion
  42.0 1.2 select_reduce_fusion.2
  43.2 0.1 reshape.182.slots_ref
  43.3 0.1 reshape.179.slots_ref
  43.4 0.1 pad_maximum_fusion.weight_ref
  43.4 13.4 %deposit.2.refs_0_ = f32[2,128,16,128]{3,2,1,0:T(8,128)S(1)} custom-call(s32[256]{0:T(256)S(1)} %reshape.179.slots_ref, f32[16,136,128]{2,1,0:T(8,128)S(1)} %all-to-all-done.recv_ref), custom_call_target="tpu_custom_call" | custom-call | tf_op jit(solution)/shard_map/deposit/pallas_call | solution.py:578
  56.8 0.0 copy-start.2
  56.8 0.0 copy-start.8
  56.8 8.3 %collective-permute-done.1.recv_ref = f32[16,136,128]{2,1,0:T(8,128)S(1)} collective-permute-done((f32[16,136,128]{2,1,0:T(8,128)S(1)}, f32[16,136,128]{2,1,0:T(8,128)S(1)}, u32[]{:S(2)}, u32[]{:S(2)}) %collective-permute-start.1) | collective-permute-done | bytes 1114144 | tf_op jit(solution)/shard_map/ppermute | solution.py:563
  65.1 13.5 %deposit.3.refs_1_ = f32[2,128,16,128]{3,2,1,0:T(8,128)S(1)} custom-call(s32[256]{0:T(256)S(1)} %reshape.182.slots_ref, f32[16,136,128]{2,1,0:T(8,128)S(1)} %collective-permute-done.1.recv_ref), custom_call_target="tpu_custom_call" | custom-call | tf_op jit(solution)/shard_map/deposit/pallas_call | solution.py:578
  78.6 1.3 copy-done
  80.0 0.0 copy-done.2
  80.0 0.0 copy-done.8
  80.0 4.4 %rows.1 = (f32[2,128,2048]{2,1,0:T(8,128)}, f32[16,2,128,128]{3,2,1,0:T(8,128)S(1)}) custom-call(f32[2,5]{1,0:T(2,128)S(1)} %pad_maximum_fusion.weight_ref, f32[2,128,16,128]{3,2,1,0:T(8,128)S(1)} %deposit.2.refs_0_, f32[2,128,16,128]{3,2,1,0:T(8,128)} %copy-done, f32[16,8,128]{2,1,0:T(8,128)S(1)} %slice.23.refs_2_, f32[16,8,128]{2,1,0:T(8,128)S(1)} %slice.24.refs_3_, ...), custom_call_target="tpu_custom_call" | custom-call | tf_op jit(solution)/shard_map/rows/pallas_call | solution.py:584
  84.4 54.8 %all_to_all.15.in_ref = f32[16,2,128,128]{3,2,1,0:T(8,128)S(1)} all-to-all(f32[16,2,128,128]{3,2,1,0:T(8,128)S(1)} %get-tuple-element.8), channel_id=1, replica_groups=mesh['shell'=2,'pix'=16] {'pix'}, dimensions={0} | all-to-all | bytes 4194304 | tf_op jit(solution)/shard_map/all_to_all | solution.py:599
  139.2 0.0 copy-done.1
  139.2 0.0 copy-done.4
  139.2 10.2 %columns.1 = f32[16,4,128,128]{3,2,1,0:T(8,128)} custom-call(s32[1]{0:T(128)} %bitcast.3.me_ref, f32[16,2,128,128]{3,2,1,0:T(8,128)S(1)} %all_to_all.15.in_ref, f32[2,128,16]{2,1,0:T(8,128)S(1)} %copy-done.4, bf16[2,256,256]{2,1,0:T(8,128)(2,1)S(1)} %copy-done.1, bf16[2,256,256]{2,1,0:T(8,128)(2,1)S(1)} %copy-done.2), custom_call_target="tpu_custom_call" | custom-call | tf_op jit(solution)/shard_map/columns/pallas_call | solution.py:600
  149.5 97.2 %all_to_all.16.in_ref = f32[16,4,128,128]{3,2,1,0:T(8,128)S(1)} all-to-all(f32[16,4,128,128]{3,2,1,0:T(8,128)} %columns.1), channel_id=1, replica_groups=mesh['shell'=2,'pix'=16] {'pix'}, dimensions={0} | all-to-all | bytes 8388608 | tf_op jit(solution)/shard_map/all_to_all | solution.py:613
  246.7 5.3 %inverse_rows.1 = (f32[2,128,2048]{2,1,0:T(8,128)}, f32[2,128,2048]{2,1,0:T(8,128)}) custom-call(f32[16,4,128,128]{3,2,1,0:T(8,128)S(1)} %all_to_all.16.in_ref, f32[2,16,128]{2,1,0:T(8,128)S(1)} %copy-done.8, bf16[2,256,256]{2,1,0:T(8,128)(2,1)S(1)} %copy-done.1), custom_call_target="tpu_custom_call" | custom-call | tf_op jit(solution)/shard_map/inverse_rows/pallas_call | solution.py:614
  (14 shorter events, 0.1 us)
Async XLA Ops:
  0.6 12.8 %copy-start.9 = (f32[2]{0:T(128)S(1)}, f32[2]{0:T(128)}, u32[]{:S(2)}) copy-start(f32[2]{0:T(128)} %param.13) | copy-start | bytes 28
  0.6 12.8 %copy-start.11 = (f32[2]{0:T(128)S(1)}, f32[2]{0:T(128)}, u32[]{:S(2)}) copy-start(f32[2]{0:T(128)} %param.14) | copy-start | bytes 28
  0.7 17.2 %copy-start.10 = (f32[2]{0:T(128)S(1)}, f32[2]{0:T(128)}, u32[]{:S(2)}) copy-start(f32[2]{0:T(128)} %param.15) | copy-start | bytes 28
  0.7 1.0 copy-start.3
  1.6 0.9 copy-start.5
  2.5 0.7 copy-start.6
  3.2 10.2 %copy-start.7 = (s32[2,1024]{1,0:T(2,128)S(1)}, s32[2,1024]{1,0:T(2,128)}, u32[]{:S(2)}) copy-start(s32[2,1024]{1,0:T(2,128)} %table_ref.2) | copy-start | bytes 24580
  6.1 31.7 %all-to-all-start = ((f32[16,136,128]{2,1,0:T(8,128)}), f32[16,136,128]{2,1,0:T(8,128)S(1)}, u32[]{:S(2)}, u32[]{:S(2)}) async-start(f32[16,136,128]{2,1,0:T(8,128)} %pack.1), calls=%async_computation | async-start | bytes 2228224 | tf_op jit(solution)/shard_map/all_to_all | solution.py:550
  13.8 3.9 %collective-permute-start = (f32[2,1026]{1,0:T(2,128)S(1)}, f32[2,1026]{1,0:T(2,128)S(1)}, u32[]{:S(2)}, u32[]{:S(2)}) collective-permute-start(f32[2,1026]{1,0:T(2,128)S(1)} %concatenate.8), channel_id=1, source_target_pairs={{0,16},{1,17},{2,18},{3,19},{4,20},{5,21},{6,22},{7,23},{8,24},{9,... | collective-permute-start | bytes 24632 | tf_op jit(solution)/shard_map/ppermute | solution.py:562
  37.8 27.3 %collective-permute-start.1 = (f32[16,136,128]{2,1,0:T(8,128)S(1)}, f32[16,136,128]{2,1,0:T(8,128)S(1)}, u32[]{:S(2)}, u32[]{:S(2)}) collective-permute-start(f32[16,136,128]{2,1,0:T(8,128)S(1)} %all-to-all-done.recv_ref), channel_id=1, source_target_pairs={{0,16},{1,17},{2,18},{3,19},{4,20},{5,21},{6,22},{7,23},{8,24},{9,... | collective-permute-start | bytes 3342344 | tf_op jit(solution)/shard_map/ppermute | solution.py:563
  56.8 23.2 %copy-start.2 = (bf16[2,256,256]{2,1,0:T(8,128)(2,1)S(1)}, bf16[2,256,256]{2,1,0:T(8,128)(2,1)}, u32[]{:S(2)}) copy-start(bf16[2,256,256]{2,1,0:T(8,128)(2,1)} %constant.41.clone.refs_5_.back_ref) | copy-start | bytes 786436
  56.8 23.2 %copy-start.8 = (f32[2,16,128]{2,1,0:T(8,128)S(1)}, f32[2,16,128]{2,1,0:T(8,128)}, u32[]{:S(2)}) copy-start(f32[2,16,128]{2,1,0:T(8,128)} %constant.40.clone.refs_4_.twiddle_ref) | copy-start | bytes 49156
  78.6 1.3 copy-start
  84.4 54.8 %copy-start.1 = (bf16[2,256,256]{2,1,0:T(8,128)(2,1)S(1)}, bf16[2,256,256]{2,1,0:T(8,128)(2,1)}, u32[]{:S(2)}) copy-start(bf16[2,256,256]{2,1,0:T(8,128)(2,1)} %constant.42.clone.forward_ref.table_ref) | copy-start | bytes 786436
  84.4 54.8 %copy-start.4 = (f32[2,128,16]{2,1,0:T(8,128)S(1)}, f32[2,128,16]{2,1,0:T(8,128)}, u32[]{:S(2)}) copy-start(f32[2,128,16]{2,1,0:T(8,128)} %constant.43.clone.turn_ref) | copy-start | bytes 49156

commit v2 on v0

--- a/solution.py
+++ b/solution.py
@@ -3,7 +3,10 @@
 
 import jax
 import jax.numpy as jnp
+import numpy as np
 from jax import lax
+from jax.experimental import pallas as pl
+from jax.experimental.pallas import tpu as pltpu
 from jax.sharding import PartitionSpec as P
 
 L = 2048
@@ -221,19 +224,527 @@
     return (convergence, shear_one * scale, shear_two * scale)
 
 
+def bf16_pair(value):
+    high = value.astype(jnp.bfloat16)
+    return (high, (value - high.astype(jnp.float32)).astype(jnp.bfloat16))
+
+
+def dft_block(size, sign_value):
+    turn = 2.0 * np.pi / size * (np.outer(np.arange(size), np.arange(size)) % size)
+    cosine, sine = (np.cos(turn), sign_value * np.sin(turn))
+    whole = np.block([[cosine, sine], [-sine, cosine]]).astype(np.float32)
+    high = whole.astype(jnp.bfloat16)
+    low = (whole - high.astype(np.float32)).astype(jnp.bfloat16)
+    return np.stack([high, low])
+
+
+def twiddle_pair(outer, inner):
+    turn = 2.0 * np.pi / (outer * inner) * np.outer(np.arange(outer), np.arange(inner))
+    return np.stack([np.cos(turn), np.sin(turn)]).astype(np.float32)
+
+
+def quarter(values, sign_value):
+    (ar, ai), (br, bi), (cr, ci), (dr, di) = values
+    pr, pi, mr, mi = (ar + cr, ai + ci, ar - cr, ai - ci)
+    qr, qi, nr, ni = (br + dr, bi + di, br - dr, bi - di)
+    if sign_value < 0:
+        return [(pr + qr, pi + qi), (mr + ni, mi - nr), (pr - qr, pi - qi), (mr - ni, mi + nr)]
+    return [(pr + qr, pi + qi), (mr - ni, mi + nr), (pr - qr, pi - qi), (mr + ni, mi - nr)]
+
+
+def rotate(value, step, sign_value):
+    real_part, imag_part = value
+    if step == 0:
+        return value
+    if step == 4:
+        return (-sign_value * imag_part, sign_value * real_part)
+    cosine = math.cos(2.0 * math.pi * step / 16)
+    sine = sign_value * math.sin(2.0 * math.pi * step / 16)
+    return (real_part * cosine - imag_part * sine, real_part * sine + imag_part * cosine)
+
+
+def sixteen(values, sign_value, count=16):
+    inner = [quarter([values[4 * a + b] for a in range(4)], sign_value) for b in range(4)]
+    result = [None] * 16
+    for k in range(4):
+        turned_values = [rotate(inner[b][k], b * k, sign_value) for b in range(4)]
+        for place, value in enumerate(quarter(turned_values, sign_value)):
+            result[k + 4 * place] = value
+    return result[:count]
+
+
+def dot3(left, right):
+    mul = partial(jnp.dot, preferred_element_type=jnp.float32)
+    (left_high, left_low), (right_high, right_low) = (left, right)
+    return mul(left_high, right_high) + (mul(left_low, right_high) + mul(left_high, right_low))
+
+
+def widen_kernel(cell_ref, mass_ref, out_ref):
+    out_ref[0] = cell_ref[...].astype(jnp.float32)
+    out_ref[1] = mass_ref[...].astype(jnp.float32)
+
+
+def pack_kernel(half, cap, per_owner, from_ref, table_ref, raw_ref, out_ref, count_ref):
+    _, planes, local_tiles, per_tile = raw_ref.shape
+    groups = out_ref.shape[0]
+    chunks = per_tile // TC
+    lines = 2 * chunks * cap
+    out_ref[...] = jnp.zeros(out_ref.shape, jnp.float32)
+    base = from_ref[0] * local_tiles
+    for plane in range(planes):
+
+        @pl.loop(0, groups)
+        def _(slot):
+            count_ref[slot] = 0
+
+        @pl.loop(0, local_tiles // 8)
+        def _(bunch):
+            here = pl.ds(pl.multiple_of(bunch * 8, 8), 8)
+            lists = [raw_ref[kind, plane, here, :] for kind in range(2)]
+            for at in range(8):
+                owner = lax.div(table_ref[plane, base + bunch * 8 + at], per_owner)
+                low = lax.rem(owner, half)
+                side = lax.rem(lax.div(owner, half) + lax.rem(low, 2), 2)
+                place = side * half + low
+                rank = count_ref[place]
+                count_ref[place] = rank + 1
+                for kind, values in enumerate(lists):
+                    for chunk in range(chunks):
+                        row = plane * lines + kind * chunks * cap + chunk * cap + rank
+                        out_ref[place, pl.ds(row, 1), :] = values[at : at + 1, chunk * TC : (chunk + 1) * TC]
+
+        total = jnp.sum(raw_ref[1, plane], axis=0, keepdims=True)
+        total = jnp.sum(total, axis=1, keepdims=True)
+        line = jnp.broadcast_to(total, (1, TC))
+        for place in range(groups):
+            out_ref[place, planes * lines + plane : planes * lines + plane + 1, :] = line
+
+
+def deposit_kernel(cap, chunks, slots_ref, recv_ref, out_ref):
+    out_ref[...] = jnp.zeros(out_ref.shape, jnp.float32)
+    all_planes = out_ref.shape[0]
+    planes = all_planes // 2
+    half = recv_ref.shape[0] // 2
+    width = 32
+    bunch = 4
+    parts = TC // width
+    low = lax.broadcasted_iota(jnp.int32, (TR, TC), 0).astype(jnp.float32)
+    lines = [(low + float(TR * part)).astype(jnp.bfloat16) for part in range(parts)]
+    one = jnp.ones((TR, TC), jnp.bfloat16)
+    none = jnp.zeros((TR, TC), jnp.bfloat16)
+
+    def spread(value, slot):
+        return jnp.broadcast_to(value[slot : slot + 1, :], (TR, TC)).astype(jnp.bfloat16)
+
+    for plane in range(all_planes):
+        start = (plane % planes) * 2 * chunks * cap
+
+        @pl.loop(0, half, unroll=4)
+        def _(source):
+            place = (plane // planes) * half + source
+            cells = [recv_ref[place, start + k * cap : start + (k + 1) * cap, :] for k in range(chunks)]
+            weights = [
+                recv_ref[place, start + (chunks + k) * cap : start + (chunks + k + 1) * cap, :] for k in range(chunks)
+            ]
+            rows = [jnp.floor(cell * (1.0 / TC)) for cell in cells]
+            strips = [jnp.floor(cell * (1.0 / width)) for cell in cells]
+            cols = [cell - strip * float(width) for cell, strip in zip(cells, strips)]
+            rows = [row + (strip - row * float(parts)) * float(TR) for row, strip in zip(rows, strips)]
+            sums = []
+            for first in range(0, cap, bunch):
+                row_hot = []
+                col_hot = []
+                for k in range(chunks):
+                    row_lines = []
+                    col_lines = []
+                    for slot in range(first, first + bunch):
+                        row = spread(rows[k], slot)
+                        weight = spread(weights[k], slot)
+                        row_lines += [jnp.where(lines[at] == row, weight, none) for at in range(parts)]
+                        col = spread(cols[k], slot)
+                        col_lines += [jnp.where(lines[at] == col, one, none) for at in range(width // TR)]
+                    row_hot.append(jnp.concatenate(row_lines, axis=0))
+                    col_hot.append(jnp.concatenate(col_lines, axis=0))
+                done = lax.dot_general(
+                    jnp.concatenate(row_hot, axis=1),
+                    jnp.concatenate(col_hot, axis=1),
+                    (((1,), (1,)), ((), ())),
+                    preferred_element_type=jnp.float32,
+                )
+                for at in range(bunch):
+                    base = at * TR * parts
+                    side = slice(at * width, (at + 1) * width)
+                    strips_of = [done[base + j * TR : base + (j + 1) * TR, side] for j in range(parts)]
+                    sums.append(jnp.concatenate(strips_of, axis=1))
+            for slot in range(cap):
+                tile = slots_ref[(plane * half + source) * cap + slot]
+                out_ref[plane, tile] = out_ref[plane, tile] + sums[slot]
+
+
+def rows_kernel(
+    cap, chunks, weight_ref, side_ref, slots_ref, near_dens_ref, near_ref, far_ref, twiddle_ref, table_ref,
+    mine_ref, other_ref, out_ref, high_ref, low_ref, far_dens_ref,
+):
+    step = pl.program_id(0)
+    pl.when(step == 0)(lambda: deposit_kernel(cap, chunks, slots_ref, far_ref, far_dens_ref))
+    first_line = 2 * (far_dens_ref.shape[0] // 2) * cap * chunks
+    planes, slab, length = mine_ref.shape
+    all_planes = far_dens_ref.shape[0]
+    outer = length // TC
+    first_tile = step * (slab // TR * outer)
+    half = near_ref.shape[0] // 2
+    scales = []
+    for plane in range(all_planes):
+        line = plane % planes
+        total = jnp.zeros((1, TC), jnp.float32)
+        for source in range(half):
+            place = (plane // planes) * half + source
+            total = total + near_ref[place, line : line + 1, :]
+            total = total + far_ref[place, first_line + line : first_line + line + 1, :]
+        scales.append(float(length * length) / total)
+    table = (table_ref[0], table_ref[1])
+    for side, conv_ref in enumerate((mine_ref, other_ref)):
+        here_maps = [side * planes + i for i in range(planes)]
+        factors = [
+            [jnp.broadcast_to(weight_ref[i, j] * scales[j], (TR, TC)) for j in range(all_planes)] for i in here_maps
+        ]
+        shift = [weight_ref[i, all_planes] for i in here_maps]
+
+        for line in range(slab // TR):
+            values = []
+            here = slice(line * TR, (line + 1) * TR)
+            for col in range(outer):
+                at = line * outer + col
+                tiles = [near_dens_ref[j, at] + far_dens_ref[j, first_tile + at] for j in range(all_planes)]
+                pair = []
+                for i in range(planes):
+                    field = tiles[0] * factors[i][0]
+                    for tile, factor in zip(tiles[1:], factors[i][1:]):
+                        field = field + tile * factor
+                    field = field - shift[i]
+                    conv_ref[i, here, col * TC : (col + 1) * TC] = field
+                    pair.append(field)
+                values.append(tuple(pair))
+            for place, (real_part, imag_part) in enumerate(sixteen(values, -1.0)):
+                if place:
+                    cosine = twiddle_ref[0, place : place + 1, :]
+                    sine = twiddle_ref[1, place : place + 1, :]
+                    real_part, imag_part = (
+                        real_part * cosine + imag_part * sine,
+                        imag_part * cosine - real_part * sine,
+                    )
+                spot = slice(place * slab + line * TR, place * slab + (line + 1) * TR)
+                for at, value in enumerate((real_part, imag_part)):
+                    high, low = bf16_pair(value)
+                    high_ref[spot, at * TC : (at + 1) * TC] = high
+                    low_ref[spot, at * TC : (at + 1) * TC] = low
+
+        base = side_ref[side] * half
+        done = dot3((high_ref[...], low_ref[...]), table)
+        for place in range(outer):
+            here = slice(place * slab, (place + 1) * slab)
+            out_ref[base + place // 2, place % 2, 0] = done[here, :TC]
+            out_ref[base + place // 2, place % 2, 1] = done[here, TC:]
+
+
+def turned(turn_ref, place, here, value, sign_value):
+    if place == 0:
+        return value
+    real_part, imag_part = value
+    shape = real_part.shape
+    cosine = jnp.broadcast_to(turn_ref[0, here, place : place + 1], shape)
+    sine = jnp.broadcast_to(turn_ref[1, here, place : place + 1], shape) * sign_value
+    return (real_part * cosine - imag_part * sine, real_part * sine + imag_part * cosine)
+
+
+def columns_kernel(
+    order, me_ref, in_ref, turn_ref, forward_ref, back_ref, out_ref, high_ref, low_ref, spectrum_ref, back_f
+):
+    outer, _, _, inner, lanes = in_ref.shape
+    length = outer * inner
+    forward = (forward_ref[0], forward_ref[1])
+    back = (back_ref[0], back_ref[1])
+
+    @pl.loop(0, inner // TR)
+    def _(line):
+        here = pl.ds(line * TR, TR)
+        there = pl.ds(inner + line * TR, TR)
+        values = [(in_ref[place, 0, 0, here, :], in_ref[place, 0, 1, here, :]) for place in order]
+        for place, value in enumerate(sixteen(values, -1.0)):
+            for spot, part in zip((here, there), turned(turn_ref, place, here, value, -1.0)):
+                high, low = bf16_pair(part)
+                high_ref[spot, place * lanes : (place + 1) * lanes] = high
+                low_ref[spot, place * lanes : (place + 1) * lanes] = low
+
+    for bunch in range(outer // 2):
+        span = slice(bunch * 2 * lanes, (bunch + 1) * 2 * lanes)
+        spectrum_ref[:, span] = dot3(forward, (high_ref[:, span], low_ref[:, span]))
+
+    middle = length // 2
+    wave_v = lax.broadcasted_iota(jnp.int32, (inner, lanes), 1) * outer + (2 * me_ref[0] + pl.program_id(0))
+    keep_v = wave_v != middle
+    sv = jnp.where(wave_v >= middle, wave_v - length, wave_v).astype(jnp.float32)
+    line_u = lax.broadcasted_iota(jnp.int32, (inner, lanes), 0) * outer
+    flip = jnp.where(me_ref[1] > 0, -1.0, 1.0)
+    for place in range(outer):
+        side = slice(place * lanes, (place + 1) * lanes)
+        wave_u = line_u + place
+        su = jnp.where(wave_u >= middle, wave_u - length, wave_u).astype(jnp.float32)
+        scale = 1.0 / (float(length) * float(length))
+        keep = jnp.where(keep_v & (wave_u != middle), scale * flip if place % 2 else scale, 0.0)
+        factor = keep / jnp.maximum(sv * sv + su * su, 1.0)
+        first = factor * (sv * sv - su * su)
+        second = factor * (2.0 * sv * su)
+        real_part = spectrum_ref[:inner, side]
+        imag_part = spectrum_ref[inner:, side]
+        stacked = jnp.concatenate(
+            [
+                jnp.concatenate([real_part * first, real_part * second], axis=1),
+                jnp.concatenate([imag_part * first, imag_part * second], axis=1),
+            ],
+            axis=0,
+        )
+        back_f[place] = dot3(back, bf16_pair(stacked))
+
+    half = outer // 2
+
+    @pl.loop(0, inner // TR)
+    def _(line):
+        here = pl.ds(line * TR, TR)
+        there = pl.ds(inner + line * TR, TR)
+        for field in range(2):
+            side = slice(field * lanes, (field + 1) * lanes)
+            values = [
+                turned(turn_ref, place, here, (back_f[place, here, side], back_f[place, there, side]), 1.0)
+                for place in range(outer)
+            ]
+            for low, (real_part, imag_part) in enumerate(sixteen(values, 1.0, half)):
+                out_ref[low, 0, field, 0, here, :] = real_part
+                out_ref[low, 0, field, 1, here, :] = imag_part
+
+
+def inverse_rows_kernel(in_ref, twiddle_ref, table_ref, first_ref, second_ref, back_f):
+    half, _, _, _, slab, lanes = in_ref.shape
+    outer = 2 * half
+    table = (table_ref[0], table_ref[1])
+    for field, out_ref in enumerate((first_ref, second_ref)):
+        joined = [
+            jnp.concatenate([in_ref[place // 2, place % 2, field, part] for place in range(outer)], axis=0)
+            for part in range(2)
+        ]
+        back_f[...] = dot3(bf16_pair(jnp.concatenate(joined, axis=1)), table)
+        for line in range(slab // TR):
+            here = slice(line * TR, (line + 1) * TR)
+            values = []
+            for place in range(outer):
+                spot = slice(place * slab + line * TR, place * slab + (line + 1) * TR)
+                real_part = back_f[spot, :lanes]
+                imag_part = back_f[spot, lanes:]
+                if place:
+                    cosine = twiddle_ref[0, place : place + 1, :]
+                    sine = twiddle_ref[1, place : place + 1, :]
+                    real_part, imag_part = (
+                        real_part * cosine - imag_part * sine,
+                        real_part * sine + imag_part * cosine,
+                    )
+                values.append((real_part, imag_part))
+            for place, (real_part, imag_part) in enumerate(sixteen(values, 1.0)):
+                out_ref[0, here, place * lanes : (place + 1) * lanes] = real_part
+                out_ref[1, here, place * lanes : (place + 1) * lanes] = imag_part
+
+
+VMEM = pl.BlockSpec(memory_space=pltpu.VMEM)
+SMEM = pl.BlockSpec(memory_space=pltpu.SMEM)
+
+
+def room(mib):
+    return pltpu.CompilerParams(vmem_limit_bytes=mib * 1024 * 1024)
+
+
+def whole(shape):
+    return pl.BlockSpec(shape, lambda step: (0,) * len(shape))
+
+
+def slot_tiles(table, held, per_owner, cap):
+    local_tiles = table.shape[-1]
+    mine = table // per_owner == held
+    earlier = jnp.arange(local_tiles)[:, None] < jnp.arange(local_tiles)[None, :]
+    rank = jnp.sum(jnp.where(mine[..., :, None] & earlier, 1, 0), axis=-2)
+    chosen = mine[..., None, :] & (rank[..., None, :] == jnp.arange(cap)[:, None])
+    spot = table - held * per_owner
+    return jnp.sum(jnp.where(chosen, spot[..., None, :], 0), axis=-1)
+
+
+def cube_exchange(value):
+    return lax.all_to_all(value, ("shell", "low"), split_axis=0, concat_axis=0, tiled=True)
+
+
+def local_cube(block_tile, cell_index, masses, plane_coef, plane_dist, source_inv):
+    half = lax.axis_size("low")
+    groups = 2 * half
+    shell = lax.axis_index("shell")
+    upper = lax.axis_index("upper")
+    low = lax.axis_index("low")
+    planes, local_tiles, per_tile = cell_index.shape
+    slab = L // groups
+    outer = L // TC
+    per_owner = slab // TR * outer
+    cap = max(1, 2 * local_tiles // groups)
+    chunks = per_tile // TC
+    lines = 2 * chunks * cap * planes
+    part = (shell + low) % 2
+    held = part * half + low
+    order = [((s // half + s % 2) % 2) * half + s % half for s in range(groups)]
+
+    raw = pl.pallas_call(
+        widen_kernel,
+        in_specs=[VMEM, VMEM],
+        out_specs=VMEM,
+        out_shape=jax.ShapeDtypeStruct((2, planes, local_tiles, per_tile), jnp.float32),
+        compiler_params=room(8),
+        name="widen",
+    )(cell_index, masses)
+    raw_far = lax.ppermute(raw, "upper", [(0, 1), (1, 0)])
+
+    def pack(source, lists):
+        return pl.pallas_call(
+            partial(pack_kernel, half, cap, per_owner),
+            in_specs=[SMEM, SMEM, VMEM],
+            out_specs=VMEM,
+            out_shape=jax.ShapeDtypeStruct((groups, lines + 8, TC), jnp.float32),
+            scratch_shapes=[pltpu.SMEM((groups,), jnp.int32)],
+            compiler_params=room(12),
+            name="pack",
+        )(source.reshape(1).astype(jnp.int32), block_tile, lists)
+
+    near = cube_exchange(pack(upper * half + low, raw))
+    far = cube_exchange(pack((1 - upper) * half + low, raw_far))
+
+    note = jnp.concatenate(
+        [block_tile.astype(jnp.float32), plane_coef[:, None], (plane_coef * plane_dist)[:, None], source_inv[:, None]],
+        axis=1,
+    )
+    other = lax.ppermute(note, "shell", [(0, 1), (1, 0)])
+    both = jnp.where(shell == 0, jnp.concatenate([note, other]), jnp.concatenate([other, note]))
+    tiles = slot_tiles(
+        both[:, : groups * local_tiles].astype(jnp.int32).reshape(2 * planes, groups, local_tiles), held, per_owner, cap
+    )
+    tiles = tiles.reshape(2 * planes, 2, half, cap)
+    near_slots = lax.dynamic_index_in_dim(tiles, upper, axis=1, keepdims=False).reshape(-1)
+    far_slots = lax.dynamic_index_in_dim(tiles, 1 - upper, axis=1, keepdims=False).reshape(-1)
+    maps = jnp.concatenate([shell * planes + jnp.arange(planes), (1 - shell) * planes + jnp.arange(planes)])
+    inverse = jnp.concatenate([note[:, -1], other[:, -1]])
+    weight = jnp.where(
+        jnp.arange(2 * planes)[None, :] <= maps[:, None], both[None, :, -3] - inverse[:, None] * both[None, :, -2], 0.0
+    )
+    weight = jnp.concatenate([weight, jnp.sum(weight, axis=1, keepdims=True)], axis=1)
+
+    near_dens = pl.pallas_call(
+        partial(deposit_kernel, cap, chunks),
+        in_specs=[SMEM, VMEM],
+        out_specs=VMEM,
+        out_shape=pltpu.HBM((2 * planes, per_owner, TR, TC), jnp.float32),
+        compiler_params=room(16),
+        name="deposit",
+    )(near_slots, near)
+    twiddle = jnp.asarray(twiddle_pair(outer, TC))
+    turn = jnp.asarray(twiddle_pair(outer, TC).transpose(0, 2, 1))
+    minus = jnp.asarray(dft_block(TC, -1.0))
+    plus = jnp.asarray(dft_block(TC, 1.0))
+    field = jax.ShapeDtypeStruct((planes, slab, L), jnp.float32)
+    some = 2 * TR
+    conv_mine, conv_other, row_sent = pl.pallas_call(
+        partial(rows_kernel, cap, chunks),
+        grid=(slab // some,),
+        in_specs=[
+            SMEM,
+            SMEM,
+            SMEM,
+            pl.BlockSpec((2 * planes, some // TR * outer, TR, TC), lambda step: (0, step, 0, 0)),
+            pl.BlockSpec((groups, 8, TC), lambda step: (0, lines // 8, 0)),
+            whole(far.shape),
+            whole(twiddle.shape),
+            whole(minus.shape),
+        ],
+        out_specs=(
+            pl.BlockSpec((planes, some, L), lambda step: (0, step, 0)),
+            pl.BlockSpec((planes, some, L), lambda step: (0, step, 0)),
+            pl.BlockSpec((groups, 2, 2, some, TC), lambda step: (0, 0, 0, step, 0)),
+        ),
+        out_shape=(
+            pltpu.HBM(field.shape, field.dtype),
+            pltpu.HBM(field.shape, field.dtype),
+            pltpu.HBM((groups, 2, 2, slab, TC), jnp.float32),
+        ),
+        scratch_shapes=[
+            pltpu.VMEM((outer * some, 2 * TC), jnp.bfloat16),
+            pltpu.VMEM((outer * some, 2 * TC), jnp.bfloat16),
+            pltpu.VMEM((2 * planes, per_owner, TR, TC), jnp.float32),
+        ],
+        compiler_params=room(28),
+        name="rows",
+    )(weight, jnp.stack([shell, 1 - shell]).astype(jnp.int32), far_slots, near_dens, near, far, twiddle, minus)
+    arrived = lax.all_to_all(row_sent, ("shell", "low"), split_axis=0, concat_axis=0, tiled=True)
+    swaps = []
+    for side in range(2):
+        for top in range(2):
+            for at in range(half):
+                if (side + at) % 2 == top:
+                    swaps.append(((side * 2 + top) * half + at, ((1 - side) * 2 + top) * half + at))
+    conv_held = lax.ppermute(conv_other, ("shell", "upper", "low"), swaps)
+    convergence = jnp.where(part == upper, conv_mine, conv_held)
+    col_sent = pl.pallas_call(
+        partial(columns_kernel, order),
+        grid=(2,),
+        in_specs=[
+            SMEM,
+            pl.BlockSpec((groups, 1, 2, slab, TC), lambda step: (0, step, 0, 0, 0)),
+            whole(turn.shape),
+            whole(plus.shape),
+            whole(minus.shape),
+        ],
+        out_specs=pl.BlockSpec((half, 1, 2, 2, slab, TC), lambda step: (0, step, 0, 0, 0, 0)),
+        out_shape=pltpu.HBM((half, 2, 2, 2, slab, TC), jnp.float32),
+        scratch_shapes=[
+            pltpu.VMEM((2 * slab, L), jnp.bfloat16),
+            pltpu.VMEM((2 * slab, L), jnp.bfloat16),
+            pltpu.VMEM((2 * slab, L), jnp.float32),
+            pltpu.VMEM((outer, 2 * slab, 2 * TC), jnp.float32),
+        ],
+        compiler_params=room(32),
+        name="columns",
+    )(jnp.stack([low, upper]).astype(jnp.int32), arrived, turn, plus, minus)
+    landed = lax.all_to_all(col_sent, "low", split_axis=0, concat_axis=0, tiled=True)
+    shear_one, shear_two = pl.pallas_call(
+        inverse_rows_kernel,
+        grid=(slab // some,),
+        in_specs=[
+            pl.BlockSpec((half, 2, 2, 2, some, TC), lambda step: (0, 0, 0, 0, step, 0)),
+            whole(twiddle.shape),
+            whole(plus.shape),
+        ],
+        out_specs=(
+            pl.BlockSpec((planes, some, L), lambda step: (0, step, 0)),
+            pl.BlockSpec((planes, some, L), lambda step: (0, step, 0)),
+        ),
+        out_shape=(field, field),
+        scratch_shapes=[pltpu.VMEM((outer * some, 2 * TC), jnp.float32)],
+        compiler_params=room(24),
+        name="inverse_rows",
+    )(landed, twiddle, plus)
+    return (convergence, shear_one, shear_two)
+
+
 def solution(mesh):
-    placed = (
-        P("shell", None),
-        P("shell", "pix", None),
-        P("shell", "pix", None),
-        P("shell"),
-        P("shell"),
-        P("shell"),
-    )
-    return jax.shard_map(
-        local,
-        mesh=mesh,
-        in_specs=placed,
-        out_specs=(P("shell", "pix", None), P("shell", "pix", None), P("shell", "pix", None)),
-        check_vma=False,
-    )
+    shells, groups = (mesh.shape["shell"], mesh.shape["pix"])
+    body, pix = (local, "pix")
+    if shells == 2 and groups * TC == L:
+        body, pix = (local_cube, ("upper", "low"))
+        mesh = type(mesh)(mesh.devices.reshape(shells, 2, groups // 2), ("shell", "upper", "low"))
+    placed = (P("shell", None), P("shell", pix, None), P("shell", pix, None), P("shell"), P("shell"), P("shell"))
+    out = P("shell", pix, None)
+
+    def step(*arrays):
+        return body(*arrays)
+
+    return jax.shard_map(step, mesh=mesh, in_specs=placed, out_specs=(out, out, out), check_vma=False)

time: 508 us -> 219 us (0.43); the launches traced: 498 us -> 218 us
  blocking collectives: 137 us -> 0 us
  matrix products: 106 us -> 0 us
  Pallas kernels: 0 us -> 53.3 us
  local copies, waits for them, and re-layouts: 47.2 us -> 5.88 us
  other arithmetic: 31.7 us -> 5.87 us
  waiting for transfers between devices: 147 us -> 122 us
  starting transfers between devices: 14 us -> 30.1 us
  between operations: 15.1 us -> 0.79 us
    dot_general x67 -> x0, matrix products: 106 us -> none  [the longest x16 21.1 us: deposit_group(): jnp.einsum('grk,gkc->grc', row_hot, col_hot, preferred_element_type=jnp.f...]
    all_to_all x1 -> x0, blocking collectives: 103 us -> none  [local(): lax.all_to_all(columns_to_sending(stacked, groups, slab, cols_own), 'pix'...]
    all_gather x2 -> x0, waiting for transfers between devices: 65.5 us -> none  [entering(): pieces = jax.tree.map(lambda part: lax.all_gather(part, axis), value)]
    pallas_call x0 -> x7, Pallas kernels: none -> 53.3 us  [the longest x1 15.5 us: local_cube(): pl.pallas_call(partial(columns_kernel, order), grid=(2,), in_specs=[SMEM,...]
    ppermute x0 -> x3, waiting for transfers between devices: none -> 45.9 us  [the longest x1 26.1 us: local_cube(): conv_held = lax.ppermute(conv_other, ('shell', 'upper', 'low'), swaps)]
    psum x1 -> x0, blocking collectives: 33.9 us -> none  [local(): total = lax.psum(jnp.sum(density, axis=(1, 2)), 'pix')]
    select_n x32 -> x3, other arithmetic: 23.4 us -> 3.46 us  [the longest x1 3.26 us: local_cube(): convergence = jnp.where(part == upper, conv_mine, conv_held)]
    all_to_all x2 -> x4, starting transfers between devices: 13.7 us -> 25.2 us  [the longest x2 14.5 us: cube_exchange(): lax.all_to_all(value, ('shell', 'low'), split_axis=0, concat_axis=0, tile...]
  transfers between devices with their start and end apart: 4 -> 7, of which waited for: 4 -> 5; matrix products, arithmetic and copies ran while one was open for 1% -> 3% of each run, Pallas kernels for 0% -> 6%
where the time goes in v2:
time: 219 us; the launch traced here: 218 us
  waiting for transfers between devices  122 us (56%)
  Pallas kernels  53.3 us (24%)
  starting transfers between devices  30.1 us (14%)
  local copies, waits for them, and re-layouts  5.88 us (3%)
  other arithmetic  5.87 us (3%)
    all_to_all x1, waiting for transfers between devices, local_cube(): lax.all_to_all(row_sent, ('shell', 'low'), split_axis=0, concat_axis=0, t...  55.9 us
    ppermute x1, waiting for transfers between devices, local_cube(): conv_held = lax.ppermute(conv_other, ('shell', 'upper', 'low'), swaps)  26.1 us
    ppermute x1, waiting for transfers between devices, local_cube(): raw_far = lax.ppermute(raw, 'upper', [(0, 1), (1, 0)])  19.8 us
    all_to_all x1, waiting for transfers between devices, local_cube(): lax.all_to_all(col_sent, 'low', split_axis=0, concat_axis=0, tiled=True)  16.7 us
    pallas_call x1, Pallas kernels, local_cube(): pl.pallas_call(partial(columns_kernel, order), grid=(2,), in_specs=[SMEM,...  15.5 us
    pallas_call x1, Pallas kernels, local_cube(): pl.pallas_call(partial(rows_kernel, cap, chunks), grid=(slab // some,), i...  14.7 us
    all_to_all x2, starting transfers between devices, cube_exchange(): lax.all_to_all(value, ('shell', 'low'), split_axis=0, concat_axis=0, tile...  14.5 us
    pallas_call x1, Pallas kernels, local_cube(): pl.pallas_call(partial(deposit_kernel, cap, chunks), in_specs=[SMEM, VMEM...  9.38 us
  transfers between devices with their start and end apart: 7, of which 5 were waited for; matrix products, arithmetic and copies ran while one was open for 3% of the time, Pallas kernels for 6%

profile of v2, /device:TPU:1, one launch (start us, length us, event | category | flops | bytes accessed | tf_op | source)
XLA Modules:
  0.0 217.8 jit_solution(10561167084975922341)
XLA Ops:
  0.6 0.9 copy-done.3
  1.6 0.9 copy-done.5
  2.5 0.0 copy-start.9
  2.5 0.0 copy-start.10
  2.6 0.0 copy-start.11
  2.6 0.0 copy-start.6
  2.6 0.7 copy-done.6
  3.3 3.7 %pack.2 = f32[16,136,128]{2,1,0:T(8,128)} custom-call(s32[1]{0:T(128)} %bitcast.7.from_ref, s32[2,1024]{1,0:T(2,128)S(1)} %copy-done.6, f32[2,2,64,512]{3,2,1,0:T(8,128)S(1)} %widen.1.raw_ref), custom_call_target="tpu_custom_call" | custom-call | tf_op jit(solution)/shard_map/pack/pallas_call | solution.py:610
  7.0 6.2 %all-to-all-start = ((f32[16,136,128]{2,1,0:T(8,128)}), f32[16,136,128]{2,1,0:T(8,128)S(1)}, u32[]{:S(2)}, u32[]{:S(2)}) async-start(f32[16,136,128]{2,1,0:T(8,128)} %pack.2), calls=%async_computation | async-start | bytes 2228224 | tf_op jit(solution)/shard_map/all_to_all | solution.py:579
  13.2 2.3 %collective-permute-start.1 = (f32[2,2,64,512]{3,2,1,0:T(8,128)S(1)}, f32[2,2,64,512]{3,2,1,0:T(8,128)S(1)}, u32[]{:S(2)}, u32[]{:S(2)}) collective-permute-start(f32[2,2,64,512]{3,2,1,0:T(8,128)S(1)} %widen.1.raw_ref), channel_id=1, source_target_pairs={{0,8},{8,0},{1,9},{9,1},{2,10},{10,2},{3,11},{11,3},{4,12},{12,4},... | collective-permute-start | bytes 1572872 | tf_op jit(solution)/shard_map/ppermute | solution.py:607
  15.6 0.0 copy-done.10
  15.6 0.1 copy.22
  15.7 0.1 copy.23
  15.8 0.1 copy.21
  15.9 0.1 concatenate.19
  16.0 1.4 collective-permute-start
  17.3 19.8 %collective-permute-done.1.raw_ref = f32[2,2,64,512]{3,2,1,0:T(8,128)S(1)} collective-permute-done((f32[2,2,64,512]{3,2,1,0:T(8,128)S(1)}, f32[2,2,64,512]{3,2,1,0:T(8,128)S(1)}, u32[]{:S(2)}, u32[]{:S(2)}) %collective-permute-start.1) | collective-permute-done | bytes 524320 | tf_op jit(solution)/shard_map/ppermute | solution.py:607
  37.1 3.7 %pack.3 = f32[16,136,128]{2,1,0:T(8,128)} custom-call(s32[1]{0:T(128)} %bitcast.8.from_ref, s32[2,1024]{1,0:T(2,128)S(1)} %copy-done.7, f32[2,2,64,512]{3,2,1,0:T(8,128)S(1)} %collective-permute-done.1.raw_ref), custom_call_target="tpu_custom_call" | custom-call | tf_op jit(solution)/shard_map/pack/pallas_call | solution.py:610
  40.8 0.0 all-to-all-done.recv_ref.near_ref
  40.8 8.2 %all-to-all-start.1 = ((f32[16,136,128]{2,1,0:T(8,128)}), f32[16,136,128]{2,1,0:T(8,128)S(1)}, u32[]{:S(2)}, u32[]{:S(2)}) async-start(f32[16,136,128]{2,1,0:T(8,128)} %pack.3), calls=%async_computation.1 | async-start | bytes 2228224 | tf_op jit(solution)/shard_map/all_to_all | solution.py:579
  49.1 0.1 pad_add_fusion
  49.1 0.1 pad_add_fusion.1.side_ref
  49.2 0.0 collective-permute-done
  49.2 0.2 slice_reduce_fusion.2
  49.4 0.1 pad_maximum_fusion.1
  49.5 0.2 slice_reduce_fusion.1
  49.7 0.2 subtract_select_fusion
  49.9 0.1 copy.24
  50.0 0.1 reshape.106
  50.1 0.8 select_reduce_fusion
  50.9 1.2 select_reduce_fusion.1
  52.1 0.1 reshape.109.slots_ref
  52.2 0.1 reshape.108.slots_ref
  52.3 0.1 pad_maximum_fusion.weight_ref
  52.4 9.4 %deposit.1.near_dens_ref = f32[4,128,16,128]{3,2,1,0:T(8,128)} custom-call(s32[256]{0:T(256)S(1)} %reshape.109.slots_ref, f32[16,136,128]{2,1,0:T(8,128)S(1)} %all-to-all-done.recv_ref.near_ref), custom_call_target="tpu_custom_call" | custom-call | tf_op jit(solution)/shard_map/deposit/pallas_call | solution.py:642
  61.8 3.3 %all-to-all-done.1.far_ref = f32[16,136,128]{2,1,0:T(8,128)S(1)} async-done(((f32[16,136,128]{2,1,0:T(8,128)}), f32[16,136,128]{2,1,0:T(8,128)S(1)}, u32[]{:S(2)}, u32[]{:S(2)}) %all-to-all-start.1) | async-done | bytes 1114144 | tf_op jit(solution)/shard_map/all_to_all | solution.py:579
  65.1 2.2 %copy-done = f32[4,128,16,128]{3,2,1,0:T(8,128)S(1)} copy-done((f32[4,128,16,128]{3,2,1,0:T(8,128)S(1)}, f32[4,128,16,128]{3,2,1,0:T(8,128)}, u32[]{:S(2)}) %copy-start) | copy-done | bytes 4194328
  67.3 14.7 %rows.1 = (f32[2,128,2048]{2,1,0:T(8,128)}, f32[2,128,2048]{2,1,0:T(8,128)}, f32[16,2,2,128,128]{4,3,2,1,0:T(8,128)}) custom-call(f32[4,5]{1,0:T(4,128)S(1)} %pad_maximum_fusion.weight_ref, s32[2]{0:T(128)S(1)} %pad_add_fusion.1.side_ref, s32[256]{0:T(256)S(1)} %reshape.108.slots_ref, f32[4,128,16,128]{3,2,1,0:T(8,128)S(1)} %copy-done, ...), custom_call_target="tpu_custom_call" | custom-call | tf_op jit(solution)/shard_map/rows/pallas_call | solution.py:656
  81.9 5.3 %all-to-all-start.2 = ((f32[16,2,2,128,128]{4,3,2,1,0:T(8,128)}), f32[16,2,2,128,128]{4,3,2,1,0:T(8,128)}, u32[]{:S(2)}, u32[]{:S(2)}) async-start(f32[16,2,2,128,128]{4,3,2,1,0:T(8,128)} %get-tuple-element.10), calls=%async_computation.2 | async-start | bytes 8388608 | tf_op jit(solution)/shard_map/all_to_all | solution.py:687
  87.3 0.1 pad_add_fusion.2.me_ref
  87.4 55.9 %all-to-all-done.2.in_ref = f32[16,2,2,128,128]{4,3,2,1,0:T(8,128)} async-done(((f32[16,2,2,128,128]{4,3,2,1,0:T(8,128)}), f32[16,2,2,128,128]{4,3,2,1,0:T(8,128)}, u32[]{:S(2)}, u32[]{:S(2)}) %all-to-all-start.2) | async-done | bytes 4194336 | tf_op jit(solution)/shard_map/all_to_all | solution.py:687
  143.3 15.5 %columns.1 = f32[8,2,2,2,128,128]{5,4,3,2,1,0:T(8,128)} custom-call(s32[2]{0:T(128)S(1)} %pad_add_fusion.2.me_ref, f32[16,2,2,128,128]{4,3,2,1,0:T(8,128)} %all-to-all-done.2.in_ref, f32[2,128,16]{2,1,0:T(8,128)S(1)} %copy-done.4, bf16[2,256,256]{2,1,0:T(8,128)(2,1)S(1)} %copy-done.1, bf16[2,256,256]{2,1,0:T(8,128)(2,1)S(1)} %copy-done.2), custom_call_target="tpu_custom_call" | custom-call | tf_op jit(solution)/shard_map/columns/pallas_call | solution.py:696
  158.8 5.4 %all-to-all-start.3 = ((f32[8,2,2,2,128,128]{5,4,3,2,1,0:T(8,128)}), f32[8,2,2,2,128,128]{5,4,3,2,1,0:T(8,128)}, u32[]{:S(2)}, u32[]{:S(2)}) async-start(f32[8,2,2,2,128,128]{5,4,3,2,1,0:T(8,128)} %columns.1), calls=%async_computation.3 | async-start | bytes 8388608 | tf_op jit(solution)/shard_map/all_to_all | solution.py:717
  164.2 1.3 collective-permute-start.2
  165.5 26.1 %collective-permute-done.2 = f32[2,128,2048]{2,1,0:T(8,128)} collective-permute-done((f32[2,128,2048]{2,1,0:T(8,128)}, f32[2,128,2048]{2,1,0:T(8,128)}, u32[]{:S(2)}, u32[]{:S(2)}) %collective-permute-start.2) | collective-permute-done | bytes 2097184 | tf_op jit(solution)/shard_map/ppermute | solution.py:694
  191.6 3.3 %broadcast_select_fusion = f32[2,128,2048]{2,1,0:T(8,128)} fusion(f32[2,128,2048]{2,1,0:T(8,128)} %get-tuple-element.8, f32[2,128,2048]{2,1,0:T(8,128)} %collective-permute-done.2, pred[]{:T(512)S(6)} %eq.35), kind=kLoop, calls=%fused_computation.1 | loop fusion | flops 524288 | bytes 6291457 | tf_op jit(solution)/shard_map/jit(_where)/select_n | solution.py:695
  194.8 16.7 %all-to-all-done.3.in_ref = f32[8,2,2,2,128,128]{5,4,3,2,1,0:T(8,128)} async-done(((f32[8,2,2,2,128,128]{5,4,3,2,1,0:T(8,128)}), f32[8,2,2,2,128,128]{5,4,3,2,1,0:T(8,128)}, u32[]{:S(2)}, u32[]{:S(2)}) %all-to-all-start.3) | async-done | bytes 4194336 | tf_op jit(solution)/shard_map/all_to_all | solution.py:717
  211.6 6.2 %inverse_rows.1 = (f32[2,128,2048]{2,1,0:T(8,128)}, f32[2,128,2048]{2,1,0:T(8,128)}) custom-call(f32[8,2,2,2,128,128]{5,4,3,2,1,0:T(8,128)} %all-to-all-done.3.in_ref, f32[2,16,128]{2,1,0:T(8,128)S(1)} %copy-done.8, bf16[2,256,256]{2,1,0:T(8,128)(2,1)S(1)} %copy-done.1), custom_call_target="tpu_custom_call" | custom-call | tf_op jit(solution)/shard_map/inverse_rows/pallas_call | solution.py:718
  (25 shorter events, 0.2 us)
Async XLA Ops:
  0.6 1.0 copy-start.3
  1.6 0.9 copy-start.5
  2.5 13.0 %copy-start.9 = (f32[2]{0:T(128)S(1)}, f32[2]{0:T(128)}, u32[]{:S(2)}) copy-start(f32[2]{0:T(128)} %param.14) | copy-start | bytes 28
  2.5 13.0 %copy-start.10 = (f32[2]{0:T(128)S(1)}, f32[2]{0:T(128)}, u32[]{:S(2)}) copy-start(f32[2]{0:T(128)} %param.13) | copy-start | bytes 28
  2.6 13.1 %copy-start.11 = (f32[2]{0:T(128)S(1)}, f32[2]{0:T(128)}, u32[]{:S(2)}) copy-start(f32[2]{0:T(128)} %param.15) | copy-start | bytes 28
  2.6 0.7 copy-start.6
  3.3 12.3 %copy-start.7 = (s32[2,1024]{1,0:T(2,128)S(1)}, s32[2,1024]{1,0:T(2,128)}, u32[]{:S(2)}) copy-start(s32[2,1024]{1,0:T(2,128)} %table_ref.5) | copy-start | bytes 24580
  7.0 33.8 %all-to-all-start = ((f32[16,136,128]{2,1,0:T(8,128)}), f32[16,136,128]{2,1,0:T(8,128)S(1)}, u32[]{:S(2)}, u32[]{:S(2)}) async-start(f32[16,136,128]{2,1,0:T(8,128)} %pack.2), calls=%async_computation | async-start | bytes 2228224 | tf_op jit(solution)/shard_map/all_to_all | solution.py:579
  13.2 23.9 %collective-permute-start.1 = (f32[2,2,64,512]{3,2,1,0:T(8,128)S(1)}, f32[2,2,64,512]{3,2,1,0:T(8,128)S(1)}, u32[]{:S(2)}, u32[]{:S(2)}) collective-permute-start(f32[2,2,64,512]{3,2,1,0:T(8,128)S(1)} %widen.1.raw_ref), channel_id=1, source_target_pairs={{0,8},{8,0},{1,9},{9,1},{2,10},{10,2},{3,11},{11,3},{4,12},{12,4},... | collective-permute-start | bytes 1572872 | tf_op jit(solution)/shard_map/ppermute | solution.py:607
  16.0 33.2 %collective-permute-start = (f32[2,1027]{1,0:T(2,128)S(1)}, f32[2,1027]{1,0:T(2,128)S(1)}, u32[]{:S(2)}, u32[]{:S(2)}) collective-permute-start(f32[2,1027]{1,0:T(2,128)S(1)} %concatenate.19), channel_id=1, source_target_pairs={{0,16},{16,0},{1,17},{17,1},{2,18},{18,2},{3,19},{19,3},{4,20},{20... | collective-permute-start | bytes 24656 | tf_op jit(solution)/shard_map/ppermute | solution.py:627
  40.8 24.2 %all-to-all-start.1 = ((f32[16,136,128]{2,1,0:T(8,128)}), f32[16,136,128]{2,1,0:T(8,128)S(1)}, u32[]{:S(2)}, u32[]{:S(2)}) async-start(f32[16,136,128]{2,1,0:T(8,128)} %pack.3), calls=%async_computation.1 | async-start | bytes 2228224 | tf_op jit(solution)/shard_map/all_to_all | solution.py:579
  52.4 12.7 %copy-start.2 = (bf16[2,256,256]{2,1,0:T(8,128)(2,1)S(1)}, bf16[2,256,256]{2,1,0:T(8,128)(2,1)}, u32[]{:S(2)}) copy-start(bf16[2,256,256]{2,1,0:T(8,128)(2,1)} %constant.65.clone.table_ref.back_ref) | copy-start | bytes 786436
  52.4 12.7 %copy-start.8 = (f32[2,16,128]{2,1,0:T(8,128)S(1)}, f32[2,16,128]{2,1,0:T(8,128)}, u32[]{:S(2)}) copy-start(f32[2,16,128]{2,1,0:T(8,128)} %constant.63.clone.twiddle_ref) | copy-start | bytes 49156
  65.1 2.2 %copy-start = (f32[4,128,16,128]{3,2,1,0:T(8,128)S(1)}, f32[4,128,16,128]{3,2,1,0:T(8,128)}, u32[]{:S(2)}) copy-start(f32[4,128,16,128]{3,2,1,0:T(8,128)} %deposit.1.near_dens_ref) | copy-start | bytes 12582916
  81.9 61.3 %copy-start.1 = (bf16[2,256,256]{2,1,0:T(8,128)(2,1)S(1)}, bf16[2,256,256]{2,1,0:T(8,128)(2,1)}, u32[]{:S(2)}) copy-start(bf16[2,256,256]{2,1,0:T(8,128)(2,1)} %constant.66.clone.forward_ref.table_ref) | copy-start | bytes 786436
  81.9 61.3 %copy-start.4 = (f32[2,128,16]{2,1,0:T(8,128)S(1)}, f32[2,128,16]{2,1,0:T(8,128)}, u32[]{:S(2)}) copy-start(f32[2,128,16]{2,1,0:T(8,128)} %constant.64.clone.turn_ref) | copy-start | bytes 49156
  81.9 61.3 %all-to-all-start.2 = ((f32[16,2,2,128,128]{4,3,2,1,0:T(8,128)}), f32[16,2,2,128,128]{4,3,2,1,0:T(8,128)}, u32[]{:S(2)}, u32[]{:S(2)}) async-start(f32[16,2,2,128,128]{4,3,2,1,0:T(8,128)} %get-tuple-element.10), calls=%async_computation.2 | async-start | bytes 8388608 | tf_op jit(solution)/shard_map/all_to_all | solution.py:687
  158.8 52.7 %all-to-all-start.3 = ((f32[8,2,2,2,128,128]{5,4,3,2,1,0:T(8,128)}), f32[8,2,2,2,128,128]{5,4,3,2,1,0:T(8,128)}, u32[]{:S(2)}, u32[]{:S(2)}) async-start(f32[8,2,2,2,128,128]{5,4,3,2,1,0:T(8,128)} %columns.1), calls=%async_computation.3 | async-start | bytes 8388608 | tf_op jit(solution)/shard_map/all_to_all | solution.py:717
  164.2 27.4 %collective-permute-start.2 = (f32[2,128,2048]{2,1,0:T(8,128)}, f32[2,128,2048]{2,1,0:T(8,128)}, u32[]{:S(2)}, u32[]{:S(2)}) collective-permute-start(f32[2,128,2048]{2,1,0:T(8,128)} %get-tuple-element.9), channel_id=1, source_target_pairs={{0,16},{2,18},{4,20},{6,22},{9,25},{11,27},{13,29},{15,31},{17,1},... | collective-permute-start | bytes 6291464 | tf_op jit(solution)/shard_map/ppermute | solution.py:694

commit v3 on v2

--- a/solution.py
+++ b/solution.py
@@ -284,13 +284,13 @@
     out_ref[1] = mass_ref[...].astype(jnp.float32)
 
 
-def pack_kernel(half, cap, per_owner, from_ref, table_ref, raw_ref, out_ref, count_ref):
+def pack_kernel(half, cap, per_owner, which, at_ref, table_ref, raw_ref, out_ref, count_ref):
     _, planes, local_tiles, per_tile = raw_ref.shape
     groups = out_ref.shape[0]
     chunks = per_tile // TC
     lines = 2 * chunks * cap
     out_ref[...] = jnp.zeros(out_ref.shape, jnp.float32)
-    base = from_ref[0] * local_tiles
+    base = at_ref[which] * local_tiles
     for plane in range(planes):
 
         @pl.loop(0, groups)
@@ -382,7 +382,7 @@
 
 
 def rows_kernel(
-    cap, chunks, weight_ref, side_ref, slots_ref, near_dens_ref, near_ref, far_ref, twiddle_ref, table_ref,
+    cap, chunks, weight_ref, at_ref, slots_ref, near_dens_ref, near_ref, far_ref, twiddle_ref, table_ref,
     mine_ref, other_ref, out_ref, high_ref, low_ref, far_dens_ref,
 ):
     step = pl.program_id(0)
@@ -439,7 +439,7 @@
                     high_ref[spot, at * TC : (at + 1) * TC] = high
                     low_ref[spot, at * TC : (at + 1) * TC] = low
 
-        base = side_ref[side] * half
+        base = at_ref[2 + side] * half
         done = dot3((high_ref[...], low_ref[...]), table)
         for place in range(outer):
             here = slice(place * slab, (place + 1) * slab)
@@ -458,7 +458,7 @@
 
 
 def columns_kernel(
-    order, me_ref, in_ref, turn_ref, forward_ref, back_ref, out_ref, high_ref, low_ref, spectrum_ref, back_f
+    order, at_ref, in_ref, turn_ref, forward_ref, back_ref, out_ref, high_ref, low_ref, spectrum_ref, back_f
 ):
     outer, _, _, inner, lanes = in_ref.shape
     length = outer * inner
@@ -481,11 +481,11 @@
         spectrum_ref[:, span] = dot3(forward, (high_ref[:, span], low_ref[:, span]))
 
     middle = length // 2
-    wave_v = lax.broadcasted_iota(jnp.int32, (inner, lanes), 1) * outer + (2 * me_ref[0] + pl.program_id(0))
+    wave_v = lax.broadcasted_iota(jnp.int32, (inner, lanes), 1) * outer + (2 * at_ref[4] + pl.program_id(0))
     keep_v = wave_v != middle
     sv = jnp.where(wave_v >= middle, wave_v - length, wave_v).astype(jnp.float32)
     line_u = lax.broadcasted_iota(jnp.int32, (inner, lanes), 0) * outer
-    flip = jnp.where(me_ref[1] > 0, -1.0, 1.0)
+    flip = jnp.where(at_ref[5] > 0, -1.0, 1.0)
     for place in range(outer):
         side = slice(place * lanes, (place + 1) * lanes)
         wave_u = line_u + place
@@ -606,19 +606,21 @@
     )(cell_index, masses)
     raw_far = lax.ppermute(raw, "upper", [(0, 1), (1, 0)])
 
-    def pack(source, lists):
+    here = jnp.stack([upper * half + low, (1 - upper) * half + low, shell, 1 - shell, low, upper]).astype(jnp.int32)
+
+    def pack(which, lists):
         return pl.pallas_call(
-            partial(pack_kernel, half, cap, per_owner),
+            partial(pack_kernel, half, cap, per_owner, which),
             in_specs=[SMEM, SMEM, VMEM],
             out_specs=VMEM,
             out_shape=jax.ShapeDtypeStruct((groups, lines + 8, TC), jnp.float32),
             scratch_shapes=[pltpu.SMEM((groups,), jnp.int32)],
             compiler_params=room(12),
             name="pack",
-        )(source.reshape(1).astype(jnp.int32), block_tile, lists)
-
-    near = cube_exchange(pack(upper * half + low, raw))
-    far = cube_exchange(pack((1 - upper) * half + low, raw_far))
+        )(here, block_tile, lists)
+
+    near = cube_exchange(pack(0, raw))
+    far = cube_exchange(pack(1, raw_far))
 
     note = jnp.concatenate(
         [block_tile.astype(jnp.float32), plane_coef[:, None], (plane_coef * plane_dist)[:, None], source_inv[:, None]],
@@ -683,7 +685,7 @@
         ],
         compiler_params=room(28),
         name="rows",
-    )(weight, jnp.stack([shell, 1 - shell]).astype(jnp.int32), far_slots, near_dens, near, far, twiddle, minus)
+    )(weight, here, far_slots, near_dens, near, far, twiddle, minus)
     arrived = lax.all_to_all(row_sent, ("shell", "low"), split_axis=0, concat_axis=0, tiled=True)
     swaps = []
     for side in range(2):
@@ -713,7 +715,7 @@
         ],
         compiler_params=room(32),
         name="columns",
-    )(jnp.stack([low, upper]).astype(jnp.int32), arrived, turn, plus, minus)
+    )(here, arrived, turn, plus, minus)
     landed = lax.all_to_all(col_sent, "low", split_axis=0, concat_axis=0, tiled=True)
     shear_one, shear_two = pl.pallas_call(
         inverse_rows_kernel,

time: 219 us -> 211 us (0.963)
  waiting for transfers between devices: 122 us -> 66 us
  blocking collectives: 0 us -> 53.3 us
  starting transfers between devices: 30.1 us -> 25.1 us
    all_to_all x1 -> x0, waiting for transfers between devices: 55.9 us -> none  [local_cube(): lax.all_to_all(row_sent, ('shell', 'low'), split_axis=0, concat_axis=0, t...]
    all_to_all x0 -> x1, blocking collectives: none -> 53.3 us  [local_cube(): lax.all_to_all(row_sent, ('shell', 'low'), split_axis=0, concat_axis=0, t...]
    all_to_all x1 -> x0, starting transfers between devices: 5.33 us -> none  [local_cube(): lax.all_to_all(row_sent, ('shell', 'low'), split_axis=0, concat_axis=0, t...]
  transfers between devices with their start and end apart: 7 -> 6, of which waited for: 5 -> 4; matrix products, arithmetic and copies ran while one was open for 3% -> 3% of each run, Pallas kernels for 6% -> 6%
where the time goes in v3:
time: 211 us; the launch traced here: 209 us
  waiting for transfers between devices  66 us (31%)
  blocking collectives  53.3 us (25%)
  Pallas kernels  52.5 us (25%)
  starting transfers between devices  25.1 us (12%)
  local copies, waits for them, and re-layouts  5.97 us (3%)
  other arithmetic  5.72 us (3%)
    all_to_all x1, blocking collectives, local_cube(): lax.all_to_all(row_sent, ('shell', 'low'), split_axis=0, concat_axis=0, t...  53.3 us
    ppermute x1, waiting for transfers between devices, local_cube(): conv_held = lax.ppermute(conv_other, ('shell', 'upper', 'low'), swaps)  26.1 us
    ppermute x1, waiting for transfers between devices, local_cube(): raw_far = lax.ppermute(raw, 'upper', [(0, 1), (1, 0)])  19.8 us
    all_to_all x1, waiting for transfers between devices, local_cube(): lax.all_to_all(col_sent, 'low', split_axis=0, concat_axis=0, tiled=True)  16.7 us
    pallas_call x1, Pallas kernels, local_cube(): pl.pallas_call(partial(rows_kernel, cap, chunks), grid=(slab // some,), i...  14.8 us
    pallas_call x1, Pallas kernels, local_cube(): pl.pallas_call(partial(columns_kernel, order), grid=(2,), in_specs=[SMEM,...  14.6 us
    all_to_all x2, starting transfers between devices, cube_exchange(): lax.all_to_all(value, ('shell', 'low'), split_axis=0, concat_axis=0, tile...  14.5 us
    pallas_call x1, Pallas kernels, local_cube(): pl.pallas_call(partial(deposit_kernel, cap, chunks), in_specs=[SMEM, VMEM...  9.37 us
  transfers between devices with their start and end apart: 6, of which 4 were waited for; matrix products, arithmetic and copies ran while one was open for 3% of the time, Pallas kernels for 6%

profile of v3, /device:TPU:1, one launch (start us, length us, event | category | flops | bytes accessed | tf_op | source)
XLA Modules:
  0.0 209.4 jit_solution(6506031021313508145)
XLA Ops:
  0.6 0.0 copy-start.3
  0.7 0.9 copy-done.3
  1.6 0.9 copy-done.5
  2.5 0.0 copy-start.7
  2.5 0.0 copy-start.9
  2.6 0.0 copy-start.10
  2.6 0.0 copy-start.11
  2.6 0.1 stack.27.at_ref
  2.7 0.7 copy-done.6
  3.4 3.7 %pack.2 = f32[16,136,128]{2,1,0:T(8,128)} custom-call(s32[6]{0:T(128)S(1)} %stack.27.at_ref, s32[2,1024]{1,0:T(2,128)S(1)} %copy-done.6, f32[2,2,64,512]{3,2,1,0:T(8,128)S(1)} %widen.1.raw_ref), custom_call_target="tpu_custom_call" | custom-call | tf_op jit(solution)/shard_map/pack/pallas_call | solution.py:612
  7.1 6.2 %all-to-all-start = ((f32[16,136,128]{2,1,0:T(8,128)}), f32[16,136,128]{2,1,0:T(8,128)S(1)}, u32[]{:S(2)}, u32[]{:S(2)}) async-start(f32[16,136,128]{2,1,0:T(8,128)} %pack.2), calls=%async_computation | async-start | bytes 2228224 | tf_op jit(solution)/shard_map/all_to_all | solution.py:579
  13.3 2.3 %collective-permute-start.1 = (f32[2,2,64,512]{3,2,1,0:T(8,128)S(1)}, f32[2,2,64,512]{3,2,1,0:T(8,128)S(1)}, u32[]{:S(2)}, u32[]{:S(2)}) collective-permute-start(f32[2,2,64,512]{3,2,1,0:T(8,128)S(1)} %widen.1.raw_ref), channel_id=1, source_target_pairs={{0,8},{8,0},{1,9},{9,1},{2,10},{10,2},{3,11},{11,3},{4,12},{12,4},... | collective-permute-start | bytes 1572872 | tf_op jit(solution)/shard_map/ppermute | solution.py:607
  15.6 0.0 copy-done.7
  15.6 0.0 copy-done.9
  15.7 0.1 copy.22
  15.8 0.1 copy.23
  15.9 0.1 copy.21
  16.0 0.1 concatenate.19
  16.0 1.4 collective-permute-start
  17.4 19.8 %collective-permute-done.1.raw_ref = f32[2,2,64,512]{3,2,1,0:T(8,128)S(1)} collective-permute-done((f32[2,2,64,512]{3,2,1,0:T(8,128)S(1)}, f32[2,2,64,512]{3,2,1,0:T(8,128)S(1)}, u32[]{:S(2)}, u32[]{:S(2)}) %collective-permute-start.1) | collective-permute-done | bytes 524320 | tf_op jit(solution)/shard_map/ppermute | solution.py:607
  37.2 3.7 %pack.3 = f32[16,136,128]{2,1,0:T(8,128)} custom-call(s32[6]{0:T(128)S(1)} %stack.27.at_ref, s32[2,1024]{1,0:T(2,128)S(1)} %copy-done.7, f32[2,2,64,512]{3,2,1,0:T(8,128)S(1)} %collective-permute-done.1.raw_ref), custom_call_target="tpu_custom_call" | custom-call | tf_op jit(solution)/shard_map/pack/pallas_call | solution.py:612
  40.9 0.0 all-to-all-done.recv_ref.near_ref
  40.9 8.2 %all-to-all-start.1 = ((f32[16,136,128]{2,1,0:T(8,128)}), f32[16,136,128]{2,1,0:T(8,128)S(1)}, u32[]{:S(2)}, u32[]{:S(2)}) async-start(f32[16,136,128]{2,1,0:T(8,128)} %pack.3), calls=%async_computation.1 | async-start | bytes 2228224 | tf_op jit(solution)/shard_map/all_to_all | solution.py:579
  49.1 0.1 pad_add_fusion
  49.2 0.0 collective-permute-done
  49.2 0.2 slice_reduce_fusion.2
  49.4 0.1 pad_maximum_fusion.1
  49.5 0.2 slice_reduce_fusion.1
  49.7 0.2 subtract_select_fusion
  49.9 0.1 copy.24
  50.0 0.1 reshape.100
  50.1 0.8 select_reduce_fusion
  50.9 1.2 select_reduce_fusion.1
  52.1 0.1 reshape.103.slots_ref
  52.2 0.1 reshape.102.slots_ref
  52.3 0.1 pad_maximum_fusion.weight_ref
  52.4 9.4 %deposit.1.near_dens_ref = f32[4,128,16,128]{3,2,1,0:T(8,128)} custom-call(s32[256]{0:T(256)S(1)} %reshape.103.slots_ref, f32[16,136,128]{2,1,0:T(8,128)S(1)} %all-to-all-done.recv_ref.near_ref), custom_call_target="tpu_custom_call" | custom-call | tf_op jit(solution)/shard_map/deposit/pallas_call | solution.py:644
  61.7 3.4 %all-to-all-done.1.far_ref = f32[16,136,128]{2,1,0:T(8,128)S(1)} async-done(((f32[16,136,128]{2,1,0:T(8,128)}), f32[16,136,128]{2,1,0:T(8,128)S(1)}, u32[]{:S(2)}, u32[]{:S(2)}) %all-to-all-start.1) | async-done | bytes 1114144 | tf_op jit(solution)/shard_map/all_to_all | solution.py:579
  65.2 2.2 %copy-done = f32[4,128,16,128]{3,2,1,0:T(8,128)S(1)} copy-done((f32[4,128,16,128]{3,2,1,0:T(8,128)S(1)}, f32[4,128,16,128]{3,2,1,0:T(8,128)}, u32[]{:S(2)}) %copy-start) | copy-done | bytes 4194328
  67.3 14.8 %rows.1 = (f32[2,128,2048]{2,1,0:T(8,128)}, f32[2,128,2048]{2,1,0:T(8,128)}, f32[16,2,2,128,128]{4,3,2,1,0:T(8,128)}) custom-call(f32[4,5]{1,0:T(4,128)S(1)} %pad_maximum_fusion.weight_ref, s32[6]{0:T(128)S(1)} %stack.27.at_ref, s32[256]{0:T(256)S(1)} %reshape.102.slots_ref, f32[4,128,16,128]{3,2,1,0:T(8,128)S(1)} %copy-done, ...), custom_call_target="tpu_custom_call" | custom-call | tf_op jit(solution)/shard_map/rows/pallas_call | solution.py:658
  82.1 53.3 %all_to_all.20.in_ref = f32[16,2,2,128,128]{4,3,2,1,0:T(8,128)S(1)} all-to-all(f32[16,2,2,128,128]{4,3,2,1,0:T(8,128)} %get-tuple-element.10), channel_id=1, replica_groups=mesh['shell'=2,'upper'=2,'low'=8] {'shell','low'}, dimensions={0} | all-to-all | bytes 8388608 | tf_op jit(solution)/shard_map/all_to_all | solution.py:689
  135.5 14.6 %columns.1 = f32[8,2,2,2,128,128]{5,4,3,2,1,0:T(8,128)} custom-call(s32[6]{0:T(128)S(1)} %stack.27.at_ref, f32[16,2,2,128,128]{4,3,2,1,0:T(8,128)S(1)} %all_to_all.20.in_ref, f32[2,128,16]{2,1,0:T(8,128)S(1)} %copy-done.4, bf16[2,256,256]{2,1,0:T(8,128)(2,1)S(1)} %copy-done.1, bf16[2,256,256]{2,1,0:T(8,128)(2,1)S(1)} %copy-done.2), custom_call_target="tpu_custom_call" | custom-call | tf_op jit(solution)/shard_map/columns/pallas_call | solution.py:698
  150.1 5.7 %all-to-all-start.3 = ((f32[8,2,2,2,128,128]{5,4,3,2,1,0:T(8,128)}), f32[8,2,2,2,128,128]{5,4,3,2,1,0:T(8,128)}, u32[]{:S(2)}, u32[]{:S(2)}) async-start(f32[8,2,2,2,128,128]{5,4,3,2,1,0:T(8,128)} %columns.1), calls=%async_computation.3 | async-start | bytes 8388608 | tf_op jit(solution)/shard_map/all_to_all | solution.py:719
  155.8 1.3 collective-permute-start.2
  157.1 26.1 %collective-permute-done.2 = f32[2,128,2048]{2,1,0:T(8,128)} collective-permute-done((f32[2,128,2048]{2,1,0:T(8,128)}, f32[2,128,2048]{2,1,0:T(8,128)}, u32[]{:S(2)}, u32[]{:S(2)}) %collective-permute-start.2) | collective-permute-done | bytes 2097184 | tf_op jit(solution)/shard_map/ppermute | solution.py:696
  183.1 3.3 %broadcast_select_fusion = f32[2,128,2048]{2,1,0:T(8,128)} fusion(f32[2,128,2048]{2,1,0:T(8,128)} %get-tuple-element.8, f32[2,128,2048]{2,1,0:T(8,128)} %collective-permute-done.2, pred[]{:T(512)S(6)} %eq.35), kind=kLoop, calls=%fused_computation.1 | loop fusion | flops 524288 | bytes 6291457 | tf_op jit(solution)/shard_map/jit(_where)/select_n | solution.py:697
  186.4 16.7 %all-to-all-done.3.in_ref = f32[8,2,2,2,128,128]{5,4,3,2,1,0:T(8,128)} async-done(((f32[8,2,2,2,128,128]{5,4,3,2,1,0:T(8,128)}), f32[8,2,2,2,128,128]{5,4,3,2,1,0:T(8,128)}, u32[]{:S(2)}, u32[]{:S(2)}) %all-to-all-start.3) | async-done | bytes 4194336 | tf_op jit(solution)/shard_map/all_to_all | solution.py:719
  203.1 6.3 %inverse_rows.1 = (f32[2,128,2048]{2,1,0:T(8,128)}, f32[2,128,2048]{2,1,0:T(8,128)}) custom-call(f32[8,2,2,2,128,128]{5,4,3,2,1,0:T(8,128)} %all-to-all-done.3.in_ref, f32[2,16,128]{2,1,0:T(8,128)S(1)} %copy-done.8, bf16[2,256,256]{2,1,0:T(8,128)(2,1)S(1)} %copy-done.1), custom_call_target="tpu_custom_call" | custom-call | tf_op jit(solution)/shard_map/inverse_rows/pallas_call | solution.py:720
  (23 shorter events, 0.2 us)
Async XLA Ops:
  0.6 1.0 copy-start.3
  1.6 0.9 copy-start.5
  2.5 13.1 %copy-start.7 = (s32[2,1024]{1,0:T(2,128)S(1)}, s32[2,1024]{1,0:T(2,128)}, u32[]{:S(2)}) copy-start(s32[2,1024]{1,0:T(2,128)} %table_ref.5) | copy-start | bytes 24580
  2.5 13.1 %copy-start.9 = (f32[2]{0:T(128)S(1)}, f32[2]{0:T(128)}, u32[]{:S(2)}) copy-start(f32[2]{0:T(128)} %param.14) | copy-start | bytes 28
  2.6 13.1 %copy-start.10 = (f32[2]{0:T(128)S(1)}, f32[2]{0:T(128)}, u32[]{:S(2)}) copy-start(f32[2]{0:T(128)} %param.13) | copy-start | bytes 28
  2.6 13.2 %copy-start.11 = (f32[2]{0:T(128)S(1)}, f32[2]{0:T(128)}, u32[]{:S(2)}) copy-start(f32[2]{0:T(128)} %param.15) | copy-start | bytes 28
  2.7 0.7 copy-start.6
  7.1 33.8 %all-to-all-start = ((f32[16,136,128]{2,1,0:T(8,128)}), f32[16,136,128]{2,1,0:T(8,128)S(1)}, u32[]{:S(2)}, u32[]{:S(2)}) async-start(f32[16,136,128]{2,1,0:T(8,128)} %pack.2), calls=%async_computation | async-start | bytes 2228224 | tf_op jit(solution)/shard_map/all_to_all | solution.py:579
  13.3 23.9 %collective-permute-start.1 = (f32[2,2,64,512]{3,2,1,0:T(8,128)S(1)}, f32[2,2,64,512]{3,2,1,0:T(8,128)S(1)}, u32[]{:S(2)}, u32[]{:S(2)}) collective-permute-start(f32[2,2,64,512]{3,2,1,0:T(8,128)S(1)} %widen.1.raw_ref), channel_id=1, source_target_pairs={{0,8},{8,0},{1,9},{9,1},{2,10},{10,2},{3,11},{11,3},{4,12},{12,4},... | collective-permute-start | bytes 1572872 | tf_op jit(solution)/shard_map/ppermute | solution.py:607
  16.0 33.2 %collective-permute-start = (f32[2,1027]{1,0:T(2,128)S(1)}, f32[2,1027]{1,0:T(2,128)S(1)}, u32[]{:S(2)}, u32[]{:S(2)}) collective-permute-start(f32[2,1027]{1,0:T(2,128)S(1)} %concatenate.19), channel_id=1, source_target_pairs={{0,16},{16,0},{1,17},{17,1},{2,18},{18,2},{3,19},{19,3},{4,20},{20... | collective-permute-start | bytes 24656 | tf_op jit(solution)/shard_map/ppermute | solution.py:629
  40.9 24.2 %all-to-all-start.1 = ((f32[16,136,128]{2,1,0:T(8,128)}), f32[16,136,128]{2,1,0:T(8,128)S(1)}, u32[]{:S(2)}, u32[]{:S(2)}) async-start(f32[16,136,128]{2,1,0:T(8,128)} %pack.3), calls=%async_computation.1 | async-start | bytes 2228224 | tf_op jit(solution)/shard_map/all_to_all | solution.py:579
  52.4 12.8 %copy-start.2 = (bf16[2,256,256]{2,1,0:T(8,128)(2,1)S(1)}, bf16[2,256,256]{2,1,0:T(8,128)(2,1)}, u32[]{:S(2)}) copy-start(bf16[2,256,256]{2,1,0:T(8,128)(2,1)} %constant.65.clone.table_ref.back_ref) | copy-start | bytes 786436
  52.4 12.8 %copy-start.8 = (f32[2,16,128]{2,1,0:T(8,128)S(1)}, f32[2,16,128]{2,1,0:T(8,128)}, u32[]{:S(2)}) copy-start(f32[2,16,128]{2,1,0:T(8,128)} %constant.63.clone.twiddle_ref) | copy-start | bytes 49156
  65.2 2.2 %copy-start = (f32[4,128,16,128]{3,2,1,0:T(8,128)S(1)}, f32[4,128,16,128]{3,2,1,0:T(8,128)}, u32[]{:S(2)}) copy-start(f32[4,128,16,128]{3,2,1,0:T(8,128)} %deposit.1.near_dens_ref) | copy-start | bytes 12582916
  82.1 53.3 %copy-start.1 = (bf16[2,256,256]{2,1,0:T(8,128)(2,1)S(1)}, bf16[2,256,256]{2,1,0:T(8,128)(2,1)}, u32[]{:S(2)}) copy-start(bf16[2,256,256]{2,1,0:T(8,128)(2,1)} %constant.66.clone.forward_ref.table_ref) | copy-start | bytes 786436
  82.1 53.3 %copy-start.4 = (f32[2,128,16]{2,1,0:T(8,128)S(1)}, f32[2,128,16]{2,1,0:T(8,128)}, u32[]{:S(2)}) copy-start(f32[2,128,16]{2,1,0:T(8,128)} %constant.64.clone.turn_ref) | copy-start | bytes 49156
  150.1 53.0 %all-to-all-start.3 = ((f32[8,2,2,2,128,128]{5,4,3,2,1,0:T(8,128)}), f32[8,2,2,2,128,128]{5,4,3,2,1,0:T(8,128)}, u32[]{:S(2)}, u32[]{:S(2)}) async-start(f32[8,2,2,2,128,128]{5,4,3,2,1,0:T(8,128)} %columns.1), calls=%async_computation.3 | async-start | bytes 8388608 | tf_op jit(solution)/shard_map/all_to_all | solution.py:719
  155.8 27.4 %collective-permute-start.2 = (f32[2,128,2048]{2,1,0:T(8,128)}, f32[2,128,2048]{2,1,0:T(8,128)}, u32[]{:S(2)}, u32[]{:S(2)}) collective-permute-start(f32[2,128,2048]{2,1,0:T(8,128)} %get-tuple-element.9), channel_id=1, source_target_pairs={{0,16},{2,18},{4,20},{6,22},{9,25},{11,27},{13,29},{15,31},{17,1},... | collective-permute-start | bytes 6291464 | tf_op jit(solution)/shard_map/ppermute | solution.py:696

commit v4 on v3

--- a/solution.py
+++ b/solution.py
@@ -284,35 +284,39 @@
     out_ref[1] = mass_ref[...].astype(jnp.float32)
 
 
-def pack_kernel(half, cap, per_owner, which, at_ref, table_ref, raw_ref, out_ref, count_ref):
+def divided(value, count):
+    return value >> (count.bit_length() - 1) if count & (count - 1) == 0 else lax.div(value, count)
+
+
+def pack_kernel(half, cap, per_owner, which, at_ref, table_ref, raw_ref, out_ref, *count_refs):
     _, planes, local_tiles, per_tile = raw_ref.shape
     groups = out_ref.shape[0]
     chunks = per_tile // TC
     lines = 2 * chunks * cap
     out_ref[...] = jnp.zeros(out_ref.shape, jnp.float32)
     base = at_ref[which] * local_tiles
-    for plane in range(planes):
-
-        @pl.loop(0, groups)
-        def _(slot):
-            count_ref[slot] = 0
-
-        @pl.loop(0, local_tiles // 8)
-        def _(bunch):
-            here = pl.ds(pl.multiple_of(bunch * 8, 8), 8)
-            lists = [raw_ref[kind, plane, here, :] for kind in range(2)]
-            for at in range(8):
-                owner = lax.div(table_ref[plane, base + bunch * 8 + at], per_owner)
-                low = lax.rem(owner, half)
-                side = lax.rem(lax.div(owner, half) + lax.rem(low, 2), 2)
-                place = side * half + low
+    for place in range(groups):
+        for count_ref in count_refs:
+            count_ref[place] = 0
+
+    @pl.loop(0, local_tiles // 8)
+    def _(bunch):
+        here = pl.ds(pl.multiple_of(bunch * 8, 8), 8)
+        lists = [[raw_ref[kind, plane, here, :] for kind in range(2)] for plane in range(planes)]
+        for at in range(8):
+            for plane, count_ref in enumerate(count_refs):
+                owner = divided(table_ref[plane, base + bunch * 8 + at], per_owner)
+                upper = divided(owner, half)
+                low = owner - upper * half
+                place = ((upper + low) & 1) * half + low
                 rank = count_ref[place]
                 count_ref[place] = rank + 1
-                for kind, values in enumerate(lists):
+                for kind, values in enumerate(lists[plane]):
                     for chunk in range(chunks):
                         row = plane * lines + kind * chunks * cap + chunk * cap + rank
                         out_ref[place, pl.ds(row, 1), :] = values[at : at + 1, chunk * TC : (chunk + 1) * TC]
 
+    for plane in range(planes):
         total = jnp.sum(raw_ref[1, plane], axis=0, keepdims=True)
         total = jnp.sum(total, axis=1, keepdims=True)
         line = jnp.broadcast_to(total, (1, TC))
@@ -339,7 +343,7 @@
     for plane in range(all_planes):
         start = (plane % planes) * 2 * chunks * cap
 
-        @pl.loop(0, half, unroll=4)
+        @pl.loop(0, half, unroll=True)
         def _(source):
             place = (plane // planes) * half + source
             cells = [recv_ref[place, start + k * cap : start + (k + 1) * cap, :] for k in range(chunks)]
@@ -383,13 +387,20 @@
 
 def rows_kernel(
     cap, chunks, weight_ref, at_ref, slots_ref, near_dens_ref, near_ref, far_ref, twiddle_ref, table_ref,
-    mine_ref, other_ref, out_ref, high_ref, low_ref, far_dens_ref,
+    mine_ref, other_ref, out_ref, high_ref, low_ref, far_dens_ref, dens_ref, maps_ref, copied,
 ):
     step = pl.program_id(0)
-    pl.when(step == 0)(lambda: deposit_kernel(cap, chunks, slots_ref, far_ref, far_dens_ref))
-    first_line = 2 * (far_dens_ref.shape[0] // 2) * cap * chunks
+
+    @pl.when(step == 0)
+    def _():
+        fetch = pltpu.make_async_copy(near_dens_ref, dens_ref, copied)
+        fetch.start()
+        deposit_kernel(cap, chunks, slots_ref, far_ref, far_dens_ref)
+        fetch.wait()
+
     planes, slab, length = mine_ref.shape
     all_planes = far_dens_ref.shape[0]
+    first_line = planes * 2 * cap * chunks
     outer = length // TC
     first_tile = step * (slab // TR * outer)
     half = near_ref.shape[0] // 2
@@ -402,29 +413,32 @@
             total = total + near_ref[place, line : line + 1, :]
             total = total + far_ref[place, first_line + line : first_line + line + 1, :]
         scales.append(float(length * length) / total)
+    factors = [
+        [jnp.broadcast_to(weight_ref[i, j] * scales[j], (TR, TC)) for j in range(i + 1)] for i in range(all_planes)
+    ]
+    shift = [weight_ref[i, all_planes] for i in range(all_planes)]
+    first_shell = at_ref[2] == 0
+    for line in range(slab // TR):
+        here = slice(line * TR, (line + 1) * TR)
+        for col in range(outer):
+            at = line * outer + col
+            tiles = [dens_ref[j, first_tile + at] + far_dens_ref[j, first_tile + at] for j in range(all_planes)]
+            maps = []
+            for i in range(all_planes):
+                field = tiles[0] * factors[i][0]
+                for j in range(1, i + 1):
+                    field = field + tiles[j] * factors[i][j]
+                maps.append(field - shift[i])
+                maps_ref[i, at] = maps[i]
+            side = slice(col * TC, (col + 1) * TC)
+            for i in range(planes):
+                mine_ref[i, here, side] = jnp.where(first_shell, maps[i], maps[planes + i])
+                other_ref[i, here, side] = jnp.where(first_shell, maps[planes + i], maps[i])
+
     table = (table_ref[0], table_ref[1])
-    for side, conv_ref in enumerate((mine_ref, other_ref)):
-        here_maps = [side * planes + i for i in range(planes)]
-        factors = [
-            [jnp.broadcast_to(weight_ref[i, j] * scales[j], (TR, TC)) for j in range(all_planes)] for i in here_maps
-        ]
-        shift = [weight_ref[i, all_planes] for i in here_maps]
-
+    for pair in range(all_planes // 2):
         for line in range(slab // TR):
-            values = []
-            here = slice(line * TR, (line + 1) * TR)
-            for col in range(outer):
-                at = line * outer + col
-                tiles = [near_dens_ref[j, at] + far_dens_ref[j, first_tile + at] for j in range(all_planes)]
-                pair = []
-                for i in range(planes):
-                    field = tiles[0] * factors[i][0]
-                    for tile, factor in zip(tiles[1:], factors[i][1:]):
-                        field = field + tile * factor
-                    field = field - shift[i]
-                    conv_ref[i, here, col * TC : (col + 1) * TC] = field
-                    pair.append(field)
-                values.append(tuple(pair))
+            values = [tuple(maps_ref[2 * pair + i, line * outer + col] for i in range(2)) for col in range(outer)]
             for place, (real_part, imag_part) in enumerate(sixteen(values, -1.0)):
                 if place:
                     cosine = twiddle_ref[0, place : place + 1, :]
@@ -436,15 +450,14 @@
                 spot = slice(place * slab + line * TR, place * slab + (line + 1) * TR)
                 for at, value in enumerate((real_part, imag_part)):
                     high, low = bf16_pair(value)
-                    high_ref[spot, at * TC : (at + 1) * TC] = high
-                    low_ref[spot, at * TC : (at + 1) * TC] = low
-
-        base = at_ref[2 + side] * half
-        done = dot3((high_ref[...], low_ref[...]), table)
+                    high_ref[pair, spot, at * TC : (at + 1) * TC] = high
+                    low_ref[pair, spot, at * TC : (at + 1) * TC] = low
+
+        done = dot3((high_ref[pair], low_ref[pair]), table)
         for place in range(outer):
             here = slice(place * slab, (place + 1) * slab)
-            out_ref[base + place // 2, place % 2, 0] = done[here, :TC]
-            out_ref[base + place // 2, place % 2, 1] = done[here, TC:]
+            out_ref[pair * half + place // 2, place % 2, 0] = done[here, :TC]
+            out_ref[pair * half + place // 2, place % 2, 1] = done[here, TC:]
 
 
 def turned(turn_ref, place, here, value, sign_value):
@@ -457,15 +470,35 @@
     return (real_part * cosine - imag_part * sine, real_part * sine + imag_part * cosine)
 
 
+def filters_kernel(length, at_ref, out_ref):
+    _, _, outer, inner, lanes = out_ref.shape
+    middle = length // 2
+    wave_v = lax.broadcasted_iota(jnp.int32, (inner, lanes), 1) * outer + (2 * at_ref[4] + pl.program_id(0))
+    keep_v = wave_v != middle
+    sv = jnp.where(wave_v >= middle, wave_v - length, wave_v).astype(jnp.float32)
+    line_u = lax.broadcasted_iota(jnp.int32, (inner, lanes), 0) * outer
+    flip = jnp.where(at_ref[5] > 0, -1.0, 1.0)
+    for place in range(outer):
+        wave_u = line_u + place
+        su = jnp.where(wave_u >= middle, wave_u - length, wave_u).astype(jnp.float32)
+        scale = 1.0 / (float(length) * float(length))
+        keep = jnp.where(keep_v & (wave_u != middle), scale * flip if place % 2 else scale, 0.0)
+        factor = keep / jnp.maximum(sv * sv + su * su, 1.0)
+        out_ref[0, 0, place] = factor * (sv * sv - su * su)
+        out_ref[0, 1, place] = factor * (2.0 * sv * su)
+
+
 def columns_kernel(
-    order, at_ref, in_ref, turn_ref, forward_ref, back_ref, out_ref, high_ref, low_ref, spectrum_ref, back_f
+    order, filters_ref, in_ref, turn_ref, forward_ref, back_ref, out_ref,
+    high_ref, low_ref, spectrum_ref, back_f, filter_ref, copied,
 ):
+    fetch = pltpu.make_async_copy(filters_ref.at[pl.program_id(0)], filter_ref, copied)
+    fetch.start()
     outer, _, _, inner, lanes = in_ref.shape
-    length = outer * inner
     forward = (forward_ref[0], forward_ref[1])
     back = (back_ref[0], back_ref[1])
 
-    @pl.loop(0, inner // TR)
+    @pl.loop(0, inner // TR, unroll=True)
     def _(line):
         here = pl.ds(line * TR, TR)
         there = pl.ds(inner + line * TR, TR)
@@ -480,21 +513,11 @@
         span = slice(bunch * 2 * lanes, (bunch + 1) * 2 * lanes)
         spectrum_ref[:, span] = dot3(forward, (high_ref[:, span], low_ref[:, span]))
 
-    middle = length // 2
-    wave_v = lax.broadcasted_iota(jnp.int32, (inner, lanes), 1) * outer + (2 * at_ref[4] + pl.program_id(0))
-    keep_v = wave_v != middle
-    sv = jnp.where(wave_v >= middle, wave_v - length, wave_v).astype(jnp.float32)
-    line_u = lax.broadcasted_iota(jnp.int32, (inner, lanes), 0) * outer
-    flip = jnp.where(at_ref[5] > 0, -1.0, 1.0)
+    fetch.wait()
     for place in range(outer):
         side = slice(place * lanes, (place + 1) * lanes)
-        wave_u = line_u + place
-        su = jnp.where(wave_u >= middle, wave_u - length, wave_u).astype(jnp.float32)
-        scale = 1.0 / (float(length) * float(length))
-        keep = jnp.where(keep_v & (wave_u != middle), scale * flip if place % 2 else scale, 0.0)
-        factor = keep / jnp.maximum(sv * sv + su * su, 1.0)
-        first = factor * (sv * sv - su * su)
-        second = factor * (2.0 * sv * su)
+        first = filter_ref[0, place]
+        second = filter_ref[1, place]
         real_part = spectrum_ref[:inner, side]
         imag_part = spectrum_ref[inner:, side]
         stacked = jnp.concatenate(
@@ -508,7 +531,7 @@
 
     half = outer // 2
 
-    @pl.loop(0, inner // TR)
+    @pl.loop(0, inner // TR, unroll=True)
     def _(line):
         here = pl.ds(line * TR, TR)
         there = pl.ds(inner + line * TR, TR)
@@ -561,6 +584,10 @@
     return pltpu.CompilerParams(vmem_limit_bytes=mib * 1024 * 1024)
 
 
+def in_hbm(value):
+    return pltpu.with_memory_space_constraint(value, pltpu.HBM)
+
+
 def whole(shape):
     return pl.BlockSpec(shape, lambda step: (0,) * len(shape))
 
@@ -603,7 +630,7 @@
         out_shape=jax.ShapeDtypeStruct((2, planes, local_tiles, per_tile), jnp.float32),
         compiler_params=room(8),
         name="widen",
-    )(cell_index, masses)
+    )(in_hbm(cell_index), in_hbm(masses))
     raw_far = lax.ppermute(raw, "upper", [(0, 1), (1, 0)])
 
     here = jnp.stack([upper * half + low, (1 - upper) * half + low, shell, 1 - shell, low, upper]).astype(jnp.int32)
@@ -614,7 +641,7 @@
             in_specs=[SMEM, SMEM, VMEM],
             out_specs=VMEM,
             out_shape=jax.ShapeDtypeStruct((groups, lines + 8, TC), jnp.float32),
-            scratch_shapes=[pltpu.SMEM((groups,), jnp.int32)],
+            scratch_shapes=[pltpu.SMEM((groups,), jnp.int32)] * planes,
             compiler_params=room(12),
             name="pack",
         )(here, block_tile, lists)
@@ -634,13 +661,21 @@
     tiles = tiles.reshape(2 * planes, 2, half, cap)
     near_slots = lax.dynamic_index_in_dim(tiles, upper, axis=1, keepdims=False).reshape(-1)
     far_slots = lax.dynamic_index_in_dim(tiles, 1 - upper, axis=1, keepdims=False).reshape(-1)
-    maps = jnp.concatenate([shell * planes + jnp.arange(planes), (1 - shell) * planes + jnp.arange(planes)])
-    inverse = jnp.concatenate([note[:, -1], other[:, -1]])
+    maps = jnp.arange(2 * planes)
     weight = jnp.where(
-        jnp.arange(2 * planes)[None, :] <= maps[:, None], both[None, :, -3] - inverse[:, None] * both[None, :, -2], 0.0
+        maps[None, :] <= maps[:, None], both[None, :, -3] - both[:, -1][:, None] * both[None, :, -2], 0.0
     )
     weight = jnp.concatenate([weight, jnp.sum(weight, axis=1, keepdims=True)], axis=1)
 
+    filters = pl.pallas_call(
+        partial(filters_kernel, L),
+        grid=(2,),
+        in_specs=[SMEM],
+        out_specs=pl.BlockSpec((1, 2, outer, slab, TC), lambda step: (step, 0, 0, 0, 0)),
+        out_shape=pltpu.HBM((2, 2, outer, slab, TC), jnp.float32),
+        compiler_params=room(16),
+        name="filters",
+    )(here)
     near_dens = pl.pallas_call(
         partial(deposit_kernel, cap, chunks),
         in_specs=[SMEM, VMEM],
@@ -662,7 +697,7 @@
             SMEM,
             SMEM,
             SMEM,
-            pl.BlockSpec((2 * planes, some // TR * outer, TR, TC), lambda step: (0, step, 0, 0)),
+            pl.BlockSpec(memory_space=pltpu.HBM),
             pl.BlockSpec((groups, 8, TC), lambda step: (0, lines // 8, 0)),
             whole(far.shape),
             whole(twiddle.shape),
@@ -679,13 +714,16 @@
             pltpu.HBM((groups, 2, 2, slab, TC), jnp.float32),
         ),
         scratch_shapes=[
-            pltpu.VMEM((outer * some, 2 * TC), jnp.bfloat16),
-            pltpu.VMEM((outer * some, 2 * TC), jnp.bfloat16),
+            pltpu.VMEM((2, outer * some, 2 * TC), jnp.bfloat16),
+            pltpu.VMEM((2, outer * some, 2 * TC), jnp.bfloat16),
             pltpu.VMEM((2 * planes, per_owner, TR, TC), jnp.float32),
+            pltpu.VMEM((2 * planes, per_owner, TR, TC), jnp.float32),
+            pltpu.VMEM((2 * planes, some // TR * outer, TR, TC), jnp.float32),
+            pltpu.SemaphoreType.DMA(()),
         ],
         compiler_params=room(28),
         name="rows",
-    )(weight, here, far_slots, near_dens, near, far, twiddle, minus)
+    )(weight, here, far_slots, in_hbm(near_dens), near, far, twiddle, minus)
     arrived = lax.all_to_all(row_sent, ("shell", "low"), split_axis=0, concat_axis=0, tiled=True)
     swaps = []
     for side in range(2):
@@ -699,7 +737,7 @@
         partial(columns_kernel, order),
         grid=(2,),
         in_specs=[
-            SMEM,
+            pl.BlockSpec(memory_space=pltpu.HBM),
             pl.BlockSpec((groups, 1, 2, slab, TC), lambda step: (0, step, 0, 0, 0)),
             whole(turn.shape),
             whole(plus.shape),
@@ -712,10 +750,12 @@
             pltpu.VMEM((2 * slab, L), jnp.bfloat16),
             pltpu.VMEM((2 * slab, L), jnp.float32),
             pltpu.VMEM((outer, 2 * slab, 2 * TC), jnp.float32),
+            pltpu.VMEM((2, outer, slab, TC), jnp.float32),
+            pltpu.SemaphoreType.DMA(()),
         ],
         compiler_params=room(32),
         name="columns",
-    )(here, arrived, turn, plus, minus)
+    )(in_hbm(filters), arrived, turn, plus, minus)
     landed = lax.all_to_all(col_sent, "low", split_axis=0, concat_axis=0, tiled=True)
     shear_one, shear_two = pl.pallas_call(
         inverse_rows_kernel,

time: 211 us -> 220 us (1.043)
  waiting for transfers between devices: 66 us -> 130 us
  blocking collectives: 53.3 us -> 0 us
  starting transfers between devices: 25.1 us -> 29.9 us
  local copies, waits for them, and re-layouts: 5.97 us -> 1.76 us
    all_to_all x1 -> x0, blocking collectives: 53.3 us -> none  [local_cube(): lax.all_to_all(row_sent, ('shell', 'low'), split_axis=0, concat_axis=0, t...]
    all_to_all x0 -> x1, waiting for transfers between devices: none -> 52.8 us  [local_cube(): lax.all_to_all(row_sent, ('shell', 'low'), split_axis=0, concat_axis=0, t...]
    ppermute x1, waiting for transfers between devices: 0.01 us -> 12.3 us  [local_cube(): other = lax.ppermute(note, 'shell', [(0, 1), (1, 0)])]
    all_to_all x0 -> x1, starting transfers between devices: none -> 5.65 us  [local_cube(): lax.all_to_all(row_sent, ('shell', 'low'), split_axis=0, concat_axis=0, t...]
    unnamed x24 -> x18, local copies, waits for them, and re-layouts: 4.77 us -> 0.74 us
    all_to_all x2, waiting for transfers between devices: 3.41 us -> 0.67 us  [cube_exchange(): lax.all_to_all(value, ('shell', 'low'), split_axis=0, concat_axis=0, tile...]
    pallas_call x1 -> x2, Pallas kernels: 14.6 us -> 15.9 us  [the longest x1 12.8 us: local_cube(): pl.pallas_call(partial(columns_kernel, order), grid=(2,), in_specs=[pl.Bl...]
  transfers between devices with their start and end apart: 6 -> 7, of which waited for: 4 -> 6; matrix products, arithmetic and copies ran while one was open for 3% -> 3% of each run, Pallas kernels for 6% -> 6%
where the time goes in v4:
time: 220 us; the launch traced here: 218 us
  waiting for transfers between devices  130 us (59%)
  Pallas kernels  50.4 us (23%)
  starting transfers between devices  29.9 us (14%)
  other arithmetic  5.56 us (3%)
    all_to_all x1, waiting for transfers between devices, local_cube(): lax.all_to_all(row_sent, ('shell', 'low'), split_axis=0, concat_axis=0, t...  52.8 us
    ppermute x1, waiting for transfers between devices, local_cube(): conv_held = lax.ppermute(conv_other, ('shell', 'upper', 'low'), swaps)  26.1 us
    ppermute x1, waiting for transfers between devices, local_cube(): raw_far = lax.ppermute(raw, 'upper', [(0, 1), (1, 0)])  21.5 us
    all_to_all x1, waiting for transfers between devices, local_cube(): lax.all_to_all(col_sent, 'low', split_axis=0, concat_axis=0, tiled=True)  16.7 us
    pallas_call x1, Pallas kernels, local_cube(): pl.pallas_call(partial(rows_kernel, cap, chunks), grid=(slab // some,), i...  14.3 us
    all_to_all x2, starting transfers between devices, cube_exchange(): lax.all_to_all(value, ('shell', 'low'), split_axis=0, concat_axis=0, tile...  13.8 us
    pallas_call x1, Pallas kernels, local_cube(): pl.pallas_call(partial(columns_kernel, order), grid=(2,), in_specs=[pl.Bl...  12.8 us
    ppermute x1, waiting for transfers between devices, local_cube(): other = lax.ppermute(note, 'shell', [(0, 1), (1, 0)])  12.3 us
  transfers between devices with their start and end apart: 7, of which 6 were waited for; matrix products, arithmetic and copies ran while one was open for 3% of the time, Pallas kernels for 6%

profile of v4, /device:TPU:1, one launch (start us, length us, event | category | flops | bytes accessed | tf_op | source)
XLA Modules:
  0.0 218.4 jit_solution(6358578765503270388)
XLA Ops:
  0.6 1.0 widen.1.raw_ref
  1.7 0.0 copy-start.4
  1.7 0.1 stack.27.at_ref
  1.8 0.7 copy-done.3
  2.5 2.7 %pack.2 = f32[16,136,128]{2,1,0:T(8,128)} custom-call(s32[6]{0:T(128)S(1)} %stack.27.at_ref, s32[2,1024]{1,0:T(2,128)S(1)} %copy-done.3, f32[2,2,64,512]{3,2,1,0:T(8,128)S(1)} %widen.1.raw_ref), custom_call_target="tpu_custom_call" | custom-call | tf_op jit(solution)/shard_map/pack/pallas_call | solution.py:639
  5.1 6.2 %all-to-all-start = ((f32[16,136,128]{2,1,0:T(8,128)}), f32[16,136,128]{2,1,0:T(8,128)S(1)}, u32[]{:S(2)}, u32[]{:S(2)}) async-start(f32[16,136,128]{2,1,0:T(8,128)} %pack.2), calls=%async_computation | async-start | bytes 2228224 | tf_op jit(solution)/shard_map/all_to_all | solution.py:606
  11.4 0.0 copy-start.8
  11.4 0.0 copy-start.7
  11.4 2.4 %collective-permute-start.1 = (f32[2,2,64,512]{3,2,1,0:T(8,128)S(1)}, f32[2,2,64,512]{3,2,1,0:T(8,128)S(1)}, u32[]{:S(2)}, u32[]{:S(2)}) collective-permute-start(f32[2,2,64,512]{3,2,1,0:T(8,128)S(1)} %widen.1.raw_ref), channel_id=1, source_target_pairs={{0,8},{8,0},{1,9},{9,1},{2,10},{10,2},{3,11},{11,3},{4,12},{12,4},... | collective-permute-start | bytes 1572872 | tf_op jit(solution)/shard_map/ppermute | solution.py:634
  13.8 21.5 %collective-permute-done.1.raw_ref = f32[2,2,64,512]{3,2,1,0:T(8,128)S(1)} collective-permute-done((f32[2,2,64,512]{3,2,1,0:T(8,128)S(1)}, f32[2,2,64,512]{3,2,1,0:T(8,128)S(1)}, u32[]{:S(2)}, u32[]{:S(2)}) %collective-permute-start.1) | collective-permute-done | bytes 524320 | tf_op jit(solution)/shard_map/ppermute | solution.py:634
  35.2 0.0 copy-done.4
  35.2 2.7 %pack.3 = f32[16,136,128]{2,1,0:T(8,128)} custom-call(s32[6]{0:T(128)S(1)} %stack.27.at_ref, s32[2,1024]{1,0:T(2,128)S(1)} %copy-done.4, f32[2,2,64,512]{3,2,1,0:T(8,128)S(1)} %collective-permute-done.1.raw_ref), custom_call_target="tpu_custom_call" | custom-call | tf_op jit(solution)/shard_map/pack/pallas_call | solution.py:639
  37.9 0.7 all-to-all-done.recv_ref.near_ref
  38.6 7.6 %all-to-all-start.1 = ((f32[16,136,128]{2,1,0:T(8,128)}), f32[16,136,128]{2,1,0:T(8,128)S(1)}, u32[]{:S(2)}, u32[]{:S(2)}) async-start(f32[16,136,128]{2,1,0:T(8,128)} %pack.3), calls=%async_computation.1 | async-start | bytes 2228224 | tf_op jit(solution)/shard_map/all_to_all | solution.py:606
  46.1 0.0 copy-done.6
  46.1 0.0 copy-done.8
  46.2 0.1 copy.22
  46.3 0.0 copy-done.7
  46.3 0.1 copy.23
  46.4 0.1 copy.21
  46.4 0.1 concatenate.12
  46.5 1.4 collective-permute-start
  47.9 12.3 %collective-permute-done = f32[2,1027]{1,0:T(2,128)S(1)} collective-permute-done((f32[2,1027]{1,0:T(2,128)S(1)}, f32[2,1027]{1,0:T(2,128)S(1)}, u32[]{:S(2)}, u32[]{:S(2)}) %collective-permute-start) | collective-permute-done | bytes 8248 | tf_op jit(solution)/shard_map/ppermute | solution.py:656
  60.2 0.2 slice_reduce_fusion.2
  60.4 0.2 subtract_select_fusion
  60.6 0.1 copy.24
  60.7 0.1 reshape.98
  60.8 0.8 select_reduce_fusion
  61.6 1.2 select_reduce_fusion.1
  62.8 0.1 reshape.101.slots_ref
  62.9 0.1 reshape.100.slots_ref
  63.0 0.1 pad_maximum_fusion.weight_ref
  63.1 7.6 %deposit.1.near_dens_ref = f32[4,128,16,128]{3,2,1,0:T(8,128)} custom-call(s32[256]{0:T(256)S(1)} %reshape.101.slots_ref, f32[16,136,128]{2,1,0:T(8,128)S(1)} %all-to-all-done.recv_ref.near_ref), custom_call_target="tpu_custom_call" | custom-call | tf_op jit(solution)/shard_map/deposit/pallas_call | solution.py:679
  70.6 0.0 all-to-all-done.1.far_ref
  70.6 0.0 copy-done.1
  70.6 0.0 copy-done.5
  70.6 14.3 %rows.1 = (f32[2,128,2048]{2,1,0:T(8,128)}, f32[2,128,2048]{2,1,0:T(8,128)}, f32[16,2,2,128,128]{4,3,2,1,0:T(8,128)}) custom-call(f32[4,5]{1,0:T(4,128)S(1)} %pad_maximum_fusion.weight_ref, s32[6]{0:T(128)S(1)} %stack.27.at_ref, s32[256]{0:T(256)S(1)} %reshape.100.slots_ref, f32[4,128,16,128]{3,2,1,0:T(8,128)} %deposit.1.near_dens_ref, ...), custom_call_target="tpu_custom_call" | custom-call | tf_op jit(solution)/shard_map/rows/pallas_call | solution.py:693
  85.0 5.6 %all-to-all-start.2 = ((f32[16,2,2,128,128]{4,3,2,1,0:T(8,128)}), f32[16,2,2,128,128]{4,3,2,1,0:T(8,128)}, u32[]{:S(2)}, u32[]{:S(2)}) async-start(f32[16,2,2,128,128]{4,3,2,1,0:T(8,128)} %get-tuple-element.10), calls=%async_computation.2 | async-start | bytes 8388608 | tf_op jit(solution)/shard_map/all_to_all | solution.py:727
  90.6 0.0 copy-start.2
  90.6 3.2 %filters.1.filters_ref = f32[2,2,16,128,128]{4,3,2,1,0:T(8,128)} custom-call(s32[6]{0:T(128)S(1)} %stack.27.at_ref), custom_call_target="tpu_custom_call" | custom-call | tf_op jit(solution)/shard_map/filters/pallas_call | solution.py:670
  93.8 52.8 %all-to-all-done.2.in_ref = f32[16,2,2,128,128]{4,3,2,1,0:T(8,128)} async-done(((f32[16,2,2,128,128]{4,3,2,1,0:T(8,128)}), f32[16,2,2,128,128]{4,3,2,1,0:T(8,128)}, u32[]{:S(2)}, u32[]{:S(2)}) %all-to-all-start.2) | async-done | bytes 4194336 | tf_op jit(solution)/shard_map/all_to_all | solution.py:727
  146.6 12.8 %columns.1 = f32[8,2,2,2,128,128]{5,4,3,2,1,0:T(8,128)} custom-call(f32[2,2,16,128,128]{4,3,2,1,0:T(8,128)} %filters.1.filters_ref, f32[16,2,2,128,128]{4,3,2,1,0:T(8,128)} %all-to-all-done.2.in_ref, f32[2,128,16]{2,1,0:T(8,128)S(1)} %copy-done.2, bf16[2,256,256]{2,1,0:T(8,128)(2,1)S(1)} %copy-done, bf16[2,256,256]{2,1,0:T(8,128)(2,1)S(1)} %copy-done.1), custom_call_target="tpu_custom_call" | custom-call | tf_op jit(solution)/shard_map/columns/pallas_call | solution.py:736
  159.4 5.4 %all-to-all-start.3 = ((f32[8,2,2,2,128,128]{5,4,3,2,1,0:T(8,128)}), f32[8,2,2,2,128,128]{5,4,3,2,1,0:T(8,128)}, u32[]{:S(2)}, u32[]{:S(2)}) async-start(f32[8,2,2,2,128,128]{5,4,3,2,1,0:T(8,128)} %columns.1), calls=%async_computation.3 | async-start | bytes 8388608 | tf_op jit(solution)/shard_map/all_to_all | solution.py:759
  164.8 1.3 collective-permute-start.2
  166.1 26.1 %collective-permute-done.2 = f32[2,128,2048]{2,1,0:T(8,128)} collective-permute-done((f32[2,128,2048]{2,1,0:T(8,128)}, f32[2,128,2048]{2,1,0:T(8,128)}, u32[]{:S(2)}, u32[]{:S(2)}) %collective-permute-start.2) | collective-permute-done | bytes 2097184 | tf_op jit(solution)/shard_map/ppermute | solution.py:734
  192.2 3.3 %broadcast_select_fusion = f32[2,128,2048]{2,1,0:T(8,128)} fusion(f32[2,128,2048]{2,1,0:T(8,128)} %get-tuple-element.8, f32[2,128,2048]{2,1,0:T(8,128)} %collective-permute-done.2, pred[]{:T(512)S(6)} %eq.35), kind=kLoop, calls=%fused_computation.1 | loop fusion | flops 524288 | bytes 6291457 | tf_op jit(solution)/shard_map/jit(_where)/select_n | solution.py:735
  195.5 16.7 %all-to-all-done.3.in_ref = f32[8,2,2,2,128,128]{5,4,3,2,1,0:T(8,128)} async-done(((f32[8,2,2,2,128,128]{5,4,3,2,1,0:T(8,128)}), f32[8,2,2,2,128,128]{5,4,3,2,1,0:T(8,128)}, u32[]{:S(2)}, u32[]{:S(2)}) %all-to-all-start.3) | async-done | bytes 4194336 | tf_op jit(solution)/shard_map/all_to_all | solution.py:759
  212.2 6.3 %inverse_rows.1 = (f32[2,128,2048]{2,1,0:T(8,128)}, f32[2,128,2048]{2,1,0:T(8,128)}) custom-call(f32[8,2,2,2,128,128]{5,4,3,2,1,0:T(8,128)} %all-to-all-done.3.in_ref, f32[2,16,128]{2,1,0:T(8,128)S(1)} %copy-done.5, bf16[2,256,256]{2,1,0:T(8,128)(2,1)S(1)} %copy-done), custom_call_target="tpu_custom_call" | custom-call | tf_op jit(solution)/shard_map/inverse_rows/pallas_call | solution.py:760
  (15 shorter events, 0.1 us)
Async XLA Ops:
  1.7 33.6 %copy-start.4 = (s32[2,1024]{1,0:T(2,128)S(1)}, s32[2,1024]{1,0:T(2,128)}, u32[]{:S(2)}) copy-start(s32[2,1024]{1,0:T(2,128)} %table_ref.5) | copy-start | bytes 24580
  1.8 0.7 copy-start.3
  5.1 33.4 %all-to-all-start = ((f32[16,136,128]{2,1,0:T(8,128)}), f32[16,136,128]{2,1,0:T(8,128)S(1)}, u32[]{:S(2)}, u32[]{:S(2)}) async-start(f32[16,136,128]{2,1,0:T(8,128)} %pack.2), calls=%async_computation | async-start | bytes 2228224 | tf_op jit(solution)/shard_map/all_to_all | solution.py:606
  11.4 34.8 %copy-start.6 = (f32[2]{0:T(128)S(1)}, f32[2]{0:T(128)}, u32[]{:S(2)}) copy-start(f32[2]{0:T(128)} %param.14) | copy-start | bytes 28
  11.4 34.8 %copy-start.8 = (f32[2]{0:T(128)S(1)}, f32[2]{0:T(128)}, u32[]{:S(2)}) copy-start(f32[2]{0:T(128)} %param.13) | copy-start | bytes 28
  11.4 34.9 %copy-start.7 = (f32[2]{0:T(128)S(1)}, f32[2]{0:T(128)}, u32[]{:S(2)}) copy-start(f32[2]{0:T(128)} %param.15) | copy-start | bytes 28
  11.4 23.8 %collective-permute-start.1 = (f32[2,2,64,512]{3,2,1,0:T(8,128)S(1)}, f32[2,2,64,512]{3,2,1,0:T(8,128)S(1)}, u32[]{:S(2)}, u32[]{:S(2)}) collective-permute-start(f32[2,2,64,512]{3,2,1,0:T(8,128)S(1)} %widen.1.raw_ref), channel_id=1, source_target_pairs={{0,8},{8,0},{1,9},{9,1},{2,10},{10,2},{3,11},{11,3},{4,12},{12,4},... | collective-permute-start | bytes 1572872 | tf_op jit(solution)/shard_map/ppermute | solution.py:634
  38.6 32.1 %all-to-all-start.1 = ((f32[16,136,128]{2,1,0:T(8,128)}), f32[16,136,128]{2,1,0:T(8,128)S(1)}, u32[]{:S(2)}, u32[]{:S(2)}) async-start(f32[16,136,128]{2,1,0:T(8,128)} %pack.3), calls=%async_computation.1 | async-start | bytes 2228224 | tf_op jit(solution)/shard_map/all_to_all | solution.py:606
  46.5 13.6 %collective-permute-start = (f32[2,1027]{1,0:T(2,128)S(1)}, f32[2,1027]{1,0:T(2,128)S(1)}, u32[]{:S(2)}, u32[]{:S(2)}) collective-permute-start(f32[2,1027]{1,0:T(2,128)S(1)} %concatenate.12), channel_id=1, source_target_pairs={{0,16},{16,0},{1,17},{17,1},{2,18},{18,2},{3,19},{19,3},{4,20},{20... | collective-permute-start | bytes 24656 | tf_op jit(solution)/shard_map/ppermute | solution.py:656
  63.1 7.6 %copy-start.1 = (bf16[2,256,256]{2,1,0:T(8,128)(2,1)S(1)}, bf16[2,256,256]{2,1,0:T(8,128)(2,1)}, u32[]{:S(2)}) copy-start(bf16[2,256,256]{2,1,0:T(8,128)(2,1)} %constant.65.clone.table_ref.back_ref) | copy-start | bytes 786436
  63.1 7.6 %copy-start.5 = (f32[2,16,128]{2,1,0:T(8,128)S(1)}, f32[2,16,128]{2,1,0:T(8,128)}, u32[]{:S(2)}) copy-start(f32[2,16,128]{2,1,0:T(8,128)} %constant.63.clone.twiddle_ref) | copy-start | bytes 49156
  85.0 61.7 %all-to-all-start.2 = ((f32[16,2,2,128,128]{4,3,2,1,0:T(8,128)}), f32[16,2,2,128,128]{4,3,2,1,0:T(8,128)}, u32[]{:S(2)}, u32[]{:S(2)}) async-start(f32[16,2,2,128,128]{4,3,2,1,0:T(8,128)} %get-tuple-element.10), calls=%async_computation.2 | async-start | bytes 8388608 | tf_op jit(solution)/shard_map/all_to_all | solution.py:727
  90.6 56.0 %copy-start = (bf16[2,256,256]{2,1,0:T(8,128)(2,1)S(1)}, bf16[2,256,256]{2,1,0:T(8,128)(2,1)}, u32[]{:S(2)}) copy-start(bf16[2,256,256]{2,1,0:T(8,128)(2,1)} %constant.66.clone.forward_ref.table_ref) | copy-start | bytes 786436
  90.6 56.0 %copy-start.2 = (f32[2,128,16]{2,1,0:T(8,128)S(1)}, f32[2,128,16]{2,1,0:T(8,128)}, u32[]{:S(2)}) copy-start(f32[2,128,16]{2,1,0:T(8,128)} %constant.64.clone.turn_ref) | copy-start | bytes 49156
  159.4 52.8 %all-to-all-start.3 = ((f32[8,2,2,2,128,128]{5,4,3,2,1,0:T(8,128)}), f32[8,2,2,2,128,128]{5,4,3,2,1,0:T(8,128)}, u32[]{:S(2)}, u32[]{:S(2)}) async-start(f32[8,2,2,2,128,128]{5,4,3,2,1,0:T(8,128)} %columns.1), calls=%async_computation.3 | async-start | bytes 8388608 | tf_op jit(solution)/shard_map/all_to_all | solution.py:759
  164.8 27.4 %collective-permute-start.2 = (f32[2,128,2048]{2,1,0:T(8,128)}, f32[2,128,2048]{2,1,0:T(8,128)}, u32[]{:S(2)}, u32[]{:S(2)}) collective-permute-start(f32[2,128,2048]{2,1,0:T(8,128)} %get-tuple-element.9), channel_id=1, source_target_pairs={{0,16},{2,18},{4,20},{6,22},{9,25},{11,27},{13,29},{15,31},{17,1},... | collective-permute-start | bytes 6291464 | tf_op jit(solution)/shard_map/ppermute | solution.py:734

commit v5 on v4

--- a/solution.py
+++ b/solution.py
@@ -279,9 +279,13 @@
     return mul(left_high, right_high) + (mul(left_low, right_high) + mul(left_high, right_low))
 
 
-def widen_kernel(cell_ref, mass_ref, out_ref):
-    out_ref[0] = cell_ref[...].astype(jnp.float32)
-    out_ref[1] = mass_ref[...].astype(jnp.float32)
+def widen_kernel(cell_ref, mass_ref, all_ref, first_ref):
+    cells = cell_ref[...].astype(jnp.float32)
+    weights = mass_ref[...].astype(jnp.float32)
+    all_ref[0] = cells
+    all_ref[1] = weights
+    first_ref[0] = cells[:1]
+    first_ref[1] = weights[:1]
 
 
 def divided(value, count):
@@ -316,6 +320,8 @@
                         row = plane * lines + kind * chunks * cap + chunk * cap + rank
                         out_ref[place, pl.ds(row, 1), :] = values[at : at + 1, chunk * TC : (chunk + 1) * TC]
 
+    if out_ref.shape[1] == planes * lines:
+        return
     for plane in range(planes):
         total = jnp.sum(raw_ref[1, plane], axis=0, keepdims=True)
         total = jnp.sum(total, axis=1, keepdims=True)
@@ -324,10 +330,7 @@
             out_ref[place, planes * lines + plane : planes * lines + plane + 1, :] = line
 
 
-def deposit_kernel(cap, chunks, slots_ref, recv_ref, out_ref):
-    out_ref[...] = jnp.zeros(out_ref.shape, jnp.float32)
-    all_planes = out_ref.shape[0]
-    planes = all_planes // 2
+def deposit_into(cap, chunks, out_ref, out_planes, slots_ref, slot_planes, recv_ref, starts):
     half = recv_ref.shape[0] // 2
     width = 32
     bunch = 4
@@ -340,12 +343,11 @@
     def spread(value, slot):
         return jnp.broadcast_to(value[slot : slot + 1, :], (TR, TC)).astype(jnp.bfloat16)
 
-    for plane in range(all_planes):
-        start = (plane % planes) * 2 * chunks * cap
+    for out_plane, slot_plane, (sender, start) in zip(out_planes, slot_planes, starts):
 
         @pl.loop(0, half, unroll=True)
         def _(source):
-            place = (plane // planes) * half + source
+            place = sender * half + source
             cells = [recv_ref[place, start + k * cap : start + (k + 1) * cap, :] for k in range(chunks)]
             weights = [
                 recv_ref[place, start + (chunks + k) * cap : start + (chunks + k + 1) * cap, :] for k in range(chunks)
@@ -381,26 +383,36 @@
                     strips_of = [done[base + j * TR : base + (j + 1) * TR, side] for j in range(parts)]
                     sums.append(jnp.concatenate(strips_of, axis=1))
             for slot in range(cap):
-                tile = slots_ref[(plane * half + source) * cap + slot]
-                out_ref[plane, tile] = out_ref[plane, tile] + sums[slot]
+                tile = slots_ref[(slot_plane * half + source) * cap + slot]
+                out_ref[out_plane, tile] = out_ref[out_plane, tile] + sums[slot]
+
+
+def deposit_kernel(cap, chunks, near_slots_ref, near_ref, far_slots_ref, far_ref, out_ref):
+    out_ref[...] = jnp.zeros(out_ref.shape, jnp.float32)
+    lines = 2 * chunks * cap
+    every = range(4)
+    near_starts = [(plane // 2, (plane % 2) * lines) for plane in every]
+    deposit_into(cap, chunks, out_ref, every, near_slots_ref, every, near_ref, near_starts)
+    deposit_into(cap, chunks, out_ref, (0, 2), far_slots_ref, (0, 2), far_ref, ((0, 0), (1, 0)))
 
 
 def rows_kernel(
-    cap, chunks, weight_ref, at_ref, slots_ref, near_dens_ref, near_ref, far_ref, twiddle_ref, table_ref,
+    cap, chunks, weight_ref, at_ref, slots_ref, some_dens_ref, near_ref, far_ref, twiddle_ref, table_ref,
     mine_ref, other_ref, out_ref, high_ref, low_ref, far_dens_ref, dens_ref, maps_ref, copied,
 ):
     step = pl.program_id(0)
 
     @pl.when(step == 0)
     def _():
-        fetch = pltpu.make_async_copy(near_dens_ref, dens_ref, copied)
+        fetch = pltpu.make_async_copy(some_dens_ref, dens_ref, copied)
         fetch.start()
-        deposit_kernel(cap, chunks, slots_ref, far_ref, far_dens_ref)
+        far_dens_ref[...] = jnp.zeros(far_dens_ref.shape, jnp.float32)
+        deposit_into(cap, chunks, far_dens_ref, (0, 1), slots_ref, (1, 3), far_ref, ((0, 0), (1, 0)))
         fetch.wait()
 
     planes, slab, length = mine_ref.shape
-    all_planes = far_dens_ref.shape[0]
-    first_line = planes * 2 * cap * chunks
+    all_planes = dens_ref.shape[0]
+    first_line = 2 * cap * chunks
     outer = length // TC
     first_tile = step * (slab // TR * outer)
     half = near_ref.shape[0] // 2
@@ -422,7 +434,9 @@
         here = slice(line * TR, (line + 1) * TR)
         for col in range(outer):
             at = line * outer + col
-            tiles = [dens_ref[j, first_tile + at] + far_dens_ref[j, first_tile + at] for j in range(all_planes)]
+            tiles = [dens_ref[j, first_tile + at] for j in range(all_planes)]
+            for j in range(1, all_planes, 2):
+                tiles[j] = tiles[j] + far_dens_ref[j // 2, first_tile + at]
             maps = []
             for i in range(all_planes):
                 field = tiles[0] * factors[i][0]
@@ -618,36 +632,40 @@
     per_owner = slab // TR * outer
     cap = max(1, 2 * local_tiles // groups)
     chunks = per_tile // TC
-    lines = 2 * chunks * cap * planes
+    lines = 2 * chunks * cap
     part = (shell + low) % 2
     held = part * half + low
     order = [((s // half + s % 2) % 2) * half + s % half for s in range(groups)]
 
-    raw = pl.pallas_call(
+    raw, raw_first = pl.pallas_call(
         widen_kernel,
         in_specs=[VMEM, VMEM],
-        out_specs=VMEM,
-        out_shape=jax.ShapeDtypeStruct((2, planes, local_tiles, per_tile), jnp.float32),
+        out_specs=(VMEM, VMEM),
+        out_shape=(
+            jax.ShapeDtypeStruct((2, planes, local_tiles, per_tile), jnp.float32),
+            jax.ShapeDtypeStruct((2, 1, local_tiles, per_tile), jnp.float32),
+        ),
         compiler_params=room(8),
         name="widen",
     )(in_hbm(cell_index), in_hbm(masses))
-    raw_far = lax.ppermute(raw, "upper", [(0, 1), (1, 0)])
-
+    raw_far = lax.ppermute(raw_first, "upper", [(0, 1), (1, 0)])
     here = jnp.stack([upper * half + low, (1 - upper) * half + low, shell, 1 - shell, low, upper]).astype(jnp.int32)
 
-    def pack(which, lists):
+    def pack(which, lists, spare):
+        count = lists.shape[1]
         return pl.pallas_call(
             partial(pack_kernel, half, cap, per_owner, which),
             in_specs=[SMEM, SMEM, VMEM],
             out_specs=VMEM,
-            out_shape=jax.ShapeDtypeStruct((groups, lines + 8, TC), jnp.float32),
-            scratch_shapes=[pltpu.SMEM((groups,), jnp.int32)] * planes,
+            out_shape=jax.ShapeDtypeStruct((groups, count * lines + spare, TC), jnp.float32),
+            scratch_shapes=[pltpu.SMEM((groups,), jnp.int32)] * count,
             compiler_params=room(12),
             name="pack",
         )(here, block_tile, lists)
 
-    near = cube_exchange(pack(0, raw))
-    far = cube_exchange(pack(1, raw_far))
+    near = cube_exchange(pack(0, raw, 8))
+    far_second = lax.ppermute(near[:, lines:, :], "upper", [(0, 1), (1, 0)])
+    far_first = cube_exchange(pack(1, raw_far, 0))
 
     note = jnp.concatenate(
         [block_tile.astype(jnp.float32), plane_coef[:, None], (plane_coef * plane_dist)[:, None], source_inv[:, None]],
@@ -676,14 +694,14 @@
         compiler_params=room(16),
         name="filters",
     )(here)
-    near_dens = pl.pallas_call(
+    some_dens = pl.pallas_call(
         partial(deposit_kernel, cap, chunks),
-        in_specs=[SMEM, VMEM],
+        in_specs=[SMEM, VMEM, SMEM, VMEM],
         out_specs=VMEM,
         out_shape=pltpu.HBM((2 * planes, per_owner, TR, TC), jnp.float32),
         compiler_params=room(16),
         name="deposit",
-    )(near_slots, near)
+    )(near_slots, near, far_slots, far_first)
     twiddle = jnp.asarray(twiddle_pair(outer, TC))
     turn = jnp.asarray(twiddle_pair(outer, TC).transpose(0, 2, 1))
     minus = jnp.asarray(dft_block(TC, -1.0))
@@ -698,8 +716,8 @@
             SMEM,
             SMEM,
             pl.BlockSpec(memory_space=pltpu.HBM),
-            pl.BlockSpec((groups, 8, TC), lambda step: (0, lines // 8, 0)),
-            whole(far.shape),
+            pl.BlockSpec((groups, 8, TC), lambda step: (0, planes * lines // 8, 0)),
+            whole(far_second.shape),
             whole(twiddle.shape),
             whole(minus.shape),
         ],
@@ -716,14 +734,14 @@
         scratch_shapes=[
             pltpu.VMEM((2, outer * some, 2 * TC), jnp.bfloat16),
             pltpu.VMEM((2, outer * some, 2 * TC), jnp.bfloat16),
-            pltpu.VMEM((2 * planes, per_owner, TR, TC), jnp.float32),
+            pltpu.VMEM((planes, per_owner, TR, TC), jnp.float32),
             pltpu.VMEM((2 * planes, per_owner, TR, TC), jnp.float32),
             pltpu.VMEM((2 * planes, some // TR * outer, TR, TC), jnp.float32),
             pltpu.SemaphoreType.DMA(()),
         ],
         compiler_params=room(28),
         name="rows",
-    )(weight, here, far_slots, in_hbm(near_dens), near, far, twiddle, minus)
+    )(weight, here, far_slots, in_hbm(some_dens), near, far_second, twiddle, minus)
     arrived = lax.all_to_all(row_sent, ("shell", "low"), split_axis=0, concat_axis=0, tiled=True)
     swaps = []
     for side in range(2):

time: 220 us -> 215 us (0.977)
  waiting for transfers between devices: 130 us -> 127 us
    all_to_all x2, waiting for transfers between devices: 0.67 us -> 11.3 us  [cube_exchange(): lax.all_to_all(value, ('shell', 'low'), split_axis=0, concat_axis=0, tile...]
    ppermute x1 -> x2, waiting for transfers between devices: 21.5 us -> 14.4 us  [the longest x1 8.03 us: local_cube(): raw_far = lax.ppermute(raw_first, 'upper', [(0, 1), (1, 0)])]
    ppermute x1, waiting for transfers between devices: 12.3 us -> 5.84 us  [local_cube(): other = lax.ppermute(note, 'shell', [(0, 1), (1, 0)])]
    pallas_call x1, Pallas kernels: 14.3 us -> 11.8 us  [local_cube(): pl.pallas_call(partial(rows_kernel, cap, chunks), grid=(slab // some,), i...]
    pallas_call x1, Pallas kernels: 7.55 us -> 9.8 us  [local_cube(): pl.pallas_call(partial(deposit_kernel, cap, chunks), in_specs=[SMEM, VMEM...]
  transfers between devices with their start and end apart: 7 -> 8, of which waited for: 6 -> 8; matrix products, arithmetic and copies ran while one was open for 3% -> 3% of each run, Pallas kernels for 6% -> 7%
where the time goes in v5:
time: 215 us; the launch traced here: 214 us
  waiting for transfers between devices  127 us (59%)
  Pallas kernels  49.4 us (23%)
  starting transfers between devices  28.8 us (13%)
  other arithmetic  5.56 us (3%)
    all_to_all x1, waiting for transfers between devices, local_cube(): lax.all_to_all(row_sent, ('shell', 'low'), split_axis=0, concat_axis=0, t...  52.8 us
    ppermute x1, waiting for transfers between devices, local_cube(): conv_held = lax.ppermute(conv_other, ('shell', 'upper', 'low'), swaps)  25.9 us
    all_to_all x1, waiting for transfers between devices, local_cube(): lax.all_to_all(col_sent, 'low', split_axis=0, concat_axis=0, tiled=True)  16.9 us
    all_to_all x2, starting transfers between devices, cube_exchange(): lax.all_to_all(value, ('shell', 'low'), split_axis=0, concat_axis=0, tile...  13.1 us
    pallas_call x1, Pallas kernels, local_cube(): pl.pallas_call(partial(columns_kernel, order), grid=(2,), in_specs=[pl.Bl...  12.8 us
    pallas_call x1, Pallas kernels, local_cube(): pl.pallas_call(partial(rows_kernel, cap, chunks), grid=(slab // some,), i...  11.8 us
    all_to_all x2, waiting for transfers between devices, cube_exchange(): lax.all_to_all(value, ('shell', 'low'), split_axis=0, concat_axis=0, tile...  11.3 us
    pallas_call x1, Pallas kernels, local_cube(): pl.pallas_call(partial(deposit_kernel, cap, chunks), in_specs=[SMEM, VMEM...  9.8 us
  transfers between devices with their start and end apart: 8, of which 8 were waited for; matrix products, arithmetic and copies ran while one was open for 3% of the time, Pallas kernels for 7%

profile of v5, /device:TPU:1, one launch (start us, length us, event | category | flops | bytes accessed | tf_op | source)
XLA Modules:
  0.0 213.6 jit_solution(6432839115003203669)
XLA Ops:
  0.6 0.0 copy-start.4
  0.7 0.0 copy-start.7
  0.7 0.0 copy-start.9
  0.7 0.0 copy-start.8
  0.7 1.1 widen.1
  1.7 0.1 stack.27.at_ref
  1.8 0.7 copy-done.3
  2.5 2.7 %pack.2 = f32[16,136,128]{2,1,0:T(8,128)} custom-call(s32[6]{0:T(128)S(1)} %stack.27.at_ref, s32[2,1024]{1,0:T(2,128)S(1)} %copy-done.3, f32[2,2,64,512]{3,2,1,0:T(8,128)S(1)} %get-tuple-element.10.raw_ref), custom_call_target="tpu_custom_call" | custom-call | tf_op jit(solution)/shard_map/pack/pallas_call | solution.py:656
  5.2 6.2 %all-to-all-start = ((f32[16,136,128]{2,1,0:T(8,128)}), f32[16,136,128]{2,1,0:T(8,128)S(1)}, u32[]{:S(2)}, u32[]{:S(2)}) async-start(f32[16,136,128]{2,1,0:T(8,128)} %pack.2), calls=%async_computation | async-start | bytes 2228224 | tf_op jit(solution)/shard_map/all_to_all | solution.py:620
  11.5 0.1 copy.22
  11.6 0.1 copy.23
  11.7 0.1 copy.21
  11.8 0.1 concatenate.12
  11.9 1.4 collective-permute-start
  13.2 2.3 %collective-permute-start.1 = (f32[2,1,64,512]{3,2,1,0:T(8,128)S(1)}, f32[2,1,64,512]{3,2,1,0:T(8,128)S(1)}, u32[]{:S(2)}, u32[]{:S(2)}) collective-permute-start(f32[2,1,64,512]{3,2,1,0:T(8,128)S(1)} %get-tuple-element.11), channel_id=1, source_target_pairs={{0,8},{8,0},{1,9},{9,1},{2,10},{10,2},{3,11},{11,3},{4,12},{12,4},... | collective-permute-start | bytes 786440 | tf_op jit(solution)/shard_map/ppermute | solution.py:651
  15.6 5.8 %collective-permute-done = f32[2,1027]{1,0:T(2,128)S(1)} collective-permute-done((f32[2,1027]{1,0:T(2,128)S(1)}, f32[2,1027]{1,0:T(2,128)S(1)}, u32[]{:S(2)}, u32[]{:S(2)}) %collective-permute-start) | collective-permute-done | bytes 8248 | tf_op jit(solution)/shard_map/ppermute | solution.py:674
  21.4 0.2 slice_reduce_fusion.2
  21.6 8.0 %collective-permute-done.1.raw_ref = f32[2,1,64,512]{3,2,1,0:T(8,128)S(1)} collective-permute-done((f32[2,1,64,512]{3,2,1,0:T(8,128)S(1)}, f32[2,1,64,512]{3,2,1,0:T(8,128)S(1)}, u32[]{:S(2)}, u32[]{:S(2)}) %collective-permute-start.1) | collective-permute-done | bytes 262176 | tf_op jit(solution)/shard_map/ppermute | solution.py:651
  29.6 1.9 pack.3
  31.6 1.4 all-to-all-done.near_ref
  33.0 6.8 %all-to-all-start.1 = ((f32[16,64,128]{2,1,0:T(8,128)}), f32[16,64,128]{2,1,0:T(8,128)S(1)}, u32[]{:S(2)}, u32[]{:S(2)}) async-start(f32[16,64,128]{2,1,0:T(8,128)} %pack.3), calls=%async_computation.1 | async-start | bytes 1048576 | tf_op jit(solution)/shard_map/all_to_all | solution.py:620
  39.9 0.2 subtract_select_fusion
  40.0 0.1 reshape.98
  40.2 0.1 collective-permute-start.2
  40.3 0.8 select_reduce_fusion
  41.1 0.1 copy.24
  41.2 1.2 select_reduce_fusion.1
  42.4 0.1 reshape.101.near_slots_ref
  42.5 0.1 reshape.100.far_slots_ref.slots_ref
  42.6 0.1 pad_maximum_fusion.weight_ref
  42.6 9.8 %all-to-all-done.1.far_ref = f32[16,64,128]{2,1,0:T(8,128)S(1)} async-done(((f32[16,64,128]{2,1,0:T(8,128)}), f32[16,64,128]{2,1,0:T(8,128)S(1)}, u32[]{:S(2)}, u32[]{:S(2)}) %all-to-all-start.1) | async-done | bytes 524320 | tf_op jit(solution)/shard_map/all_to_all | solution.py:620
  52.5 9.8 %deposit.1.some_dens_ref = f32[4,128,16,128]{3,2,1,0:T(8,128)} custom-call(s32[256]{0:T(256)S(1)} %reshape.101.near_slots_ref, f32[16,136,128]{2,1,0:T(8,128)S(1)} %all-to-all-done.near_ref, s32[256]{0:T(256)S(1)} %reshape.100.far_slots_ref.slots_ref, f32[16,64,128]{2,1,0:T(8,128)S(1)} %all-to-all-done.1.far_ref), custom_call_target="tpu_custom_call" | custom-call | tf_op jit(solution)/shard_map/deposit/pallas_call | solution.py:697
  62.3 6.4 %collective-permute-done.2.far_ref = f32[16,72,128]{2,1,0:T(8,128)S(1)} collective-permute-done((f32[16,72,128]{2,1,0:T(8,128)S(1)}, f32[16,72,128]{2,1,0:T(8,128)S(1)}, u32[]{:S(2)}, u32[]{:S(2)}) %collective-permute-start.2) | collective-permute-done | bytes 589856 | tf_op jit(solution)/shard_map/ppermute | solution.py:667
  68.6 0.0 copy-done.1
  68.7 11.8 %rows.1 = (f32[2,128,2048]{2,1,0:T(8,128)}, f32[2,128,2048]{2,1,0:T(8,128)}, f32[16,2,2,128,128]{4,3,2,1,0:T(8,128)}) custom-call(f32[4,5]{1,0:T(4,128)S(1)} %pad_maximum_fusion.weight_ref, s32[6]{0:T(128)S(1)} %stack.27.at_ref, s32[256]{0:T(256)S(1)} %reshape.100.far_slots_ref.slots_ref, f32[4,128,16,128]{3,2,1,0:T(8,128)} %deposit.1.some_dens_ref, ...), custom_call_target="tpu_custom_call" | custom-call | tf_op jit(solution)/shard_map/rows/pallas_call | solution.py:711
  80.4 5.2 %all-to-all-start.2 = ((f32[16,2,2,128,128]{4,3,2,1,0:T(8,128)}), f32[16,2,2,128,128]{4,3,2,1,0:T(8,128)}, u32[]{:S(2)}, u32[]{:S(2)}) async-start(f32[16,2,2,128,128]{4,3,2,1,0:T(8,128)} %get-tuple-element.14), calls=%async_computation.2 | async-start | bytes 8388608 | tf_op jit(solution)/shard_map/all_to_all | solution.py:745
  85.7 0.0 copy-start.2
  85.7 3.2 %filters.1.filters_ref = f32[2,2,16,128,128]{4,3,2,1,0:T(8,128)} custom-call(s32[6]{0:T(128)S(1)} %stack.27.at_ref), custom_call_target="tpu_custom_call" | custom-call | tf_op jit(solution)/shard_map/filters/pallas_call | solution.py:688
  88.8 52.8 %all-to-all-done.2.in_ref = f32[16,2,2,128,128]{4,3,2,1,0:T(8,128)} async-done(((f32[16,2,2,128,128]{4,3,2,1,0:T(8,128)}), f32[16,2,2,128,128]{4,3,2,1,0:T(8,128)}, u32[]{:S(2)}, u32[]{:S(2)}) %all-to-all-start.2) | async-done | bytes 4194336 | tf_op jit(solution)/shard_map/all_to_all | solution.py:745
  141.7 0.0 copy-done
  141.7 12.8 %columns.1 = f32[8,2,2,2,128,128]{5,4,3,2,1,0:T(8,128)} custom-call(f32[2,2,16,128,128]{4,3,2,1,0:T(8,128)} %filters.1.filters_ref, f32[16,2,2,128,128]{4,3,2,1,0:T(8,128)} %all-to-all-done.2.in_ref, f32[2,128,16]{2,1,0:T(8,128)S(1)} %copy-done.2, bf16[2,256,256]{2,1,0:T(8,128)(2,1)S(1)} %copy-done, bf16[2,256,256]{2,1,0:T(8,128)(2,1)S(1)} %copy-done.1), custom_call_target="tpu_custom_call" | custom-call | tf_op jit(solution)/shard_map/columns/pallas_call | solution.py:754
  154.4 0.0 copy-start.6
  154.4 5.5 %all-to-all-start.3 = ((f32[8,2,2,2,128,128]{5,4,3,2,1,0:T(8,128)}), f32[8,2,2,2,128,128]{5,4,3,2,1,0:T(8,128)}, u32[]{:S(2)}, u32[]{:S(2)}) async-start(f32[8,2,2,2,128,128]{5,4,3,2,1,0:T(8,128)} %columns.1), calls=%async_computation.3 | async-start | bytes 8388608 | tf_op jit(solution)/shard_map/all_to_all | solution.py:777
  160.0 1.3 collective-permute-start.3
  161.3 25.9 %collective-permute-done.3 = f32[2,128,2048]{2,1,0:T(8,128)} collective-permute-done((f32[2,128,2048]{2,1,0:T(8,128)S(1)}, f32[2,128,2048]{2,1,0:T(8,128)}, u32[]{:S(2)}, u32[]{:S(2)}) %collective-permute-start.3) | collective-permute-done | bytes 2097184 | tf_op jit(solution)/shard_map/ppermute | solution.py:752
  187.2 3.3 %broadcast_select_fusion = f32[2,128,2048]{2,1,0:T(8,128)} fusion(f32[2,128,2048]{2,1,0:T(8,128)} %get-tuple-element.12, f32[2,128,2048]{2,1,0:T(8,128)} %collective-permute-done.3, pred[]{:T(512)S(6)} %eq.35), kind=kLoop, calls=%fused_computation.1 | loop fusion | flops 524288 | bytes 6291457 | tf_op jit(solution)/shard_map/jit(_where)/select_n | solution.py:753
  190.4 16.9 %all-to-all-done.3.in_ref = f32[8,2,2,2,128,128]{5,4,3,2,1,0:T(8,128)} async-done(((f32[8,2,2,2,128,128]{5,4,3,2,1,0:T(8,128)}), f32[8,2,2,2,128,128]{5,4,3,2,1,0:T(8,128)}, u32[]{:S(2)}, u32[]{:S(2)}) %all-to-all-start.3) | async-done | bytes 4194336 | tf_op jit(solution)/shard_map/all_to_all | solution.py:777
  207.3 6.3 %inverse_rows.1 = (f32[2,128,2048]{2,1,0:T(8,128)}, f32[2,128,2048]{2,1,0:T(8,128)}) custom-call(f32[8,2,2,2,128,128]{5,4,3,2,1,0:T(8,128)} %all-to-all-done.3.in_ref, f32[2,16,128]{2,1,0:T(8,128)S(1)} %copy-done.5, bf16[2,256,256]{2,1,0:T(8,128)(2,1)S(1)} %copy-done), custom_call_target="tpu_custom_call" | custom-call | tf_op jit(solution)/shard_map/inverse_rows/pallas_call | solution.py:778
  (20 shorter events, 0.2 us)
Async XLA Ops:
  0.6 10.8 %copy-start.4 = (s32[2,1024]{1,0:T(2,128)S(1)}, s32[2,1024]{1,0:T(2,128)}, u32[]{:S(2)}) copy-start(s32[2,1024]{1,0:T(2,128)} %table_ref.5) | copy-start | bytes 24580
  0.7 10.8 %copy-start.7 = (f32[2]{0:T(128)S(1)}, f32[2]{0:T(128)}, u32[]{:S(2)}) copy-start(f32[2]{0:T(128)} %param.14) | copy-start | bytes 28
  0.7 10.8 %copy-start.9 = (f32[2]{0:T(128)S(1)}, f32[2]{0:T(128)}, u32[]{:S(2)}) copy-start(f32[2]{0:T(128)} %param.13) | copy-start | bytes 28
  0.7 10.9 %copy-start.8 = (f32[2]{0:T(128)S(1)}, f32[2]{0:T(128)}, u32[]{:S(2)}) copy-start(f32[2]{0:T(128)} %param.15) | copy-start | bytes 28
  1.8 0.7 copy-start.3
  5.2 27.8 %all-to-all-start = ((f32[16,136,128]{2,1,0:T(8,128)}), f32[16,136,128]{2,1,0:T(8,128)S(1)}, u32[]{:S(2)}, u32[]{:S(2)}) async-start(f32[16,136,128]{2,1,0:T(8,128)} %pack.2), calls=%async_computation | async-start | bytes 2228224 | tf_op jit(solution)/shard_map/all_to_all | solution.py:620
  11.9 9.5 %collective-permute-start = (f32[2,1027]{1,0:T(2,128)S(1)}, f32[2,1027]{1,0:T(2,128)S(1)}, u32[]{:S(2)}, u32[]{:S(2)}) collective-permute-start(f32[2,1027]{1,0:T(2,128)S(1)} %concatenate.12), channel_id=1, source_target_pairs={{0,16},{16,0},{1,17},{17,1},{2,18},{18,2},{3,19},{19,3},{4,20},{20... | collective-permute-start | bytes 24656 | tf_op jit(solution)/shard_map/ppermute | solution.py:674
  13.2 16.4 %collective-permute-start.1 = (f32[2,1,64,512]{3,2,1,0:T(8,128)S(1)}, f32[2,1,64,512]{3,2,1,0:T(8,128)S(1)}, u32[]{:S(2)}, u32[]{:S(2)}) collective-permute-start(f32[2,1,64,512]{3,2,1,0:T(8,128)S(1)} %get-tuple-element.11), channel_id=1, source_target_pairs={{0,8},{8,0},{1,9},{9,1},{2,10},{10,2},{3,11},{11,3},{4,12},{12,4},... | collective-permute-start | bytes 786440 | tf_op jit(solution)/shard_map/ppermute | solution.py:651
  33.0 19.4 %all-to-all-start.1 = ((f32[16,64,128]{2,1,0:T(8,128)}), f32[16,64,128]{2,1,0:T(8,128)S(1)}, u32[]{:S(2)}, u32[]{:S(2)}) async-start(f32[16,64,128]{2,1,0:T(8,128)} %pack.3), calls=%async_computation.1 | async-start | bytes 1048576 | tf_op jit(solution)/shard_map/all_to_all | solution.py:620
  40.2 28.4 %collective-permute-start.2 = (f32[16,72,128]{2,1,0:T(8,128)S(1)}, f32[16,72,128]{2,1,0:T(8,128)S(1)}, u32[]{:S(2)}, u32[]{:S(2)}) collective-permute-start(f32[16,72,128]{2,1,0:T(8,128)S(1)} %slice.24), channel_id=1, source_target_pairs={{0,8},{8,0},{1,9},{9,1},{2,10},{10,2},{3,11},{11,3},{4,12},{12,4},... | collective-permute-start | bytes 1769480 | tf_op jit(solution)/shard_map/ppermute | solution.py:667
  42.6 26.0 %copy-start.1 = (bf16[2,256,256]{2,1,0:T(8,128)(2,1)S(1)}, bf16[2,256,256]{2,1,0:T(8,128)(2,1)}, u32[]{:S(2)}) copy-start(bf16[2,256,256]{2,1,0:T(8,128)(2,1)} %constant.65.clone.table_ref.back_ref) | copy-start | bytes 786436
  42.6 26.0 %copy-start.5 = (f32[2,16,128]{2,1,0:T(8,128)S(1)}, f32[2,16,128]{2,1,0:T(8,128)}, u32[]{:S(2)}) copy-start(f32[2,16,128]{2,1,0:T(8,128)} %constant.63.clone.twiddle_ref) | copy-start | bytes 49156
  80.4 61.2 %all-to-all-start.2 = ((f32[16,2,2,128,128]{4,3,2,1,0:T(8,128)}), f32[16,2,2,128,128]{4,3,2,1,0:T(8,128)}, u32[]{:S(2)}, u32[]{:S(2)}) async-start(f32[16,2,2,128,128]{4,3,2,1,0:T(8,128)} %get-tuple-element.14), calls=%async_computation.2 | async-start | bytes 8388608 | tf_op jit(solution)/shard_map/all_to_all | solution.py:745
  85.6 56.0 %copy-start = (bf16[2,256,256]{2,1,0:T(8,128)(2,1)S(1)}, bf16[2,256,256]{2,1,0:T(8,128)(2,1)}, u32[]{:S(2)}) copy-start(bf16[2,256,256]{2,1,0:T(8,128)(2,1)} %constant.66.clone.forward_ref.table_ref) | copy-start | bytes 786436
  85.7 56.0 %copy-start.2 = (f32[2,128,16]{2,1,0:T(8,128)S(1)}, f32[2,128,16]{2,1,0:T(8,128)}, u32[]{:S(2)}) copy-start(f32[2,128,16]{2,1,0:T(8,128)} %constant.64.clone.turn_ref) | copy-start | bytes 49156
  154.4 5.6 %copy-start.6 = (f32[2,128,2048]{2,1,0:T(8,128)S(1)}, f32[2,128,2048]{2,1,0:T(8,128)}, u32[]{:S(2)}) copy-start(f32[2,128,2048]{2,1,0:T(8,128)} %get-tuple-element.13) | copy-start | bytes 6291460
  154.4 52.9 %all-to-all-start.3 = ((f32[8,2,2,2,128,128]{5,4,3,2,1,0:T(8,128)}), f32[8,2,2,2,128,128]{5,4,3,2,1,0:T(8,128)}, u32[]{:S(2)}, u32[]{:S(2)}) async-start(f32[8,2,2,2,128,128]{5,4,3,2,1,0:T(8,128)} %columns.1), calls=%async_computation.3 | async-start | bytes 8388608 | tf_op jit(solution)/shard_map/all_to_all | solution.py:777
  160.0 27.2 %collective-permute-start.3 = (f32[2,128,2048]{2,1,0:T(8,128)S(1)}, f32[2,128,2048]{2,1,0:T(8,128)}, u32[]{:S(2)}, u32[]{:S(2)}) collective-permute-start(f32[2,128,2048]{2,1,0:T(8,128)S(1)} %copy-done.6), channel_id=1, source_target_pairs={{0,16},{2,18},{4,20},{6,22},{9,25},{11,27},{13,29},{15,31},{17,1},... | collective-permute-start | bytes 6291464 | tf_op jit(solution)/shard_map/ppermute | solution.py:752

commit v6 on v5

--- a/solution.py
+++ b/solution.py
@@ -387,28 +387,35 @@
                 out_ref[out_plane, tile] = out_ref[out_plane, tile] + sums[slot]
 
 
-def deposit_kernel(cap, chunks, near_slots_ref, near_ref, far_slots_ref, far_ref, out_ref):
+def deposit_kernel(cap, chunks, slots_ref, near_ref, out_ref):
     out_ref[...] = jnp.zeros(out_ref.shape, jnp.float32)
     lines = 2 * chunks * cap
     every = range(4)
-    near_starts = [(plane // 2, (plane % 2) * lines) for plane in every]
-    deposit_into(cap, chunks, out_ref, every, near_slots_ref, every, near_ref, near_starts)
-    deposit_into(cap, chunks, out_ref, (0, 2), far_slots_ref, (0, 2), far_ref, ((0, 0), (1, 0)))
+    starts = [(plane // 2, (plane % 2) * lines) for plane in every]
+    deposit_into(cap, chunks, out_ref, every, slots_ref, every, near_ref, starts)
+
+
+def deposit_first_kernel(cap, chunks, slots_ref, first_ref, out_ref):
+    out_ref[...] = jnp.zeros(out_ref.shape, jnp.float32)
+    deposit_into(cap, chunks, out_ref, (0, 1), slots_ref, (0, 2), first_ref, ((0, 0), (1, 0)))
 
 
 def rows_kernel(
-    cap, chunks, weight_ref, at_ref, slots_ref, some_dens_ref, near_ref, far_ref, twiddle_ref, table_ref,
-    mine_ref, other_ref, out_ref, high_ref, low_ref, far_dens_ref, dens_ref, maps_ref, copied,
+    cap, chunks, weight_ref, at_ref, slots_ref, near_dens_ref, first_dens_ref, near_ref, far_ref, twiddle_ref, table_ref,
+    mine_ref, other_ref, out_ref, high_ref, low_ref, far_dens_ref, dens_ref, first_ref, maps_ref, copied, copied_first,
 ):
     step = pl.program_id(0)
 
     @pl.when(step == 0)
     def _():
-        fetch = pltpu.make_async_copy(some_dens_ref, dens_ref, copied)
+        fetch = pltpu.make_async_copy(near_dens_ref, dens_ref, copied)
         fetch.start()
+        fetch_first = pltpu.make_async_copy(first_dens_ref, first_ref, copied_first)
+        fetch_first.start()
         far_dens_ref[...] = jnp.zeros(far_dens_ref.shape, jnp.float32)
         deposit_into(cap, chunks, far_dens_ref, (0, 1), slots_ref, (1, 3), far_ref, ((0, 0), (1, 0)))
         fetch.wait()
+        fetch_first.wait()
 
     planes, slab, length = mine_ref.shape
     all_planes = dens_ref.shape[0]
@@ -434,9 +441,8 @@
         here = slice(line * TR, (line + 1) * TR)
         for col in range(outer):
             at = line * outer + col
-            tiles = [dens_ref[j, first_tile + at] for j in range(all_planes)]
-            for j in range(1, all_planes, 2):
-                tiles[j] = tiles[j] + far_dens_ref[j // 2, first_tile + at]
+            rest = (first_ref, far_dens_ref)
+            tiles = [dens_ref[j, first_tile + at] + rest[j % 2][j // 2, first_tile + at] for j in range(all_planes)]
             maps = []
             for i in range(all_planes):
                 field = tiles[0] * factors[i][0]
@@ -694,14 +700,22 @@
         compiler_params=room(16),
         name="filters",
     )(here)
-    some_dens = pl.pallas_call(
+    near_dens = pl.pallas_call(
         partial(deposit_kernel, cap, chunks),
-        in_specs=[SMEM, VMEM, SMEM, VMEM],
+        in_specs=[SMEM, VMEM],
         out_specs=VMEM,
         out_shape=pltpu.HBM((2 * planes, per_owner, TR, TC), jnp.float32),
         compiler_params=room(16),
         name="deposit",
-    )(near_slots, near, far_slots, far_first)
+    )(near_slots, near)
+    first_dens = pl.pallas_call(
+        partial(deposit_first_kernel, cap, chunks),
+        in_specs=[SMEM, VMEM],
+        out_specs=VMEM,
+        out_shape=pltpu.HBM((planes, per_owner, TR, TC), jnp.float32),
+        compiler_params=room(16),
+        name="deposit_first",
+    )(far_slots, far_first)
     twiddle = jnp.asarray(twiddle_pair(outer, TC))
     turn = jnp.asarray(twiddle_pair(outer, TC).transpose(0, 2, 1))
     minus = jnp.asarray(dft_block(TC, -1.0))
@@ -715,6 +729,7 @@
             SMEM,
             SMEM,
             SMEM,
+            pl.BlockSpec(memory_space=pltpu.HBM),
             pl.BlockSpec(memory_space=pltpu.HBM),
             pl.BlockSpec((groups, 8, TC), lambda step: (0, planes * lines // 8, 0)),
             whole(far_second.shape),
@@ -736,12 +751,14 @@
             pltpu.VMEM((2, outer * some, 2 * TC), jnp.bfloat16),
             pltpu.VMEM((planes, per_owner, TR, TC), jnp.float32),
             pltpu.VMEM((2 * planes, per_owner, TR, TC), jnp.float32),
+            pltpu.VMEM((planes, per_owner, TR, TC), jnp.float32),
             pltpu.VMEM((2 * planes, some // TR * outer, TR, TC), jnp.float32),
+            pltpu.SemaphoreType.DMA(()),
             pltpu.SemaphoreType.DMA(()),
         ],
         compiler_params=room(28),
         name="rows",
-    )(weight, here, far_slots, in_hbm(some_dens), near, far_second, twiddle, minus)
+    )(weight, here, far_slots, in_hbm(near_dens), in_hbm(first_dens), near, far_second, twiddle, minus)
     arrived = lax.all_to_all(row_sent, ("shell", "low"), split_axis=0, concat_axis=0, tiled=True)
     swaps = []
     for side in range(2):

time: 215 us -> 216 us (level)
  Pallas kernels: 49.4 us -> 52.3 us
    pallas_call x0 -> x1, Pallas kernels: none -> 4.5 us  [local_cube(): pl.pallas_call(partial(deposit_first_kernel, cap, chunks), in_specs=[SMEM...]
    pallas_call x1, Pallas kernels: 9.8 us -> 7.54 us  [local_cube(): pl.pallas_call(partial(deposit_kernel, cap, chunks), in_specs=[SMEM, VMEM...]
    ppermute x1, waiting for transfers between devices: 6.37 us -> 4.14 us  [local_cube(): far_second = lax.ppermute(near[:, lines:, :], 'upper', [(0, 1), (1, 0)])]
  transfers between devices with their start and end apart: 8 -> 8, of which waited for: 8 -> 8; matrix products, arithmetic and copies ran while one was open for 3% -> 3% of each run, Pallas kernels for 7% -> 8%
where the time goes in v6:
time: 216 us; the launch traced here: 214 us
  waiting for transfers between devices  125 us (58%)
  Pallas kernels  52.3 us (24%)
  starting transfers between devices  29 us (13%)
  other arithmetic  5.73 us (3%)
    all_to_all x1, waiting for transfers between devices, local_cube(): lax.all_to_all(row_sent, ('shell', 'low'), split_axis=0, concat_axis=0, t...  52.8 us
    ppermute x1, waiting for transfers between devices, local_cube(): conv_held = lax.ppermute(conv_other, ('shell', 'upper', 'low'), swaps)  26.1 us
    all_to_all x1, waiting for transfers between devices, local_cube(): lax.all_to_all(col_sent, 'low', split_axis=0, concat_axis=0, tiled=True)  16.5 us
    all_to_all x2, starting transfers between devices, cube_exchange(): lax.all_to_all(value, ('shell', 'low'), split_axis=0, concat_axis=0, tile...  13.1 us
    pallas_call x1, Pallas kernels, local_cube(): pl.pallas_call(partial(columns_kernel, order), grid=(2,), in_specs=[pl.Bl...  12.8 us
    pallas_call x1, Pallas kernels, local_cube(): pl.pallas_call(partial(rows_kernel, cap, chunks), grid=(slab // some,), i...  12.4 us
    all_to_all x2, waiting for transfers between devices, cube_exchange(): lax.all_to_all(value, ('shell', 'low'), split_axis=0, concat_axis=0, tile...  11.3 us
    ppermute x1, waiting for transfers between devices, local_cube(): raw_far = lax.ppermute(raw_first, 'upper', [(0, 1), (1, 0)])  8.03 us
  transfers between devices with their start and end apart: 8, of which 8 were waited for; matrix products, arithmetic and copies ran while one was open for 3% of the time, Pallas kernels for 8%

profile of v6, /device:TPU:1, one launch (start us, length us, event | category | flops | bytes accessed | tf_op | source)
XLA Modules:
  0.0 214.4 jit_solution(3813902029645583727)
XLA Ops:
  0.6 0.0 copy-start.4
  0.7 0.0 copy-start.7
  0.7 0.0 copy-start.9
  0.7 1.1 widen.1
  1.7 0.1 stack.27.at_ref
  1.8 0.7 copy-done.3
  2.5 2.7 %pack.2 = f32[16,136,128]{2,1,0:T(8,128)} custom-call(s32[6]{0:T(128)S(1)} %stack.27.at_ref, s32[2,1024]{1,0:T(2,128)S(1)} %copy-done.3, f32[2,2,64,512]{3,2,1,0:T(8,128)S(1)} %get-tuple-element.10.raw_ref), custom_call_target="tpu_custom_call" | custom-call | tf_op jit(solution)/shard_map/pack/pallas_call | solution.py:662
  5.2 6.2 %all-to-all-start = ((f32[16,136,128]{2,1,0:T(8,128)}), f32[16,136,128]{2,1,0:T(8,128)S(1)}, u32[]{:S(2)}, u32[]{:S(2)}) async-start(f32[16,136,128]{2,1,0:T(8,128)} %pack.2), calls=%async_computation | async-start | bytes 2228224 | tf_op jit(solution)/shard_map/all_to_all | solution.py:626
  11.5 0.1 copy.22
  11.6 0.1 copy.23
  11.7 0.1 copy.21
  11.8 0.1 concatenate.12
  11.9 1.4 collective-permute-start
  13.2 2.3 %collective-permute-start.1 = (f32[2,1,64,512]{3,2,1,0:T(8,128)S(1)}, f32[2,1,64,512]{3,2,1,0:T(8,128)S(1)}, u32[]{:S(2)}, u32[]{:S(2)}) collective-permute-start(f32[2,1,64,512]{3,2,1,0:T(8,128)S(1)} %get-tuple-element.11), channel_id=1, source_target_pairs={{0,8},{8,0},{1,9},{9,1},{2,10},{10,2},{3,11},{11,3},{4,12},{12,4},... | collective-permute-start | bytes 786440 | tf_op jit(solution)/shard_map/ppermute | solution.py:657
  15.6 5.8 %collective-permute-done = f32[2,1027]{1,0:T(2,128)S(1)} collective-permute-done((f32[2,1027]{1,0:T(2,128)S(1)}, f32[2,1027]{1,0:T(2,128)S(1)}, u32[]{:S(2)}, u32[]{:S(2)}) %collective-permute-start) | collective-permute-done | bytes 8248 | tf_op jit(solution)/shard_map/ppermute | solution.py:680
  21.4 0.2 slice_reduce_fusion.2
  21.6 8.0 %collective-permute-done.1.raw_ref = f32[2,1,64,512]{3,2,1,0:T(8,128)S(1)} collective-permute-done((f32[2,1,64,512]{3,2,1,0:T(8,128)S(1)}, f32[2,1,64,512]{3,2,1,0:T(8,128)S(1)}, u32[]{:S(2)}, u32[]{:S(2)}) %collective-permute-start.1) | collective-permute-done | bytes 262176 | tf_op jit(solution)/shard_map/ppermute | solution.py:657
  29.6 1.9 pack.3
  31.6 1.4 all-to-all-done.near_ref
  33.0 6.8 %all-to-all-start.1 = ((f32[16,64,128]{2,1,0:T(8,128)}), f32[16,64,128]{2,1,0:T(8,128)S(1)}, u32[]{:S(2)}, u32[]{:S(2)}) async-start(f32[16,64,128]{2,1,0:T(8,128)} %pack.3), calls=%async_computation.1 | async-start | bytes 1048576 | tf_op jit(solution)/shard_map/all_to_all | solution.py:626
  39.9 0.2 subtract_select_fusion
  40.0 0.1 reshape.98
  40.2 0.1 collective-permute-start.2
  40.3 0.8 select_reduce_fusion
  41.1 0.1 copy.24
  41.2 1.2 select_reduce_fusion.1
  42.4 0.1 reshape.101.slots_ref
  42.5 0.1 reshape.100.slots_ref
  42.6 0.1 pad_maximum_fusion.weight_ref
  42.6 9.8 %all-to-all-done.1.first_ref = f32[16,64,128]{2,1,0:T(8,128)S(1)} async-done(((f32[16,64,128]{2,1,0:T(8,128)}), f32[16,64,128]{2,1,0:T(8,128)S(1)}, u32[]{:S(2)}, u32[]{:S(2)}) %all-to-all-start.1) | async-done | bytes 524320 | tf_op jit(solution)/shard_map/all_to_all | solution.py:626
  52.5 4.5 %deposit_first.1.first_dens_ref = f32[2,128,16,128]{3,2,1,0:T(8,128)} custom-call(s32[256]{0:T(256)S(1)} %reshape.100.slots_ref, f32[16,64,128]{2,1,0:T(8,128)S(1)} %all-to-all-done.1.first_ref), custom_call_target="tpu_custom_call" | custom-call | tf_op jit(solution)/shard_map/deposit_first/pallas_call | solution.py:711
  57.0 7.5 %deposit.1.near_dens_ref = f32[4,128,16,128]{3,2,1,0:T(8,128)} custom-call(s32[256]{0:T(256)S(1)} %reshape.101.slots_ref, f32[16,136,128]{2,1,0:T(8,128)S(1)} %all-to-all-done.near_ref), custom_call_target="tpu_custom_call" | custom-call | tf_op jit(solution)/shard_map/deposit/pallas_call | solution.py:703
  64.5 4.1 %collective-permute-done.2.far_ref = f32[16,72,128]{2,1,0:T(8,128)S(1)} collective-permute-done((f32[16,72,128]{2,1,0:T(8,128)S(1)}, f32[16,72,128]{2,1,0:T(8,128)S(1)}, u32[]{:S(2)}, u32[]{:S(2)}) %collective-permute-start.2) | collective-permute-done | bytes 589856 | tf_op jit(solution)/shard_map/ppermute | solution.py:673
  68.6 0.0 copy-done.1
  68.7 12.4 %rows.1 = (f32[2,128,2048]{2,1,0:T(8,128)}, f32[2,128,2048]{2,1,0:T(8,128)}, f32[16,2,2,128,128]{4,3,2,1,0:T(8,128)}) custom-call(f32[4,5]{1,0:T(4,128)S(1)} %pad_maximum_fusion.weight_ref, s32[6]{0:T(128)S(1)} %stack.27.at_ref, s32[256]{0:T(256)S(1)} %reshape.100.slots_ref, f32[4,128,16,128]{3,2,1,0:T(8,128)} %deposit.1.near_dens_ref, ...), custom_call_target="tpu_custom_call" | custom-call | tf_op jit(solution)/shard_map/rows/pallas_call | solution.py:725
  81.1 5.4 %all-to-all-start.2 = ((f32[16,2,2,128,128]{4,3,2,1,0:T(8,128)}), f32[16,2,2,128,128]{4,3,2,1,0:T(8,128)}, u32[]{:S(2)}, u32[]{:S(2)}) async-start(f32[16,2,2,128,128]{4,3,2,1,0:T(8,128)} %get-tuple-element.14), calls=%async_computation.2 | async-start | bytes 8388608 | tf_op jit(solution)/shard_map/all_to_all | solution.py:762
  86.5 0.0 copy-start.2
  86.5 3.2 %filters.1.filters_ref = f32[2,2,16,128,128]{4,3,2,1,0:T(8,128)} custom-call(s32[6]{0:T(128)S(1)} %stack.27.at_ref), custom_call_target="tpu_custom_call" | custom-call | tf_op jit(solution)/shard_map/filters/pallas_call | solution.py:694
  89.7 52.8 %all-to-all-done.2.in_ref = f32[16,2,2,128,128]{4,3,2,1,0:T(8,128)} async-done(((f32[16,2,2,128,128]{4,3,2,1,0:T(8,128)}), f32[16,2,2,128,128]{4,3,2,1,0:T(8,128)}, u32[]{:S(2)}, u32[]{:S(2)}) %all-to-all-start.2) | async-done | bytes 4194336 | tf_op jit(solution)/shard_map/all_to_all | solution.py:762
  142.5 0.0 copy-done
  142.5 12.8 %columns.1 = f32[8,2,2,2,128,128]{5,4,3,2,1,0:T(8,128)} custom-call(f32[2,2,16,128,128]{4,3,2,1,0:T(8,128)} %filters.1.filters_ref, f32[16,2,2,128,128]{4,3,2,1,0:T(8,128)} %all-to-all-done.2.in_ref, f32[2,128,16]{2,1,0:T(8,128)S(1)} %copy-done.2, bf16[2,256,256]{2,1,0:T(8,128)(2,1)S(1)} %copy-done, bf16[2,256,256]{2,1,0:T(8,128)(2,1)S(1)} %copy-done.1), custom_call_target="tpu_custom_call" | custom-call | tf_op jit(solution)/shard_map/columns/pallas_call | solution.py:771
  155.3 0.0 copy-start.6
  155.3 5.5 %all-to-all-start.3 = ((f32[8,2,2,2,128,128]{5,4,3,2,1,0:T(8,128)}), f32[8,2,2,2,128,128]{5,4,3,2,1,0:T(8,128)}, u32[]{:S(2)}, u32[]{:S(2)}) async-start(f32[8,2,2,2,128,128]{5,4,3,2,1,0:T(8,128)} %columns.1), calls=%async_computation.3 | async-start | bytes 8388608 | tf_op jit(solution)/shard_map/all_to_all | solution.py:794
  160.8 1.3 collective-permute-start.3
  162.1 26.1 %collective-permute-done.3 = f32[2,128,2048]{2,1,0:T(8,128)} collective-permute-done((f32[2,128,2048]{2,1,0:T(8,128)}, f32[2,128,2048]{2,1,0:T(8,128)}, u32[]{:S(2)}, u32[]{:S(2)}) %collective-permute-start.3) | collective-permute-done | bytes 2097184 | tf_op jit(solution)/shard_map/ppermute | solution.py:769
  188.2 3.4 %broadcast_select_fusion = f32[2,128,2048]{2,1,0:T(8,128)} fusion(f32[2,128,2048]{2,1,0:T(8,128)S(1)} %copy-done.6, f32[2,128,2048]{2,1,0:T(8,128)} %collective-permute-done.3, pred[]{:T(512)S(6)} %eq.35), kind=kLoop, calls=%fused_computation.1 | loop fusion | flops 524288 | bytes 6291457 | tf_op jit(solution)/shard_map/jit(_where)/select_n | solution.py:770
  191.6 16.5 %all-to-all-done.3.in_ref = f32[8,2,2,2,128,128]{5,4,3,2,1,0:T(8,128)} async-done(((f32[8,2,2,2,128,128]{5,4,3,2,1,0:T(8,128)}), f32[8,2,2,2,128,128]{5,4,3,2,1,0:T(8,128)}, u32[]{:S(2)}, u32[]{:S(2)}) %all-to-all-start.3) | async-done | bytes 4194336 | tf_op jit(solution)/shard_map/all_to_all | solution.py:794
  208.2 6.3 %inverse_rows.1 = (f32[2,128,2048]{2,1,0:T(8,128)}, f32[2,128,2048]{2,1,0:T(8,128)}) custom-call(f32[8,2,2,2,128,128]{5,4,3,2,1,0:T(8,128)} %all-to-all-done.3.in_ref, f32[2,16,128]{2,1,0:T(8,128)S(1)} %copy-done.5, bf16[2,256,256]{2,1,0:T(8,128)(2,1)S(1)} %copy-done), custom_call_target="tpu_custom_call" | custom-call | tf_op jit(solution)/shard_map/inverse_rows/pallas_call | solution.py:795
  (21 shorter events, 0.2 us)
Async XLA Ops:
  0.6 10.8 %copy-start.4 = (s32[2,1024]{1,0:T(2,128)S(1)}, s32[2,1024]{1,0:T(2,128)}, u32[]{:S(2)}) copy-start(s32[2,1024]{1,0:T(2,128)} %table_ref.5) | copy-start | bytes 24580
  0.7 10.8 %copy-start.7 = (f32[2]{0:T(128)S(1)}, f32[2]{0:T(128)}, u32[]{:S(2)}) copy-start(f32[2]{0:T(128)} %param.14) | copy-start | bytes 28
  0.7 10.8 %copy-start.9 = (f32[2]{0:T(128)S(1)}, f32[2]{0:T(128)}, u32[]{:S(2)}) copy-start(f32[2]{0:T(128)} %param.13) | copy-start | bytes 28
  0.7 10.9 %copy-start.8 = (f32[2]{0:T(128)S(1)}, f32[2]{0:T(128)}, u32[]{:S(2)}) copy-start(f32[2]{0:T(128)} %param.15) | copy-start | bytes 28
  1.8 0.7 copy-start.3
  5.2 27.8 %all-to-all-start = ((f32[16,136,128]{2,1,0:T(8,128)}), f32[16,136,128]{2,1,0:T(8,128)S(1)}, u32[]{:S(2)}, u32[]{:S(2)}) async-start(f32[16,136,128]{2,1,0:T(8,128)} %pack.2), calls=%async_computation | async-start | bytes 2228224 | tf_op jit(solution)/shard_map/all_to_all | solution.py:626
  11.9 9.5 %collective-permute-start = (f32[2,1027]{1,0:T(2,128)S(1)}, f32[2,1027]{1,0:T(2,128)S(1)}, u32[]{:S(2)}, u32[]{:S(2)}) collective-permute-start(f32[2,1027]{1,0:T(2,128)S(1)} %concatenate.12), channel_id=1, source_target_pairs={{0,16},{16,0},{1,17},{17,1},{2,18},{18,2},{3,19},{19,3},{4,20},{20... | collective-permute-start | bytes 24656 | tf_op jit(solution)/shard_map/ppermute | solution.py:680
  13.2 16.4 %collective-permute-start.1 = (f32[2,1,64,512]{3,2,1,0:T(8,128)S(1)}, f32[2,1,64,512]{3,2,1,0:T(8,128)S(1)}, u32[]{:S(2)}, u32[]{:S(2)}) collective-permute-start(f32[2,1,64,512]{3,2,1,0:T(8,128)S(1)} %get-tuple-element.11), channel_id=1, source_target_pairs={{0,8},{8,0},{1,9},{9,1},{2,10},{10,2},{3,11},{11,3},{4,12},{12,4},... | collective-permute-start | bytes 786440 | tf_op jit(solution)/shard_map/ppermute | solution.py:657
  33.0 19.4 %all-to-all-start.1 = ((f32[16,64,128]{2,1,0:T(8,128)}), f32[16,64,128]{2,1,0:T(8,128)S(1)}, u32[]{:S(2)}, u32[]{:S(2)}) async-start(f32[16,64,128]{2,1,0:T(8,128)} %pack.3), calls=%async_computation.1 | async-start | bytes 1048576 | tf_op jit(solution)/shard_map/all_to_all | solution.py:626
  40.2 28.4 %collective-permute-start.2 = (f32[16,72,128]{2,1,0:T(8,128)S(1)}, f32[16,72,128]{2,1,0:T(8,128)S(1)}, u32[]{:S(2)}, u32[]{:S(2)}) collective-permute-start(f32[16,72,128]{2,1,0:T(8,128)S(1)} %slice.24), channel_id=1, source_target_pairs={{0,8},{8,0},{1,9},{9,1},{2,10},{10,2},{3,11},{11,3},{4,12},{12,4},... | collective-permute-start | bytes 1769480 | tf_op jit(solution)/shard_map/ppermute | solution.py:673
  57.0 11.7 %copy-start.1 = (bf16[2,256,256]{2,1,0:T(8,128)(2,1)S(1)}, bf16[2,256,256]{2,1,0:T(8,128)(2,1)}, u32[]{:S(2)}) copy-start(bf16[2,256,256]{2,1,0:T(8,128)(2,1)} %constant.65.clone.table_ref.back_ref) | copy-start | bytes 786436
  57.0 11.7 %copy-start.5 = (f32[2,16,128]{2,1,0:T(8,128)S(1)}, f32[2,16,128]{2,1,0:T(8,128)}, u32[]{:S(2)}) copy-start(f32[2,16,128]{2,1,0:T(8,128)} %constant.63.clone.twiddle_ref) | copy-start | bytes 49156
  81.1 61.4 %all-to-all-start.2 = ((f32[16,2,2,128,128]{4,3,2,1,0:T(8,128)}), f32[16,2,2,128,128]{4,3,2,1,0:T(8,128)}, u32[]{:S(2)}, u32[]{:S(2)}) async-start(f32[16,2,2,128,128]{4,3,2,1,0:T(8,128)} %get-tuple-element.14), calls=%async_computation.2 | async-start | bytes 8388608 | tf_op jit(solution)/shard_map/all_to_all | solution.py:762
  86.5 56.0 %copy-start = (bf16[2,256,256]{2,1,0:T(8,128)(2,1)S(1)}, bf16[2,256,256]{2,1,0:T(8,128)(2,1)}, u32[]{:S(2)}) copy-start(bf16[2,256,256]{2,1,0:T(8,128)(2,1)} %constant.66.clone.forward_ref.table_ref) | copy-start | bytes 786436
  86.5 56.0 %copy-start.2 = (f32[2,128,16]{2,1,0:T(8,128)S(1)}, f32[2,128,16]{2,1,0:T(8,128)}, u32[]{:S(2)}) copy-start(f32[2,128,16]{2,1,0:T(8,128)} %constant.64.clone.turn_ref) | copy-start | bytes 49156
  155.3 32.9 %copy-start.6 = (f32[2,128,2048]{2,1,0:T(8,128)S(1)}, f32[2,128,2048]{2,1,0:T(8,128)}, u32[]{:S(2)}) copy-start(f32[2,128,2048]{2,1,0:T(8,128)} %get-tuple-element.12) | copy-start | bytes 6291460
  155.3 52.9 %all-to-all-start.3 = ((f32[8,2,2,2,128,128]{5,4,3,2,1,0:T(8,128)}), f32[8,2,2,2,128,128]{5,4,3,2,1,0:T(8,128)}, u32[]{:S(2)}, u32[]{:S(2)}) async-start(f32[8,2,2,2,128,128]{5,4,3,2,1,0:T(8,128)} %columns.1), calls=%async_computation.3 | async-start | bytes 8388608 | tf_op jit(solution)/shard_map/all_to_all | solution.py:794
  160.8 27.4 %collective-permute-start.3 = (f32[2,128,2048]{2,1,0:T(8,128)}, f32[2,128,2048]{2,1,0:T(8,128)}, u32[]{:S(2)}, u32[]{:S(2)}) collective-permute-start(f32[2,128,2048]{2,1,0:T(8,128)} %get-tuple-element.13), channel_id=1, source_target_pairs={{0,16},{2,18},{4,20},{6,22},{9,25},{11,27},{13,29},{15,31},{17,1},... | collective-permute-start | bytes 6291464 | tf_op jit(solution)/shard_map/ppermute | solution.py:769
